TPU v7x, 32 devices: a whole 2x2x4 slice. The times are simulated.
32 devices in a mesh: seq: 4 (over y, x), tm: 8 (over z, core).
Axes of the slice: x: 2, y: 2, z: 4, core: 2. Of those that a mesh axis runs over, the one named last changes fastest.
Arguments:
- inputs: bfloat16 [32, 1024, 512], P('seq', 'tm'), may hold values from -6 to 6
- lengths: int32 [32, 8], P('seq'), may hold values from 1 to 256, 1024 in all within a row
- norm_gain: bfloat16 [512], replicated, may hold values from 0.099609375 to 1.8984375
- conv_kernel: bfloat16 [3, 3, 512], replicated, may hold values from -3.5 to 3.5
- qkv_weight: bfloat16 [3, 512, 512], replicated, may hold values from -0.25 to 0.25
- out_weight: bfloat16 [512, 512], replicated, may hold values from -1 to 1
- mlp_gain: bfloat16 [512], replicated, may hold values from 0.099609375 to 1.8984375
- up_weight: bfloat16 [512, 2048], replicated, may hold values from -0.25 to 0.25
- down_weight: bfloat16 [2048, 512], replicated, may hold values from -0.125 to 0.125
- layer_scale: bfloat16 [512], replicated, may hold values from 0.5 to 2
- cotangent: bfloat16 [32, 1024, 512], P('seq', 'tm'), may hold values from -6 to 6
Outputs:
- output: bfloat16 [32, 1024, 512], P('seq', 'tm')
- d_inputs: float32 [32, 1024, 512], P('seq', 'tm')
- d_norm_gain: float32 [512], replicated
- d_conv_kernel: float32 [3, 3, 512], replicated
- d_qkv_weight: float32 [3, 512, 512], replicated
- d_out_weight: float32 [512, 512], replicated
- d_mlp_gain: float32 [512], replicated
- d_up_weight: float32 [512, 2048], replicated
- d_down_weight: float32 [2048, 512], replicated
- d_layer_scale: float32 [512], replicated
Inputs may be any that keep to these rules, and one draw needn't show every extreme that they name: `lengths`: each row sums to 1024; the longest video of each sequence has exactly 256 frames.
All inputs are finite; a program needn't handle non-finite values.
Results may differ from a plain program's by a relative error of at most 0.012.
The roundings to bfloat16 on the way count: a program that leaves them out, or rounds other values in their place, can miss the bound.
Values may be sent and summed in bfloat16 or wider, within the bound.
A program may use at most 128 MiB of HBM per device.

v0:
```python
import jax
import jax.numpy as jnp
from jax import lax
from jax.sharding import PartitionSpec as P

HEADS = 4
HD = 128
HALF = 9


def extended(shard, sides, width):
    for axis, dim in sides:
        size, length = (lax.axis_size(axis), shard.shape[dim])
        up = [(i, (i + 1) % size) for i in range(size - 1)]
        down = [(j, i) for i, j in up]
        last = lax.slice_in_dim(shard, length - width, length, axis=dim)
        first = lax.slice_in_dim(shard, 0, width, axis=dim)
        before = lax.ppermute(last, axis, up)
        after = lax.ppermute(first, axis, down)
        shard = jnp.concatenate([before, shard, after], axis=dim)
    return shard


def from_behind(shard, axis, by):
    length = lax.axis_size(axis)
    pairs = [(i, i + by) for i in range(length) if 0 <= i + by < length]
    return lax.ppermute(shard, axis, pairs)


def layer_norm(values_in, scaling):
    average = jnp.mean(values_in, axis=-1, keepdims=True)
    centered = values_in - average
    spread = jnp.mean(centered * centered, axis=-1, keepdims=True)
    return centered * lax.rsqrt(spread + 1e-05) * scaling


def segment_rows(lengths, start_pos, row_count, seq_length):
    positions = start_pos + jnp.arange(row_count, dtype=jnp.int32)
    bounds = jnp.cumsum(lengths, axis=1)
    segment = jnp.sum((positions[None, :, None] >= bounds[:, None, :]).astype(jnp.int32), axis=2)
    inside = (positions >= 0) & (positions < seq_length)
    return jnp.where(inside[None, :], segment, -1)


def depthwise(window, kernel, segment):
    row_count = window.shape[1] - 2
    centre = segment[:, 1 : row_count + 1]
    mixed = jnp.zeros((window.shape[0], row_count, window.shape[2]), jnp.float32)
    for column in range(3):
        nearby = segment[:, column : column + row_count]
        joined = (nearby == centre) & (nearby >= 0)
        mixed = mixed + kernel[column] * window[:, column : column + row_count] * joined[..., None]
    return mixed


def project(acts, weight):
    return jnp.einsum("std,de->ste", acts, weight, preferred_element_type=jnp.float32)


def shards(
    inputs,
    lengths,
    norm_gain,
    conv_kernel,
    qkv_weight,
    out_weight,
    mlp_gain,
    up_weight,
    down_weight,
    layer_scale,
    cotangent,
):
    sequences, frames, features = inputs.shape
    reach = HALF
    seq_length = frames * lax.axis_size("tm")
    start_pos = lax.axis_index("tm") * frames
    seg_wide = segment_rows(lengths, start_pos - reach - 1, frames + 2 * reach + 2, seq_length)
    seg_own = seg_wide[:, reach : frames + reach + 2]
    gain_one = norm_gain.astype(jnp.float32)
    kernel = conv_kernel.astype(jnp.float32)
    inputs_f = inputs.astype(jnp.float32)
    normed = layer_norm(inputs_f, gain_one).astype(jnp.bfloat16)
    window = extended(normed, (("tm", 1),), 1)
    window_f = window.astype(jnp.float32)
    act_q = depthwise(window_f, kernel[0], seg_own).astype(jnp.bfloat16)
    act_k = depthwise(window_f, kernel[1], seg_own).astype(jnp.bfloat16)
    act_v = depthwise(window_f, kernel[2], seg_own).astype(jnp.bfloat16)
    queries = project(act_q, qkv_weight[0]).astype(jnp.bfloat16)
    key_value = jnp.concatenate(
        [project(act_k, qkv_weight[1]), project(act_v, qkv_weight[2])], axis=-1
    ).astype(jnp.bfloat16)
    wider = extended(key_value, (("tm", 1),), reach)
    key_rows = wider[..., :features]
    value_rows = wider[..., features:]
    span = frames + 2 * reach
    seg_keys = seg_wide[:, 1 : span + 1]
    seg_query = seg_wide[:, reach + 1 : frames + reach + 1]
    offsets = (
        jnp.arange(span, dtype=jnp.int32)[None, :] - jnp.arange(frames, dtype=jnp.int32)[:, None]
    )
    in_band = (offsets >= 0) & (offsets <= 2 * reach)
    allowed = (
        in_band[None]
        & (seg_keys[:, None, :] == seg_query[:, :, None])
        & (seg_keys[:, None, :] >= 0)
    )
    allowed = allowed[:, None]
    temper = HD ** (-0.5)
    query_heads = queries.reshape(sequences, frames, HEADS, HD)
    key_heads = key_rows.reshape(sequences, span, HEADS, HD)
    value_heads = value_rows.reshape(sequences, span, HEADS, HD)
    scores = (
        jnp.einsum("sthd,sjhd->shtj", query_heads, key_heads, preferred_element_type=jnp.float32)
        * temper
    )
    row_max = jnp.max(jnp.where(allowed, scores, -1e30), axis=-1, keepdims=True)
    raised = jnp.where(allowed, jnp.exp(jnp.where(allowed, scores - row_max, 0.0)), 0.0)
    row_sum = jnp.sum(raised, axis=-1, keepdims=True)
    probs = raised / row_sum
    log_total = row_max + jnp.log(row_sum)
    weights_low = probs.astype(jnp.bfloat16)
    attended = jnp.einsum(
        "shtj,sjhd->sthd", weights_low, value_heads, preferred_element_type=jnp.float32
    )
    act_o = attended.reshape(sequences, frames, features).astype(jnp.bfloat16)
    branch = project(act_o, out_weight)
    residual = inputs_f + branch
    gain_two = mlp_gain.astype(jnp.float32)
    normed_two = layer_norm(residual, gain_two).astype(jnp.bfloat16)
    upper = project(normed_two, up_weight)
    hidden = jax.nn.gelu(upper).astype(jnp.bfloat16)
    mlp_out = project(hidden, down_weight)
    scale_f = layer_scale.astype(jnp.float32)
    output = (residual + scale_f * mlp_out).astype(jnp.bfloat16)
    grad_out = cotangent.astype(jnp.float32)
    d_scale = jnp.sum(grad_out * mlp_out, axis=(0, 1))
    d_mlp = (grad_out * scale_f).astype(jnp.bfloat16)
    d_down = jnp.einsum("stf,std->fd", hidden, d_mlp, preferred_element_type=jnp.float32)
    d_hidden = jnp.einsum("std,fd->stf", d_mlp, down_weight, preferred_element_type=jnp.float32)
    gelu_pull = jax.vjp(jax.nn.gelu, upper)[1]
    d_upper = gelu_pull(d_hidden)[0].astype(jnp.bfloat16)
    d_up = jnp.einsum("std,stf->df", normed_two, d_upper, preferred_element_type=jnp.float32)
    d_normed_two = jnp.einsum("stf,df->std", d_upper, up_weight, preferred_element_type=jnp.float32)
    second_pull = jax.vjp(layer_norm, residual, gain_two)[1]
    d_resid_part, d_gain_two = second_pull(d_normed_two)
    d_residual = grad_out + d_resid_part
    d_branch = d_residual.astype(jnp.bfloat16)
    d_out = jnp.einsum("std,ste->de", act_o, d_branch, preferred_element_type=jnp.float32)
    d_attended = jnp.einsum("ste,de->std", d_branch, out_weight, preferred_element_type=jnp.float32)
    d_attended = d_attended.astype(jnp.bfloat16).reshape(sequences, frames, HEADS, HD)
    again = (
        jnp.einsum("sthd,sjhd->shtj", query_heads, key_heads, preferred_element_type=jnp.float32)
        * temper
    )
    probs_again = jnp.where(allowed, jnp.exp(jnp.where(allowed, again - log_total, 0.0)), 0.0)
    weights_again = probs_again.astype(jnp.bfloat16)
    d_weights = jnp.einsum(
        "sthd,sjhd->shtj", d_attended, value_heads, preferred_element_type=jnp.float32
    )
    row_dot = jnp.sum(probs_again * d_weights, axis=-1, keepdims=True)
    d_scores = (probs_again * (d_weights - row_dot)).astype(jnp.bfloat16)
    d_query = (
        jnp.einsum("shtj,sjhd->sthd", d_scores, key_heads, preferred_element_type=jnp.float32)
        * temper
    )
    d_keys = (
        jnp.einsum("shtj,sthd->sjhd", d_scores, query_heads, preferred_element_type=jnp.float32)
        * temper
    )
    d_values = jnp.einsum(
        "shtj,sthd->sjhd", weights_again, d_attended, preferred_element_type=jnp.float32
    )
    stacked = jnp.concatenate(
        [d_keys.reshape(sequences, span, features), d_values.reshape(sequences, span, features)],
        axis=-1,
    )
    from_high = from_behind(stacked[:, :reach].astype(jnp.bfloat16), "tm", -1).astype(jnp.float32)
    from_low = from_behind(stacked[:, frames + reach :].astype(jnp.bfloat16), "tm", 1).astype(
        jnp.float32
    )
    own_rows = stacked[:, reach : frames + reach]
    own_rows = own_rows.at[:, :reach].add(from_low).at[:, frames - reach :].add(from_high)
    d_query_low = d_query.reshape(sequences, frames, features).astype(jnp.bfloat16)
    d_key_low = own_rows[..., :features].astype(jnp.bfloat16)
    d_value_low = own_rows[..., features:].astype(jnp.bfloat16)
    d_qkv = jnp.stack(
        [
            jnp.einsum("std,ste->de", act_q, d_query_low, preferred_element_type=jnp.float32),
            jnp.einsum("std,ste->de", act_k, d_key_low, preferred_element_type=jnp.float32),
            jnp.einsum("std,ste->de", act_v, d_value_low, preferred_element_type=jnp.float32),
        ],
        axis=0,
    )
    d_mixed = (
        jnp.einsum("ste,de->std", d_query_low, qkv_weight[0], preferred_element_type=jnp.float32),
        jnp.einsum("ste,de->std", d_key_low, qkv_weight[1], preferred_element_type=jnp.float32),
        jnp.einsum("ste,de->std", d_value_low, qkv_weight[2], preferred_element_type=jnp.float32),
    )

    def three_convs(window_in, kernels):
        return (
            depthwise(window_in, kernels[0], seg_own),
            depthwise(window_in, kernels[1], seg_own),
            depthwise(window_in, kernels[2], seg_own),
        )

    conv_pull = jax.vjp(three_convs, window.astype(jnp.float32), kernel)[1]
    d_window, d_kernel = conv_pull(d_mixed)
    got_high = from_behind(d_window[:, :1], "tm", -1)
    got_low = from_behind(d_window[:, frames + 1 :], "tm", 1)
    d_normed = d_window[:, 1 : frames + 1].at[:, :1].add(got_low).at[:, frames - 1 :].add(got_high)
    first_pull = jax.vjp(layer_norm, inputs_f, gain_one)[1]
    d_in_part, d_gain_one = first_pull(d_normed)
    d_inputs = d_residual + d_in_part
    totals = lax.psum(
        (d_gain_one, d_kernel, d_qkv, d_out, d_gain_two, d_up, d_down, d_scale), ("seq", "tm")
    )
    return (
        output,
        d_inputs,
        totals[0],
        totals[1],
        totals[2],
        totals[3],
        totals[4],
        totals[5],
        totals[6],
        totals[7],
    )


def solution(mesh):
    placed = (
        P("seq", "tm", None),
        P("seq", None),
        P(),
        P(),
        P(),
        P(),
        P(),
        P(),
        P(),
        P(),
        P("seq", "tm", None),
    )
    return jax.shard_map(
        shards,
        mesh=mesh,
        in_specs=placed,
        out_specs=(
            P("seq", "tm", None),
            P("seq", "tm", None),
            P(),
            P(),
            P(),
            P(),
            P(),
            P(),
            P(),
            P(),
        ),
        check_vma=False,
    )
```

profile of v0, /device:TPU:1, one launch (start us, length us, event | category | flops | bytes accessed | tf_op | source)
XLA Modules:
  0.0 367.9 jit_solution(8040205689744658966)
XLA Ops:
  7.3 0.9 convert_element_type.130
  8.1 1.5 convert_reduce_fusion
  9.6 1.7 fusion.15
  11.7 1.0 copy-done.6
  12.7 4.6 %collective-permute-start = (bf16[8,1,512]{2,1,0:T(2,128)(2,1)S(1)}, bf16[8,1,512]{2,1,0:T(2,128)(2,1)S(1)}, u32[]{:S(2)}, u32[]{:S(2)}) collective-permute-start(bf16[8,1,512]{2,1,0:T(2,128)(2,1)S(1)} %get-tuple-element.110), channel_id=1, source_target_pairs={{0,1},{1,2},{2,3},{3,4},{4,5},{5,6},{6,7},{8,9},{9,10},{10,11},{11... | collective-permute-start | bytes 24584 | tf_op jit(solution)/shard_map/ppermute | solution.py:18
  17.3 1.9 collective-permute-start.1
  20.5 1.9 collective-permute-done.1
  22.4 1.6 maximum_convert_fusion
  24.0 1.0 add_convert_fusion.2
  25.0 1.2 copy-done.17
  27.2 1.6 add_convert_fusion.1
  29.8 1.9 collective-permute-start.2
  31.8 2.6 collective-permute-start.3
  35.1 4.4 %collective-permute-done.3 = bf16[8,9,1024]{2,1,0:T(8,128)(2,1)S(1)} collective-permute-done((bf16[8,9,1024]{2,1,0:T(8,128)(2,1)S(1)}, bf16[8,9,1024]{2,1,0:T(8,128)(2,1)S(1)}, u32[]{:S(2)}, u32[]{:S(2)}) %collective-permute-start.3) | collective-permute-done | bytes 147488 | tf_op jit(solution)/shard_map/ppermute | solution.py:19
  39.5 0.9 pad_maximum_fusion.1
  40.6 0.9 copy_bitcast_fusion.2
  41.5 1.2 select_reduce_fusion
  43.4 1.6 convolution_convert_fusion
  45.1 0.8 fusion.88
  46.3 1.1 copy-done.23
  47.5 2.4 fusion.27
  49.9 7.3 %fusion.6 = bf16[8,128,2048]{2,1,0:T(8,128)(2,1)S(1)} fusion(f32[8,128,2048]{2,1,0:T(8,128)S(1)} %fusion.27, bf16[2048,512]{1,0:T(8,128)(2,1)S(1)} %copy-done, bf16[8,128,512]{2,1,0:T(8,128)(2,1)S(1)} %copy-done.7, f32[512]{0:T(512)S(1)} %convert_element_type.145), kind=kOutput, calls=%fused_computation.8 | convolution fusion | flops 2190999552 | bytes 15730688 | tf_op jit(solution)/shard_map/std,fd->stf/dot_general | solution.py:139
  57.2 2.7 multiply_reduce_fusion.1
  60.0 4.7 %convolution_bitcast_fusion.1 = f32[512,2048]{1,0:T(8,128)} fusion(bf16[8,128,2048]{2,1,0:T(8,128)(2,1)S(1)} %fusion.6, f32[8,128,512]{2,1,0:T(8,128)S(1)} %get-tuple-element.127, f32[512]{0:T(512)S(1)} %convert_element_type.146, f32[8,128]{1,0:T(8,128)S(1)} %fusion.77, f32[8,128]{1,0:T(8,128)S(1)} %broadcast_multiply_fusion), kind=kOutput, calls=%fused_computation.11 | convolution fusion | flops 2149580800 | bytes 10496000 | tf_op jit(solution)/shard_map/std,stf->df/dot_general | solution.py:142
  64.6 5.6 %convolution_bitcast_fusion = f32[2048,512]{1,0:T(8,128)} fusion(bf16[8,128,512]{2,1,0:T(8,128)(2,1)S(1)} %copy-done.7, f32[512]{0:T(512)S(1)} %convert_element_type.145, f32[8,128,2048]{2,1,0:T(8,128)S(1)} %fusion.27), kind=kOutput, calls=%fused_computation.10 | convolution fusion | flops 2167930880 | bytes 13633536 | tf_op jit(solution)/shard_map/stf,std->fd/dot_general | solution.py:138
  70.2 5.1 %fusion.18 = (f32[512]{0:T(512)S(1)}, bf16[8,128,512]{2,1,0:T(8,128)(2,1)}, f32[8,128]{1,0:T(8,128)S(1)}, f32[8,128,512]{2,1,0:T(8,128)S(1)}) fusion(bf16[8,128,512]{2,1,0:T(8,128)(2,1)S(1)} %copy-done.7, f32[8,128,512]{2,1,0:T(8,128)S(1)} %get-tuple-element.127, f32[512]{0:T(512)S(1)} %convert_element_type.145, f32[8,128]{1,0:T(8,128)S(1)} %multiply_multiply_fusion.12, ...), kind=kOutput, calls=%fused_computation.45 | convolution fusion | flops 2173172224 | bytes 18896896 | tf_op jit(solution)/shard_map/std,de->ste/dot_general | solution.py:57
  75.7 1.0 copy-done.5
  76.7 0.7 fusion.31
  77.4 1.4 multiply_reduce_fusion
  78.8 0.8 convolution_bitcast_fusion.2
  79.6 0.9 multiply_convert_fusion.1
  80.5 1.3 multiply_convert_fusion.2
  81.9 0.8 multiply_bitcast_fusion
  82.7 1.4 copy.129
  84.1 1.4 copy.130
  85.5 1.4 copy_dynamic-update-slice_fusion.1
  86.8 1.4 copy_dynamic-update-slice_fusion
  88.6 2.7 slice.335
  91.4 1.7 convolution_bitcast_fusion.6
  93.2 1.9 collective-permute-start.5
  95.1 3.6 collective-permute-start.4
  98.8 1.7 convolution_bitcast_fusion.3
  100.5 1.6 collective-permute-done.4
  102.2 3.5 scatter-add.14
  105.6 1.1 slice_add_fusion
  106.8 2.9 scatter-add.15
  109.6 2.6 convert.17
  114.7 2.0 pad_maximum_fusion
  116.7 3.4 fusion.60
  120.1 3.3 fusion.50
  123.4 7.0 %multiply_reduce_fusion.4 = (f32[512]{0:T(512)S(1)}, f32[512]{0:T(512)S(1)}, f32[512]{0:T(512)S(1)}, f32[512]{0:T(512)S(1)}, f32[512]{0:T(512)S(1)}, /*index=5*/...) fusion(f32[8,128,512]{2,1,0:T(8,128)} %fusion.60, ...), kind=kOutput, calls=%fused_computation.57 | convolution fusion | flops 555740672 | bytes 30982144 | tf_op jit(solution)/shard_map/ste,de->std/dot_general | solution.py:197
  130.4 3.7 %pad_add_fusion = f32[8,130,512]{2,1,0:T(8,128)S(1)} fusion(f32[8,128,512]{2,1,0:T(8,128)S(1)} %get-tuple-element.101, f32[8,128,512]{2,1,0:T(8,128)S(1)} %get-tuple-element.102, f32[8,128,512]{2,1,0:T(8,128)} %get-tuple-element.103, f32[8,128,512]{2,1,0:T(8,128)S(1)} %get-tuple-element.96, f32[8,128,512]{2,1,0:T(8,128)S(1)} %get-tuple-element.98, ...), kind=kLoop, calls=%fused_computation.39 | loop fusion | flops 4259840 | bytes 21004288 | tf_op jit(solution)/shard_map/transpose(jvp())/add_any | solution.py:52
  134.2 1.9 collective-permute-start.7
  136.1 4.7 %collective-permute-start.6 = (f32[8,1,512]{2,1,0:T(1,128)S(1)}, f32[8,1,512]{2,1,0:T(1,128)S(1)}, u32[]{:S(2)}, u32[]{:S(2)}) collective-permute-start(f32[8,1,512]{2,1,0:T(1,128)S(1)} %get-tuple-element.94), channel_id=1, source_target_pairs={{0,1},{1,2},{2,3},{3,4},{4,5},{5,6},{6,7},{8,9},{9,10},{10,11},{11... | collective-permute-start | bytes 49160 | tf_op jit(solution)/shard_map/ppermute | solution.py:27
  142.6 1.2 fusion.14
  143.8 43.1 %all-reduce.21 = (f32[512]{0:T(512)}, f32[3,3,512]{2,1,0:T(4,128)}, f32[512]{0:T(512)}, f32[512]{0:T(512)}) all-reduce(f32[512]{0:T(512)S(1)} %get-tuple-element.69, f32[3,3,512]{2,1,0:T(4,128)S(1)} %pad_add_fusion.1, f32[512]{0:T(512)S(1)} %get-tuple-element.67, ...), channel_id=1, replica_groups=mesh['seq'=4,'tm'=8] {'seq','tm'}, use_global_device_ids=true, to_apply=%region_14.15 | all-reduce | flops 6144 | bytes 49152 | tf_op jit(solution)/shard_map/psum | solution.py:215
  186.9 3.4 add_add_fusion.2
  190.3 158.8 %all-reduce.25.cloned.1.call-done = (f32[3,512,512]{2,1,0:T(8,128)}, f32[512,512]{1,0:T(8,128)}, f32[512,2048]{1,0:T(8,128)}, f32[2048,512]{1,0:T(8,128)}) async-done(((f32[3,512,512]{2,1,0:T(8,128)}, f32[512,512]{1,0:T(8,128)}, f32[512,2048]{1,0:T(8,128)}, f32[2048,512]{1,0:T(8,128)}), (f32[3,512,512]{2,1,0:T(8,128)}, f32[512,512]{1,0:T(8,128)}, f32[512,2048]{1,0:T(8,128)}, ...) | async-done | bytes 12582928 | tf_op jit(solution)/shard_map/psum | solution.py:215
  349.1 4.0 %copy.140 = f32[3,512,512]{2,1,0:T(8,128)} copy(f32[3,512,512]{2,1,0:T(8,128)} %get-tuple-element.137) | data formatting | bytes 6291456
  353.1 1.0 copy.141
  354.1 2.1 copy.142
  356.2 1.6 copy-done.8
  357.8 2.1 copy.143
  359.9 1.0 copy-done.1
  (98 shorter events, 10.8 us)
Async XLA Ops:
  7.2 42.7 %copy-start = (bf16[2048,512]{1,0:T(8,128)(2,1)S(1)}, bf16[2048,512]{1,0:T(8,128)(2,1)}, u32[]{:S(2)}) copy-start(bf16[2048,512]{1,0:T(8,128)(2,1)} %param.27) | copy-start | bytes 6291460
  7.2 4.1 %copy-start.4 = (bf16[8,128,512]{2,1,0:T(8,128)(2,1)S(1)}, bf16[8,128,512]{2,1,0:T(8,128)(2,1)}, u32[]{:S(2)}) copy-start(bf16[8,128,512]{2,1,0:T(8,128)(2,1)} %param.19) | copy-start | bytes 3145732
  7.2 341.9 %all-reduce.25.cloned.1.call-start = ((), (), s32[]{:S(2)}) async-start(), calls=%async_computation | async-start | bytes 25165824 | tf_op jit(solution)/shard_map/psum | solution.py:215
  8.1 11.2 %copy-start.20 = (s32[8,8]{1,0:T(8,128)S(1)}, s32[8,8]{1,0:T(8,128)}, u32[]{:S(2)}) copy-start(s32[8,8]{1,0:T(8,128)} %param.20) | copy-start | bytes 772
  8.1 11.7 %copy-start.19 = (bf16[3,3,512]{2,1,0:T(4,128)(2,1)S(1)}, bf16[3,3,512]{2,1,0:T(4,128)(2,1)}, u32[]{:S(2)}) copy-start(bf16[3,3,512]{2,1,0:T(4,128)(2,1)} %param.22) | copy-start | bytes 27652
  8.1 12.3 %copy-start.21 = (bf16[512]{0:T(512)(128)(2,1)S(1)}, bf16[512]{0:T(512)(128)(2,1)}, u32[]{:S(2)}) copy-start(bf16[512]{0:T(512)(128)(2,1)} %param.25) | copy-start | bytes 3076
  8.1 12.3 %copy-start.22 = (bf16[512]{0:T(512)(128)(2,1)S(1)}, bf16[512]{0:T(512)(128)(2,1)}, u32[]{:S(2)}) copy-start(bf16[512]{0:T(512)(128)(2,1)} %param.28) | copy-start | bytes 3076
  11.7 1.0 copy-start.6
  12.7 7.8 %collective-permute-start = (bf16[8,1,512]{2,1,0:T(2,128)(2,1)S(1)}, bf16[8,1,512]{2,1,0:T(2,128)(2,1)S(1)}, u32[]{:S(2)}, u32[]{:S(2)}) collective-permute-start(bf16[8,1,512]{2,1,0:T(2,128)(2,1)S(1)} %get-tuple-element.110), channel_id=1, source_target_pairs={{0,1},{1,2},{2,3},{3,4},{4,5},{5,6},{6,7},{8,9},{9,10},{10,11},{11... | collective-permute-start | bytes 24584 | tf_op jit(solution)/shard_map/ppermute | solution.py:18
  17.3 5.1 %collective-permute-start.1 = (bf16[8,1,512]{2,1,0:T(2,128)(2,1)S(1)}, bf16[8,1,512]{2,1,0:T(2,128)(2,1)S(1)}, u32[]{:S(2)}, u32[]{:S(2)}) collective-permute-start(bf16[8,1,512]{2,1,0:T(2,128)(2,1)S(1)} %get-tuple-element.111), channel_id=1, source_target_pairs={{1,0},{2,1},{3,2},{4,3},{5,4},{6,5},{7,6},{9,8},{10,9},{11,10},{12... | collective-permute-start | bytes 24584 | tf_op jit(solution)/shard_map/ppermute | solution.py:19
  24.0 3.2 copy-start.2
  24.0 2.2 copy-start.17
  26.2 1.0 copy-start.14
  28.8 1.0 copy-start.10
  29.8 5.2 %collective-permute-start.2 = (bf16[8,9,1024]{2,1,0:T(8,128)(2,1)S(1)}, bf16[8,9,1024]{2,1,0:T(8,128)(2,1)S(1)}, u32[]{:S(2)}, u32[]{:S(2)}) collective-permute-start(bf16[8,9,1024]{2,1,0:T(8,128)(2,1)S(1)} %get-tuple-element.108), channel_id=1, source_target_pairs={{0,1},{1,2},{2,3},{3,4},{4,5},{5,6},{6,7},{8,9},{9,10},{10,11},{11... | collective-permute-start | bytes 442376 | tf_op jit(solution)/shard_map/ppermute | solution.py:18
  31.8 7.7 %collective-permute-start.3 = (bf16[8,9,1024]{2,1,0:T(8,128)(2,1)S(1)}, bf16[8,9,1024]{2,1,0:T(8,128)(2,1)S(1)}, u32[]{:S(2)}, u32[]{:S(2)}) collective-permute-start(bf16[8,9,1024]{2,1,0:T(8,128)(2,1)S(1)} %get-tuple-element.109), channel_id=1, source_target_pairs={{1,0},{2,1},{3,2},{4,3},{5,4},{6,5},{7,6},{9,8},{10,9},{11,10},{12... | collective-permute-start | bytes 442376 | tf_op jit(solution)/shard_map/ppermute | solution.py:19
  43.4 1.6 copy-start.18
  45.9 1.6 copy-start.23
  47.5 2.4 copy-start.7
  75.3 1.3 copy-start.5
  81.8 9.5 %copy-start.12 = (bf16[8,4,128,128]{3,2,1,0:T(8,128)(2,1)}, bf16[8,4,128,128]{3,2,1,0:T(8,128)(2,1)S(1)}, u32[]{:S(2)}) copy-start(bf16[8,4,128,128]{3,2,1,0:T(8,128)(2,1)S(1)} %multiply_convert_fusion.2) | copy-start | bytes 3145732
  93.2 12.5 %collective-permute-start.5 = (bf16[8,9,1024]{2,1,0:T(8,128)(2,1)S(1)}, bf16[8,9,1024]{2,1,0:T(8,128)(2,1)S(1)}, u32[]{:S(2)}, u32[]{:S(2)}) collective-permute-start(bf16[8,9,1024]{2,1,0:T(8,128)(2,1)S(1)} %get-tuple-element.87), channel_id=1, source_target_pairs={{1,0},{2,1},{3,2},{4,3},{5,4},{6,5},{7,6},{9,8},{10,9},{11,10},{12... | collective-permute-start | bytes 442376 | tf_op jit(solution)/shard_map/ppermute | solution.py:27
  95.1 6.9 %collective-permute-start.4 = (bf16[8,9,1024]{2,1,0:T(8,128)(2,1)S(1)}, bf16[8,9,1024]{2,1,0:T(8,128)(2,1)S(1)}, u32[]{:S(2)}, u32[]{:S(2)}) collective-permute-start(bf16[8,9,1024]{2,1,0:T(8,128)(2,1)S(1)} %get-tuple-element.88), channel_id=1, source_target_pairs={{0,1},{1,2},{2,3},{3,4},{4,5},{5,6},{6,7},{8,9},{9,10},{10,11},{11... | collective-permute-start | bytes 442376 | tf_op jit(solution)/shard_map/ppermute | solution.py:27
  109.6 2.6 copy-start.15
  112.2 1.2 copy-start.11
  113.5 1.2 copy-start.16
  120.1 3.3 copy-start.3
  134.2 7.7 %collective-permute-start.7 = (f32[8,1,512]{2,1,0:T(1,128)S(1)}, f32[8,1,512]{2,1,0:T(1,128)S(1)}, u32[]{:S(2)}, u32[]{:S(2)}) collective-permute-start(f32[8,1,512]{2,1,0:T(1,128)S(1)} %get-tuple-element.93), channel_id=1, source_target_pairs={{1,0},{2,1},{3,2},{4,3},{5,4},{6,5},{7,6},{9,8},{10,9},{11,10},{12... | collective-permute-start | bytes 49160 | tf_op jit(solution)/shard_map/ppermute | solution.py:27
  136.1 5.6 %collective-permute-start.6 = (f32[8,1,512]{2,1,0:T(1,128)S(1)}, f32[8,1,512]{2,1,0:T(1,128)S(1)}, u32[]{:S(2)}, u32[]{:S(2)}) collective-permute-start(f32[8,1,512]{2,1,0:T(1,128)S(1)} %get-tuple-element.94), channel_id=1, source_target_pairs={{0,1},{1,2},{2,3},{3,4},{4,5},{5,6},{6,7},{8,9},{9,10},{10,11},{11... | collective-permute-start | bytes 49160 | tf_op jit(solution)/shard_map/ppermute | solution.py:27
  349.1 4.0 %copy-start.13 = (f32[512,512]{1,0:T(8,128)S(1)}, f32[512,512]{1,0:T(8,128)}, u32[]{:S(2)}) copy-start(f32[512,512]{1,0:T(8,128)} %get-tuple-element.138) | copy-start | bytes 3145732
  349.1 5.0 %copy-start.9 = (f32[512,2048]{1,0:T(8,128)S(1)}, f32[512,2048]{1,0:T(8,128)}, u32[]{:S(2)}) copy-start(f32[512,2048]{1,0:T(8,128)} %get-tuple-element.140) | copy-start | bytes 12582916
  354.1 3.7 %copy-start.8 = (f32[2048,512]{1,0:T(8,128)S(1)}, f32[2048,512]{1,0:T(8,128)}, u32[]{:S(2)}) copy-start(f32[2048,512]{1,0:T(8,128)} %get-tuple-element.141) | copy-start | bytes 12582916
  357.8 3.1 copy-start.1
Sparse Core Ops, SparseCore 0:
  116.8 232.2 all-reduce.24
where the time goes:
time: 375 us; the launch traced here: 368 us
  waiting for transfers between devices  167 us (45%)
  matrix products  57.2 us (15%)
  blocking collectives  43.1 us (11%)
  local copies, waits for them, and re-layouts  34.2 us (9%)
  other arithmetic  28.1 us (7%)
  starting transfers between devices  23.3 us (6%)
  between operations  14.9 us (4%)
    psum x1, waiting for transfers between devices, shards(): lax.psum((d_gain_one, d_kernel, d_qkv, d_out, d_gain_two, d_up, d_down, d...  159 us
    psum x1, blocking collectives, shards(): lax.psum((d_gain_one, d_kernel, d_qkv, d_out, d_gain_two, d_up, d_down, d...  43.1 us
    unnamed x53, local copies, waits for them, and re-layouts  19 us
    ppermute x4, starting transfers between devices, from_behind(): return lax.ppermute(shard, axis, pairs)  12.2 us
    dot_general x6, matrix products, project(): jnp.einsum('std,de->ste', acts, weight, preferred_element_type=jnp.float32)  10.4 us
  transfers between devices with their start and end apart: 9, of which 5 were waited for; matrix products, arithmetic and copies ran while one was open for 8% of the time, Pallas kernels for 0%

commit v1 on v0

--- a/solution.py
+++ b/solution.py
@@ -1,7 +1,213 @@
+import functools
+
 import jax
 import jax.numpy as jnp
 from jax import lax
+from jax.experimental import pallas as pl
+from jax.experimental.pallas import tpu as pltpu
 from jax.sharding import PartitionSpec as P
+
+MESH = pl.DeviceIdType.MESH
+
+
+def bit_orders(seq_size, tm_size):
+    seq_bits = [("seq", b) for b in range(seq_size.bit_length() - 1)]
+    tm_bits = [("tm", b) for b in range(tm_size.bit_length() - 1)]
+    core, rest = tm_bits[:1], tm_bits[1:]
+    first = core + seq_bits + rest
+    second = core + seq_bits[::-1] + rest
+    third = core + rest[:1] + seq_bits + rest[1:]
+    fourth = core + rest[:1] + seq_bits[::-1] + rest[1:]
+    return [first, second, third, first, second, fourth]
+
+
+def partner_of(axis, bit):
+    me = lax.axis_index(axis)
+    mine = lax.rem(me // (1 << bit), 2)
+    other = me + (1 - 2 * mine) * (1 << bit)
+    if axis == "seq":
+        return mine, (other, lax.axis_index("tm"))
+    return mine, (lax.axis_index("seq"), other)
+
+
+def add_rows(dst, dst_at, left, left_at, right, right_at, rows):
+    step = min(rows, 32)
+
+    def body(i, carry):
+        off = pl.multiple_of(i * step, step)
+        a = left[pl.ds(left_at + off, step), :].astype(jnp.float32)
+        b = right[pl.ds(right_at + off, step), :].astype(jnp.float32)
+        dst[pl.ds(dst_at + off, step), :] = (a + b).astype(jnp.bfloat16)
+        return carry
+
+    lax.fori_loop(0, rows // step, body, 0)
+
+
+class Reducer:
+    def __init__(self, orders, rows, part, acc, recv, full, sems):
+        self.orders, self.rows = orders, rows
+        self.part, self.acc, self.recv, self.full = part, acc, recv, full
+        self.rs_send, self.rs_recv, self.ag_send, self.ag_recv = sems
+
+    def levels(self):
+        return len(self.orders[0])
+
+    def start_of(self, level):
+        return self.rows - (self.rows >> level)
+
+    def source(self, unit, level):
+        if level == 0:
+            return self.part.at[unit], 0
+        return self.acc.at[unit], self.start_of(level - 1)
+
+    def scatter_copy(self, unit, level):
+        mine, peer = partner_of(*self.orders[unit % len(self.orders)][level])
+        half = self.rows >> (level + 1)
+        ref, base = self.source(unit, level)
+        off = pl.multiple_of(base + (1 - mine) * half, 16)
+        return pltpu.make_async_remote_copy(
+            src_ref=ref.at[pl.ds(off, half)],
+            dst_ref=self.recv.at[unit, pl.ds(self.start_of(level), half)],
+            send_sem=self.rs_send.at[unit, level],
+            recv_sem=self.rs_recv.at[unit, level],
+            device_id=peer,
+            device_id_type=MESH,
+        )
+
+    def owned(self, unit, level):
+        off = 0
+        order = self.orders[unit % len(self.orders)]
+        for i in range(level + 1):
+            mine, _ = partner_of(*order[i])
+            off = off + mine * (self.rows >> (i + 1))
+        return pl.multiple_of(off, 16), self.rows >> (level + 1)
+
+    def gather_copy(self, unit, level):
+        _, peer = partner_of(*self.orders[unit % len(self.orders)][level])
+        off, size = self.owned(unit, level)
+        return pltpu.make_async_remote_copy(
+            src_ref=self.full.at[unit, pl.ds(off, size)],
+            dst_ref=self.full.at[unit, pl.ds(off, size)],
+            send_sem=self.ag_send.at[unit, level],
+            recv_sem=self.ag_recv.at[unit, level],
+            device_id=peer,
+            device_id_type=MESH,
+        )
+
+    def combine(self, unit, level):
+        self.scatter_copy(unit, level).wait_recv()
+        mine, _ = partner_of(*self.orders[unit % len(self.orders)][level])
+        half = self.rows >> (level + 1)
+        ref, base = self.source(unit, level)
+        off = pl.multiple_of(base + mine * half, 16)
+        if level == self.levels() - 1:
+            at, _ = self.owned(unit, level)
+            dst = self.full.at[unit]
+        else:
+            at, dst = self.start_of(level), self.acc.at[unit]
+        add_rows(dst, at, ref, off, self.recv.at[unit], self.start_of(level), half)
+
+    def wait_sends(self, unit):
+        for level in range(self.levels()):
+            self.scatter_copy(unit, level).wait_send()
+            self.gather_copy(unit, level).wait_send()
+
+
+def enter(bits):
+    barrier = pltpu.get_barrier_semaphore()
+    for axis, bit in bits:
+        _, peer = partner_of(axis, bit)
+        pl.semaphore_signal(barrier, inc=1, device_id=peer, device_id_type=MESH)
+    pl.semaphore_wait(barrier, len(bits))
+
+
+def reduce_kernel(
+    orders, units, rows, part_hbm, small_ref, full_hbm, small_out,
+    part, acc, recv, full, small_recv, small_acc,
+    in_sem, out_sem, rs_send, rs_recv, ag_send, ag_recv, sm_send, sm_recv,
+):
+    levels = len(orders[0])
+    red = Reducer(orders, rows, part, acc, recv, full, (rs_send, rs_recv, ag_send, ag_recv))
+    loads = [pltpu.make_async_copy(part_hbm.at[u], part.at[u], in_sem.at[u]) for u in range(units)]
+    for load in loads:
+        load.start()
+    enter(orders[0])
+
+    def small_copy(level):
+        _, peer = partner_of(*orders[0][level])
+        src = small_ref if level == 0 else small_acc.at[level - 1]
+        return pltpu.make_async_remote_copy(
+            src_ref=src, dst_ref=small_recv.at[level],
+            send_sem=sm_send.at[level], recv_sem=sm_recv.at[level],
+            device_id=peer, device_id_type=MESH,
+        )
+
+    for level in range(levels):
+        for u in range(units):
+            if level == 0:
+                loads[u].wait()
+            else:
+                red.combine(u, level - 1)
+            red.scatter_copy(u, level).start()
+        if level > 0:
+            small_copy(level - 1).wait_recv()
+            prev = small_ref[...] if level == 1 else small_acc[level - 2]
+            small_acc[level - 1] = prev + small_recv[level - 1]
+        small_copy(level).start()
+    small_copy(levels - 1).wait_recv()
+    small_out[...] = small_acc[levels - 2] + small_recv[levels - 1]
+    for level in range(levels - 1, -1, -1):
+        for u in range(units):
+            if level == levels - 1:
+                red.combine(u, level)
+            else:
+                red.gather_copy(u, level + 1).wait_recv()
+            red.gather_copy(u, level).start()
+    outs = [pltpu.make_async_copy(full.at[u], full_hbm.at[u], out_sem.at[u]) for u in range(units)]
+    for u in range(units):
+        red.gather_copy(u, 0).wait_recv()
+        outs[u].start()
+    for level in range(levels):
+        small_copy(level).wait_send()
+    for u in range(units):
+        red.wait_sends(u)
+        outs[u].wait()
+
+
+def reduce_all(parts, small, seq_size, tm_size):
+    units, rows, cols = parts.shape
+    orders = bit_orders(seq_size, tm_size)
+    levels = len(orders[0])
+    buf = pltpu.VMEM((units, rows, cols), jnp.bfloat16)
+    dma = pltpu.SemaphoreType.DMA
+    return pl.pallas_call(
+        functools.partial(reduce_kernel, orders, units, rows),
+        out_shape=(
+            jax.ShapeDtypeStruct(parts.shape, jnp.bfloat16),
+            jax.ShapeDtypeStruct(small.shape, jnp.float32),
+        ),
+        in_specs=[
+            pl.BlockSpec(memory_space=pl.ANY),
+            pl.BlockSpec(memory_space=pltpu.VMEM),
+        ],
+        out_specs=(
+            pl.BlockSpec(memory_space=pl.ANY),
+            pl.BlockSpec(memory_space=pltpu.VMEM),
+        ),
+        scratch_shapes=[
+            buf, buf, buf, buf,
+            pltpu.VMEM((levels,) + small.shape, jnp.float32),
+            pltpu.VMEM((levels,) + small.shape, jnp.float32),
+            dma((units,)), dma((units,)),
+            dma((units, levels)), dma((units, levels)),
+            dma((units, levels)), dma((units, levels)),
+            dma((levels,)), dma((levels,)),
+        ],
+        compiler_params=pltpu.CompilerParams(
+            collective_id=0, has_side_effects=True, vmem_limit_bytes=48 << 20
+        ),
+    )(parts, small)
+
 
 HEADS = 4
 HD = 128
@@ -212,20 +418,34 @@
     first_pull = jax.vjp(layer_norm, inputs_f, gain_one)[1]
     d_in_part, d_gain_one = first_pull(d_normed)
     d_inputs = d_residual + d_in_part
-    totals = lax.psum(
-        (d_gain_one, d_kernel, d_qkv, d_out, d_gain_two, d_up, d_down, d_scale), ("seq", "tm")
-    )
+    cols = features
+    pack = lambda w: w.astype(jnp.bfloat16)
+    d_up_rows = pack(d_up).reshape(cols, -1, cols).transpose(1, 0, 2).reshape(-1, cols)
+    flat = jnp.concatenate(
+        [pack(d_down), d_up_rows, pack(d_out), pack(d_qkv).reshape(-1, cols)], axis=0
+    )
+    sizes = (lax.axis_size("seq"), lax.axis_size("tm"))
+    rows = max(512, 16 * sizes[0] * sizes[1])
+    small = jnp.concatenate(
+        [
+            d_kernel.reshape(9, cols), d_gain_one[None], d_gain_two[None], d_scale[None],
+            jnp.zeros((4, cols), jnp.float32),
+        ],
+        axis=0,
+    )
+    full, small = reduce_all(flat.reshape(-1, rows, cols), small, *sizes)
+    full = full.reshape(-1, cols)
+    hidden_size = down_weight.shape[0]
+    wide = lambda w: w.astype(jnp.float32)
+    sum_down = wide(full[:hidden_size])
+    sum_up = wide(
+        full[hidden_size : 2 * hidden_size].reshape(-1, cols, cols).transpose(1, 0, 2)
+    ).reshape(cols, hidden_size)
+    sum_out = wide(full[2 * hidden_size : 2 * hidden_size + cols])
+    sum_qkv = wide(full[2 * hidden_size + cols :]).reshape(3, cols, cols)
     return (
-        output,
-        d_inputs,
-        totals[0],
-        totals[1],
-        totals[2],
-        totals[3],
-        totals[4],
-        totals[5],
-        totals[6],
-        totals[7],
+        output, d_inputs, small[9], small[:9].reshape(3, 3, cols), sum_qkv, sum_out,
+        small[10], sum_up, sum_down, small[11],
     )
 
 

time: 375 us -> 274 us (0.73)
  waiting for transfers between devices: 167 us -> 10 us
  Pallas kernels: 0 us -> 74.9 us
  blocking collectives: 43.1 us -> 0 us
  other arithmetic: 28.1 us -> 63.2 us
  between operations: 14.9 us -> 1.97 us
    psum x1 -> x0, waiting for transfers between devices: 159 us -> none  [shards(): lax.psum((d_gain_one, d_kernel, d_qkv, d_out, d_gain_two, d_up, d_down, d...]
    pallas_call x0 -> x1, Pallas kernels: none -> 74.9 us  [reduce_all(): pl.pallas_call(functools.partial(reduce_kernel, orders, units, rows), out...]
    psum x1 -> x0, blocking collectives: 43.1 us -> none  [shards(): lax.psum((d_gain_one, d_kernel, d_qkv, d_out, d_gain_two, d_up, d_down, d...]
    concatenate x0 -> x1, other arithmetic: none -> 19.2 us  [shards(): jnp.concatenate([pack(d_down), d_up_rows, pack(d_out), pack(d_qkv).reshap...]
    convert_element_type x0 -> x3, other arithmetic: none -> 9.86 us  [shards(): wide = lambda w: w.astype(jnp.float32)]
    reshape x0 -> x4, local copies, waits for them, and re-layouts: none -> 6.06 us  [the longest x1 5.24 us: shards(): sum_up = wide(full[hidden_size:2 * hidden_size].reshape(-1, cols, cols).t...]
    slice x0 -> x1, other arithmetic: none -> 5.82 us  [shards(): sum_down = wide(full[:hidden_size])]
    unnamed x53 -> x62, local copies, waits for them, and re-layouts: 19 us -> 14.9 us
  transfers between devices with their start and end apart: 9 -> 8, of which waited for: 5 -> 4; matrix products, arithmetic and copies ran while one was open for 8% -> 11% of each run, Pallas kernels for 0% -> 0%
where the time goes in v1:
time: 274 us; the launch traced here: 269 us
  Pallas kernels  74.9 us (27%)
  other arithmetic  63.2 us (23%)
  matrix products  58.7 us (21%)
  local copies, waits for them, and re-layouts  37.5 us (14%)
  starting transfers between devices  23.2 us (8%)
  waiting for transfers between devices  10 us (4%)
    pallas_call x1, Pallas kernels, reduce_all(): pl.pallas_call(functools.partial(reduce_kernel, orders, units, rows), out...  74.9 us
    concatenate x1, other arithmetic, shards(): jnp.concatenate([pack(d_down), d_up_rows, pack(d_out), pack(d_qkv).reshap...  19.2 us
    unnamed x62, local copies, waits for them, and re-layouts  14.9 us
    dot_general x6, matrix products, project(): jnp.einsum('std,de->ste', acts, weight, preferred_element_type=jnp.float32)  12.3 us
    ppermute x4, starting transfers between devices, from_behind(): return lax.ppermute(shard, axis, pairs)  12.1 us
    convert_element_type x3, other arithmetic, shards(): wide = lambda w: w.astype(jnp.float32)  9.86 us
    dot_general x1, matrix products, shards(): jnp.einsum('std,fd->stf', d_mlp, down_weight, preferred_element_type=jnp....  9.11 us
    dot_general x1, matrix products, shards(): jnp.einsum('ste,de->std', d_value_low, qkv_weight[2], preferred_element_t...  7.16 us
  transfers between devices with their start and end apart: 8, of which 4 were waited for; matrix products, arithmetic and copies ran while one was open for 11% of the time, Pallas kernels for 0%

profile of v1, /device:TPU:1, one launch (start us, length us, event | category | flops | bytes accessed | tf_op | source)
XLA Modules:
  0.0 269.5 jit_solution(16429048159692772216)
XLA Ops:
  1.5 1.5 convert_reduce_fusion
  3.0 1.7 fusion.15
  5.2 1.0 copy-done.10
  6.1 4.6 %collective-permute-start = (bf16[8,1,512]{2,1,0:T(2,128)(2,1)S(1)}, bf16[8,1,512]{2,1,0:T(2,128)(2,1)S(1)}, u32[]{:S(2)}, u32[]{:S(2)}) collective-permute-start(bf16[8,1,512]{2,1,0:T(2,128)(2,1)S(1)} %get-tuple-element.128), channel_id=1, source_target_pairs={{0,1},{1,2},{2,3},{3,4},{4,5},{5,6},{6,7},{8,9},{9,10},{10,11},{11... | collective-permute-start | bytes 24584 | tf_op jit(solution)/shard_map/ppermute | solution.py:224
  10.7 1.9 collective-permute-start.1
  13.9 1.9 collective-permute-done.1
  15.8 1.6 maximum_convert_fusion
  17.4 1.0 add_convert_fusion.2
  18.4 1.2 copy-done.18
  20.6 1.6 add_convert_fusion.1
  23.2 1.9 collective-permute-start.2
  25.1 2.6 collective-permute-start.3
  28.5 4.3 %collective-permute-done.3 = bf16[8,9,1024]{2,1,0:T(8,128)(2,1)S(1)} collective-permute-done((bf16[8,9,1024]{2,1,0:T(8,128)(2,1)S(1)}, bf16[8,9,1024]{2,1,0:T(8,128)(2,1)S(1)}, u32[]{:S(2)}, u32[]{:S(2)}) %collective-permute-start.3) | collective-permute-done | bytes 147488 | tf_op jit(solution)/shard_map/ppermute | solution.py:225
  32.8 0.9 pad_maximum_fusion.1
  33.9 0.9 copy_bitcast_fusion.3
  34.9 1.2 select_reduce_fusion
  36.8 1.6 convolution_convert_fusion
  39.7 1.1 copy-done.28
  40.8 2.4 fusion.27
  43.3 3.2 %copy-done.29 = f32[8,128,2048]{2,1,0:T(8,128)} copy-done((f32[8,128,2048]{2,1,0:T(8,128)}, f32[8,128,2048]{2,1,0:T(8,128)S(1)}, u32[]{:S(2)}) %copy-start.29) | copy-done | bytes 8388632
  46.5 5.3 %bitcast_convert_fusion.1 = bf16[2048,512]{1,0:T(8,128)(2,1)} fusion(bf16[8,128,512]{2,1,0:T(8,128)(2,1)S(1)} %copy-done.11, f32[512]{0:T(512)S(1)} %convert_element_type.179, f32[8,128,2048]{2,1,0:T(8,128)S(1)} %fusion.27), kind=kOutput, calls=%fused_computation.12 | convolution fusion | flops 2168979456 | bytes 11536384 | tf_op jit(solution)/shard_map/stf,std->fd/dot_general | solution.py:344
  51.8 9.1 %fusion.6 = bf16[8,128,2048]{2,1,0:T(8,128)(2,1)S(1)} fusion(f32[8,128,2048]{2,1,0:T(8,128)} %copy-done.29, bf16[2048,512]{1,0:T(8,128)(2,1)S(1)} %copy-done, bf16[8,128,512]{2,1,0:T(8,128)(2,1)S(1)} %copy-done.11, f32[512]{0:T(512)S(1)} %convert_element_type.179), kind=kOutput, calls=%fused_computation.8 | convolution fusion | flops 2190999552 | bytes 15730688 | tf_op jit(solution)/shard_map/std,fd->stf/dot_general | solution.py:345
  61.0 2.7 bitcast_convert_fusion
  63.6 2.8 %multiply_reduce_fusion.1 = (f32[512]{0:T(512)S(1)}, f32[8,128]{1,0:T(8,128)S(1)}, f32[8,128,512]{2,1,0:T(8,128)S(1)}) fusion(f32[8,128,512]{2,1,0:T(8,128)S(1)} %get-tuple-element.148, f32[8,128]{1,0:T(8,128)S(1)} %fusion.84, f32[8,128]{1,0:T(8,128)S(1)} %broadcast_multiply_fusion, f32[512]{0:T(512)S(1)} %convert_element_type.180, ...), kind=kOutput, calls=%fused_computation.57 | convolution fusion | flops 2151152128 | bytes 10502144 | tf_op jit(solution)/shard_map/stf,df->std/dot_general | solution.py:349
  66.4 6.9 %fusion.18 = (f32[512]{0:T(512)S(1)}, bf16[8,128,512]{2,1,0:T(8,128)(2,1)}, f32[8,128]{1,0:T(8,128)S(1)}, f32[8,128,512]{2,1,0:T(8,128)S(1)}) fusion(bf16[8,128,512]{2,1,0:T(8,128)(2,1)S(1)} %copy-done.11, f32[8,128,512]{2,1,0:T(8,128)S(1)} %get-tuple-element.148, f32[512]{0:T(512)S(1)} %convert_element_type.179, ...), kind=kOutput, calls=%fused_computation.46 | convolution fusion | flops 2173172224 | bytes 18896896 | tf_op jit(solution)/shard_map/std,de->ste/dot_general | solution.py:263
  73.7 1.0 copy-done.8
  74.7 1.5 fusion.33
  76.9 1.4 multiply_reduce_fusion
  79.1 0.9 multiply_convert_fusion.1
  80.0 1.3 multiply_convert_fusion.2
  82.1 1.4 copy.138
  83.5 1.4 copy.139
  84.9 1.4 copy_dynamic-update-slice_fusion.1
  86.3 1.4 copy_dynamic-update-slice_fusion
  88.3 2.5 slice.371
  91.0 2.1 fusion.67
  93.9 1.9 collective-permute-start.5
  95.8 3.6 %collective-permute-start.4 = (bf16[8,9,1024]{2,1,0:T(8,128)(2,1)S(1)}, bf16[8,9,1024]{2,1,0:T(8,128)(2,1)S(1)}, u32[]{:S(2)}, u32[]{:S(2)}) collective-permute-start(bf16[8,9,1024]{2,1,0:T(8,128)(2,1)S(1)} %get-tuple-element.106), channel_id=1, source_target_pairs={{0,1},{1,2},{2,3},{3,4},{4,5},{5,6},{6,7},{8,9},{9,10},{10,11},{11... | collective-permute-start | bytes 442376 | tf_op jit(solution)/shard_map/ppermute | solution.py:233
  99.5 1.6 fusion.41
  101.0 1.7 collective-permute-done.4
  102.7 0.9 slice_add_fusion.1
  103.6 3.6 %scatter-add.14 = f32[8,128,1024]{2,1,0:T(8,128)} dynamic-update-slice(f32[8,128,1024]{2,1,0:T(8,128)} %slice.371, f32[8,9,1024]{2,1,0:T(8,128)} %slice_add_fusion.1, s32[]{:T(128)} %constant.154.clone.1, s32[]{:T(128)} %constant.154.clone.1, s32[]{:T(128)} %constant.154.clone.1) | dynamic-update-slice | bytes 589828 | tf_op jit(solution)/shard_map/scatter-add | solution.py:388
  107.2 1.9 slice_add_fusion
  109.2 3.0 %scatter-add.15 = f32[8,128,1024]{2,1,0:T(8,128)} dynamic-update-slice(f32[8,128,1024]{2,1,0:T(8,128)} %scatter-add.14, f32[8,9,1024]{2,1,0:T(8,128)} %slice_add_fusion, s32[]{:T(128)} %constant.154.clone.1, s32[]{:T(128)} %constant.168.clone.1, s32[]{:T(128)} %constant.154.clone.1) | dynamic-update-slice | bytes 589828 | tf_op jit(solution)/shard_map/scatter-add | solution.py:388
  112.2 2.6 convert.33
  114.8 1.6 fusion.39
  116.4 1.6 fusion.40
  117.9 3.3 %fusion.57 = f32[8,128,512]{2,1,0:T(8,128)} fusion(bf16[8,128,1024]{2,1,0:T(8,128)(2,1)S(1)} %convert.33, bf16[3,512,512]{2,1,0:T(8,128)(2,1)} %param.23), kind=kOutput, calls=%fused_computation.128 | convolution fusion | flops 536870912 | bytes 3670016 | tf_op jit(solution)/shard_map/ste,de->std/dot_general | solution.py:402
  121.2 7.2 %multiply_reduce_fusion.4 = (f32[512]{0:T(512)S(1)}, f32[512]{0:T(512)S(1)}, f32[512]{0:T(512)S(1)}, f32[512]{0:T(512)S(1)}, f32[512]{0:T(512)S(1)}, /*index=5*/...) fusion(f32[8,128,512]{2,1,0:T(8,128)} %fusion.67, ...), kind=kOutput, calls=%fused_computation.60 | convolution fusion | flops 555740672 | bytes 30982144 | tf_op jit(solution)/shard_map/ste,de->std/dot_general | solution.py:403
  128.4 4.1 %pad_add_fusion = f32[8,130,512]{2,1,0:T(8,128)S(1)} fusion(f32[8,128,512]{2,1,0:T(8,128)S(1)} %get-tuple-element.119, f32[8,128,512]{2,1,0:T(8,128)} %get-tuple-element.120, f32[8,128,512]{2,1,0:T(8,128)} %get-tuple-element.121, f32[8,128,512]{2,1,0:T(8,128)S(1)} %get-tuple-element.114, f32[8,128,512]{2,1,0:T(8,128)S(1)} %get-tuple-element.116, ...), kind=kLoop, calls=%fused_computation.40 | loop fusion | flops 4259840 | bytes 21004288 | tf_op jit(solution)/shard_map/transpose(jvp())/add_any | solution.py:258
  132.6 4.7 %collective-permute-start.6 = (f32[8,1,512]{2,1,0:T(1,128)S(1)}, f32[8,1,512]{2,1,0:T(1,128)S(1)}, u32[]{:S(2)}, u32[]{:S(2)}) collective-permute-start(f32[8,1,512]{2,1,0:T(1,128)S(1)} %get-tuple-element.112), channel_id=1, source_target_pairs={{0,1},{1,2},{2,3},{3,4},{4,5},{5,6},{6,7},{8,9},{9,10},{10,11},{11... | collective-permute-start | bytes 49160 | tf_op jit(solution)/shard_map/ppermute | solution.py:233
  137.5 19.2 %pad_maximum_fusion = bf16[6144,512]{1,0:T(8,128)(2,1)} fusion(bf16[1536,512]{1,0:T(8,128)(2,1)S(1)} %bitcast.187, bf16[512,512]{1,0:T(8,128)(2,1)S(1)} %copy-done.19, bf16[2048,512]{1,0:T(8,128)(2,1)S(1)} %bitcast.186, bf16[2048,512]{1,0:T(8,128)(2,1)S(1)} %copy-done.13), kind=kLoop, calls=%fused_computation.10 | loop fusion | flops 25165824 | bytes 12582912 | tf_op jit(solution)/shard_map/concatenate | solution.py:424
  157.0 1.9 collective-permute-start.7
  159.0 0.9 slice_add_fusion.3
  160.0 2.1 collective-permute-done.7
  162.9 1.5 fusion.14
  164.4 74.9 %shard_map.186 = (bf16[12,512,512]{2,1,0:T(8,128)(2,1)}, f32[16,512]{1,0:T(8,128)S(1)}) custom-call(bf16[12,512,512]{2,1,0:T(8,128)(2,1)} %bitcast.182, f32[16,512]{1,0:T(8,128)S(1)} %concatenate.32.small_ref), custom_call_target="tpu_custom_call" | custom-call | tf_op jit(solution)/shard_map/pallas_call | solution.py:183
  239.3 2.1 bitcast_convert_fusion.3
  241.5 3.5 %slice_convert_fusion = f32[3,512,512]{2,1,0:T(8,128)} fusion(bf16[12,512,512]{2,1,0:T(8,128)(2,1)} %get-tuple-element.61), kind=kLoop, calls=%fused_computation.88 | loop fusion | flops 786432 | bytes 4718592 | tf_op jit(solution)/shard_map/convert_element_type | solution.py:439
  245.0 5.8 %fusion.90 = (bf16[4,512,512]{2,1,0:T(8,128)(2,1)}, f32[512,4,512]{2,0,1:T(8,128)}) fusion(bf16[12,512,512]{2,1,0:T(8,128)(2,1)} %get-tuple-element.61), kind=kLoop, calls=%fused_computation.189 | loop fusion | flops 1048576 | bytes 10485760 | tf_op jit(solution)/shard_map/slice | solution.py:440
  250.8 2.0 add_add_fusion.2
  254.1 4.2 %bitcast_convert_fusion.2 = f32[2048,512]{1,0:T(8,128)} fusion(bf16[4,512,512]{2,1,0:T(8,128)(2,1)} %get-tuple-element.103), kind=kLoop, calls=%fused_computation.48 | loop fusion | flops 1048576 | bytes 6291456 | tf_op jit(solution)/shard_map/convert_element_type | solution.py:439
  258.3 5.2 %copy.86 = f32[512,4,512]{0,2,1:T(8,128)} copy(f32[512,4,512]{2,0,1:T(8,128)} %get-tuple-element.104) | data formatting | bytes 8388608 | tf_op jit(solution)/shard_map/reshape | solution.py:443
  263.5 5.5 %copy.87 = f32[512,2048]{1,0:T(8,128)} copy(f32[512,2048]{0,1:T(8,128)} %bitcast.183) | data formatting | bytes 8388608
  (116 shorter events, 14.2 us)
Async XLA Ops:
  0.6 51.2 %copy-start = (bf16[2048,512]{1,0:T(8,128)(2,1)S(1)}, bf16[2048,512]{1,0:T(8,128)(2,1)}, u32[]{:S(2)}) copy-start(bf16[2048,512]{1,0:T(8,128)(2,1)} %param.27) | copy-start | bytes 6291460
  0.7 4.1 %copy-start.4 = (bf16[8,128,512]{2,1,0:T(8,128)(2,1)S(1)}, bf16[8,128,512]{2,1,0:T(8,128)(2,1)}, u32[]{:S(2)}) copy-start(bf16[8,128,512]{2,1,0:T(8,128)(2,1)} %param.19) | copy-start | bytes 3145732
  1.5 11.2 %copy-start.25 = (s32[8,8]{1,0:T(8,128)S(1)}, s32[8,8]{1,0:T(8,128)}, u32[]{:S(2)}) copy-start(s32[8,8]{1,0:T(8,128)} %param.20) | copy-start | bytes 772
  1.5 11.7 %copy-start.24 = (bf16[3,3,512]{2,1,0:T(4,128)(2,1)S(1)}, bf16[3,3,512]{2,1,0:T(4,128)(2,1)}, u32[]{:S(2)}) copy-start(bf16[3,3,512]{2,1,0:T(4,128)(2,1)} %param.22) | copy-start | bytes 27652
  1.5 12.4 %copy-start.26 = (bf16[512]{0:T(512)(128)(2,1)S(1)}, bf16[512]{0:T(512)(128)(2,1)}, u32[]{:S(2)}) copy-start(bf16[512]{0:T(512)(128)(2,1)} %param.25) | copy-start | bytes 3076
  1.5 12.4 %copy-start.27 = (bf16[512]{0:T(512)(128)(2,1)S(1)}, bf16[512]{0:T(512)(128)(2,1)}, u32[]{:S(2)}) copy-start(bf16[512]{0:T(512)(128)(2,1)} %param.28) | copy-start | bytes 3076
  5.1 1.0 copy-start.10
  6.1 7.8 %collective-permute-start = (bf16[8,1,512]{2,1,0:T(2,128)(2,1)S(1)}, bf16[8,1,512]{2,1,0:T(2,128)(2,1)S(1)}, u32[]{:S(2)}, u32[]{:S(2)}) collective-permute-start(bf16[8,1,512]{2,1,0:T(2,128)(2,1)S(1)} %get-tuple-element.128), channel_id=1, source_target_pairs={{0,1},{1,2},{2,3},{3,4},{4,5},{5,6},{6,7},{8,9},{9,10},{10,11},{11... | collective-permute-start | bytes 24584 | tf_op jit(solution)/shard_map/ppermute | solution.py:224
  10.7 5.1 %collective-permute-start.1 = (bf16[8,1,512]{2,1,0:T(2,128)(2,1)S(1)}, bf16[8,1,512]{2,1,0:T(2,128)(2,1)S(1)}, u32[]{:S(2)}, u32[]{:S(2)}) collective-permute-start(bf16[8,1,512]{2,1,0:T(2,128)(2,1)S(1)} %get-tuple-element.129), channel_id=1, source_target_pairs={{1,0},{2,1},{3,2},{4,3},{5,4},{6,5},{7,6},{9,8},{10,9},{11,10},{12... | collective-permute-start | bytes 24584 | tf_op jit(solution)/shard_map/ppermute | solution.py:225
  17.4 3.2 %copy-start.2 = (f32[8,130,512]{2,1,0:T(8,128)}, f32[8,130,512]{2,1,0:T(8,128)S(1)}, u32[]{:S(2)}) copy-start(f32[8,130,512]{2,1,0:T(8,128)S(1)} %maximum_convert_fusion) | copy-start | bytes 6389764
  17.4 2.2 copy-start.18
  19.6 1.0 copy-start.16
  22.2 1.0 copy-start.14
  23.2 5.3 %collective-permute-start.2 = (bf16[8,9,1024]{2,1,0:T(8,128)(2,1)S(1)}, bf16[8,9,1024]{2,1,0:T(8,128)(2,1)S(1)}, u32[]{:S(2)}, u32[]{:S(2)}) collective-permute-start(bf16[8,9,1024]{2,1,0:T(8,128)(2,1)S(1)} %get-tuple-element.126), channel_id=1, source_target_pairs={{0,1},{1,2},{2,3},{3,4},{4,5},{5,6},{6,7},{8,9},{9,10},{10,11},{11... | collective-permute-start | bytes 442376 | tf_op jit(solution)/shard_map/ppermute | solution.py:224
  25.1 7.7 %collective-permute-start.3 = (bf16[8,9,1024]{2,1,0:T(8,128)(2,1)S(1)}, bf16[8,9,1024]{2,1,0:T(8,128)(2,1)S(1)}, u32[]{:S(2)}, u32[]{:S(2)}) collective-permute-start(bf16[8,9,1024]{2,1,0:T(8,128)(2,1)S(1)} %get-tuple-element.127), channel_id=1, source_target_pairs={{1,0},{2,1},{3,2},{4,3},{5,4},{6,5},{7,6},{9,8},{10,9},{11,10},{12... | collective-permute-start | bytes 442376 | tf_op jit(solution)/shard_map/ppermute | solution.py:225
  36.8 1.6 copy-start.23
  39.3 1.6 copy-start.28
  40.8 5.6 %copy-start.11 = (bf16[8,128,512]{2,1,0:T(8,128)(2,1)S(1)}, bf16[8,128,512]{2,1,0:T(8,128)(2,1)}, u32[]{:S(2)}) copy-start(bf16[8,128,512]{2,1,0:T(8,128)(2,1)} %param.29) | copy-start | bytes 3145732
  43.3 3.2 %copy-start.29 = (f32[8,128,2048]{2,1,0:T(8,128)}, f32[8,128,2048]{2,1,0:T(8,128)S(1)}, u32[]{:S(2)}) copy-start(f32[8,128,2048]{2,1,0:T(8,128)S(1)} %fusion.27) | copy-start | bytes 25165828
  73.3 1.3 copy-start.8
  93.9 13.3 %collective-permute-start.5 = (bf16[8,9,1024]{2,1,0:T(8,128)(2,1)}, bf16[8,9,1024]{2,1,0:T(8,128)(2,1)S(1)}, u32[]{:S(2)}, u32[]{:S(2)}) collective-permute-start(bf16[8,9,1024]{2,1,0:T(8,128)(2,1)} %get-tuple-element.105), channel_id=1, source_target_pairs={{1,0},{2,1},{3,2},{4,3},{5,4},{6,5},{7,6},{9,8},{10,9},{11,10},{12... | collective-permute-start | bytes 442376 | tf_op jit(solution)/shard_map/ppermute | solution.py:233
  95.8 6.9 %collective-permute-start.4 = (bf16[8,9,1024]{2,1,0:T(8,128)(2,1)S(1)}, bf16[8,9,1024]{2,1,0:T(8,128)(2,1)S(1)}, u32[]{:S(2)}, u32[]{:S(2)}) collective-permute-start(bf16[8,9,1024]{2,1,0:T(8,128)(2,1)S(1)} %get-tuple-element.106), channel_id=1, source_target_pairs={{0,1},{1,2},{2,3},{3,4},{4,5},{5,6},{6,7},{8,9},{9,10},{10,11},{11... | collective-permute-start | bytes 442376 | tf_op jit(solution)/shard_map/ppermute | solution.py:233
  112.2 2.6 copy-start.17
  114.8 1.6 copy-start.15
  117.9 3.3 %copy-start.3 = (f32[8,130,512]{2,1,0:T(8,128)S(1)}, f32[8,130,512]{2,1,0:T(8,128)}, u32[]{:S(2)}) copy-start(f32[8,130,512]{2,1,0:T(8,128)} %copy-done.2) | copy-start | bytes 6389764
  128.4 8.9 %copy-start.20 = (bf16[1,512,512]{2,1,0:T(8,128)(2,1)S(1)}, bf16[1,512,512]{2,1,0:T(8,128)(2,1)}, u32[]{:S(2)}) copy-start(bf16[1,512,512]{2,1,0:T(8,128)(2,1)} %fusion.41) | copy-start | bytes 1572868
  128.4 8.9 %copy-start.21 = (bf16[1,512,512]{2,1,0:T(8,128)(2,1)S(1)}, bf16[1,512,512]{2,1,0:T(8,128)(2,1)}, u32[]{:S(2)}) copy-start(bf16[1,512,512]{2,1,0:T(8,128)(2,1)} %fusion.39) | copy-start | bytes 1572868
  128.4 8.9 %copy-start.22 = (bf16[1,512,512]{2,1,0:T(8,128)(2,1)S(1)}, bf16[1,512,512]{2,1,0:T(8,128)(2,1)}, u32[]{:S(2)}) copy-start(bf16[1,512,512]{2,1,0:T(8,128)(2,1)} %fusion.40) | copy-start | bytes 1572868
  132.5 24.2 %copy-start.7 = (f32[8,130,512]{2,1,0:T(8,128)}, f32[8,130,512]{2,1,0:T(8,128)S(1)}, u32[]{:S(2)}) copy-start(f32[8,130,512]{2,1,0:T(8,128)S(1)} %pad_add_fusion) | copy-start | bytes 6389764
  132.5 5.0 %copy-start.13 = (bf16[2048,512]{1,0:T(8,128)(2,1)S(1)}, bf16[2048,512]{1,0:T(8,128)(2,1)}, u32[]{:S(2)}) copy-start(bf16[2048,512]{1,0:T(8,128)(2,1)} %bitcast_convert_fusion.1) | copy-start | bytes 6291460
  132.5 5.0 %copy-start.19 = (bf16[512,512]{1,0:T(8,128)(2,1)S(1)}, bf16[512,512]{1,0:T(8,128)(2,1)}, u32[]{:S(2)}) copy-start(bf16[512,512]{1,0:T(8,128)(2,1)} %fusion.33) | copy-start | bytes 1572868
  132.6 26.4 %collective-permute-start.6 = (f32[8,1,512]{2,1,0:T(1,128)S(1)}, f32[8,1,512]{2,1,0:T(1,128)S(1)}, u32[]{:S(2)}, u32[]{:S(2)}) collective-permute-start(f32[8,1,512]{2,1,0:T(1,128)S(1)} %get-tuple-element.112), channel_id=1, source_target_pairs={{0,1},{1,2},{2,3},{3,4},{4,5},{5,6},{6,7},{8,9},{9,10},{10,11},{11... | collective-permute-start | bytes 49160 | tf_op jit(solution)/shard_map/ppermute | solution.py:233
  157.0 5.1 %collective-permute-start.7 = (f32[8,1,512]{2,1,0:T(1,128)S(1)}, f32[8,1,512]{2,1,0:T(1,128)S(1)}, u32[]{:S(2)}, u32[]{:S(2)}) collective-permute-start(f32[8,1,512]{2,1,0:T(1,128)S(1)} %get-tuple-element.111), channel_id=1, source_target_pairs={{1,0},{2,1},{3,2},{4,3},{5,4},{6,5},{7,6},{9,8},{10,9},{11,10},{12... | collective-permute-start | bytes 49160 | tf_op jit(solution)/shard_map/ppermute | solution.py:233
  162.2 2.1 copy-start.5
  245.0 5.8 %copy-start.6 = (f32[8,128,512]{2,1,0:T(8,128)S(1)}, f32[8,128,512]{2,1,0:T(8,128)}, u32[]{:S(2)}) copy-start(f32[8,128,512]{2,1,0:T(8,128)} %copy-done.5) | copy-start | bytes 6291460
  245.0 5.8 %copy-start.9 = (f32[8,128,512]{2,1,0:T(8,128)S(1)}, f32[8,128,512]{2,1,0:T(8,128)}, u32[]{:S(2)}) copy-start(f32[8,128,512]{2,1,0:T(8,128)} %copy-done.8) | copy-start | bytes 6291460
  245.0 5.8 %copy-start.12 = (bf16[8,128,512]{2,1,0:T(8,128)(2,1)S(1)}, bf16[8,128,512]{2,1,0:T(8,128)(2,1)}, u32[]{:S(2)}) copy-start(bf16[8,128,512]{2,1,0:T(8,128)(2,1)} %param.29) | copy-start | bytes 3145732
  263.5 5.5 %copy-start.1 = (bf16[2048,512]{1,0:T(8,128)(2,1)S(1)}, bf16[2048,512]{1,0:T(8,128)(2,1)}, u32[]{:S(2)}) copy-start(bf16[2048,512]{1,0:T(8,128)(2,1)} %param.27) | copy-start | bytes 6291460

commit v2 on v0

v2 whole, which is shorter than its diff:
```python
import functools

import jax
import jax.numpy as jnp
from jax import lax
from jax.experimental import pallas as pl
from jax.experimental.pallas import tpu as pltpu
from jax.sharding import PartitionSpec as P

HEADS = 4
HD = 128
HALF = 9
HALO = 16
PAD = 8
QB = 64
KB = QB + 2 * HALO
EPS = 1e-05
MESH = pl.DeviceIdType.MESH
F32 = jnp.float32
BF16 = jnp.bfloat16


def bit_orders(seq_size, tm_size):
    seq_bits = [("seq", b) for b in range(seq_size.bit_length() - 1)]
    tm_bits = [("tm", b) for b in range(tm_size.bit_length() - 1)]
    core, rest = tm_bits[:1], tm_bits[1:]
    first = core + seq_bits + rest
    second = core + seq_bits[::-1] + rest
    third = core + rest[:1] + seq_bits + rest[1:]
    fourth = core + rest[:1] + seq_bits[::-1] + rest[1:]
    return [first, second, third, first, second, fourth, first, second, third, first, second, fourth]


def partner_of(axis, bit):
    me = lax.axis_index(axis)
    mine = lax.rem(me // (1 << bit), 2)
    other = me + (1 - 2 * mine) * (1 << bit)
    if axis == "seq":
        return mine, (other, lax.axis_index("tm"))
    return mine, (lax.axis_index("seq"), other)


def neighbour(step, size):
    return (lax.axis_index("seq"), lax.rem(lax.axis_index("tm") + step + size, size))


class Reducer:
    def __init__(self, orders, rows, part, recv, fulls, sems):
        self.orders, self.rows = orders, rows
        self.part, self.recv, self.fulls = part, recv, fulls
        self.rs_send, self.rs_recv, self.ag_send, self.ag_recv = sems
        self.levels = len(orders[0])

    def landing(self, level):
        return self.rows - (self.rows >> level)

    def owned(self, unit, level):
        off = 0
        for i in range(level + 1):
            mine, _ = partner_of(*self.orders[unit][i])
            off = off + mine * (self.rows >> (i + 1))
        return off, self.rows >> (level + 1)

    def scatter_copy(self, unit, level):
        mine, peer = partner_of(*self.orders[unit][level])
        half = self.rows >> (level + 1)
        base = self.owned(unit, level - 1)[0] if level else 0
        off = pl.multiple_of(base + (1 - mine) * half, 16)
        return pltpu.make_async_remote_copy(
            src_ref=self.part.at[unit, pl.ds(off, half)],
            dst_ref=self.recv.at[unit, pl.ds(self.landing(level), half)],
            send_sem=self.rs_send.at[unit, level],
            recv_sem=self.rs_recv.at[unit, level],
            device_id=peer,
            device_id_type=MESH,
        )

    def full(self, unit):
        held = self.fulls[0].shape[0] // self.rows
        return self.fulls[unit // held], (unit % held) * self.rows

    def gather_copy(self, unit, level):
        _, peer = partner_of(*self.orders[unit][level])
        off, size = self.owned(unit, level)
        ref, start = self.full(unit)
        region = ref.at[pl.ds(pl.multiple_of(start + off, 16), size)]
        return pltpu.make_async_remote_copy(
            src_ref=region,
            dst_ref=region,
            send_sem=self.ag_send.at[unit, level],
            recv_sem=self.ag_recv.at[unit, level],
            device_id=peer,
            device_id_type=MESH,
        )

    def combine(self, unit, level):
        self.scatter_copy(unit, level).wait_recv()
        off, half = self.owned(unit, level)
        step = min(half, 32)

        def body(i, carry):
            here = pl.ds(pl.multiple_of(off + i * step, 16), step)
            there = pl.ds(pl.multiple_of(self.landing(level) + i * step, 16), step)
            total = self.part[unit, here, :].astype(F32) + self.recv[unit, there, :].astype(F32)
            if level == self.levels - 1:
                ref, start = self.full(unit)
                ref[pl.ds(pl.multiple_of(start + off + i * step, 16), step), :] = total.astype(BF16)
            else:
                self.part[unit, here, :] = total.astype(BF16)
            return carry

        lax.fori_loop(0, half // step, body, 0)

    def tick(self, unit, i):
        if i == 0:
            self.scatter_copy(unit, 0).start()
        elif i < self.levels:
            self.combine(unit, i - 1)
            self.scatter_copy(unit, i).start()
        elif i == self.levels:
            self.combine(unit, i - 1)
            self.gather_copy(unit, self.levels - 1).start()
        elif i < 2 * self.levels:
            level = 2 * self.levels - 1 - i
            self.gather_copy(unit, level + 1).wait_recv()
            self.gather_copy(unit, level).start()
        else:
            self.gather_copy(unit, 0).wait_recv()

    def wait_sends(self, unit):
        for level in range(self.levels):
            self.scatter_copy(unit, level).wait_send()
            self.gather_copy(unit, level).wait_send()


def enter(bits, tm_size):
    barrier = pltpu.get_barrier_semaphore()
    peers = [partner_of(axis, bit)[1] for axis, bit in bits]
    peers = peers + [neighbour(1, tm_size), neighbour(-1, tm_size)]
    for peer in peers:
        pl.semaphore_signal(barrier, inc=1, device_id=peer, device_id_type=MESH)
    pl.semaphore_wait(barrier, len(peers))


def nn(a, b):
    return lax.dot_general(a, b, (((1,), (0,)), ((), ())), preferred_element_type=F32)


def nt(a, b):
    return lax.dot_general(a, b, (((1,), (1,)), ((), ())), preferred_element_type=F32)


def tn(a, b):
    return lax.dot_general(a, b, (((0,), (0,)), ((), ())), preferred_element_type=F32)


def moments(v):
    mean = jnp.mean(v, axis=-1, keepdims=True)
    centered = v - mean
    var = jnp.mean(centered * centered, axis=-1, keepdims=True)
    return centered, lax.rsqrt(var + EPS)


def fold(v):
    rows, cols = v.shape
    return jnp.sum(v.reshape(rows // 8, 8, cols), axis=0)


def gelu_pair(v):
    c = 0.7978845608028654
    square = v * v
    inner = v * (c + (c * 0.044715) * square)
    t = jnp.tanh(inner)
    half = 0.5 * (1.0 + t)
    slope = half + (0.5 * v) * (1.0 - t * t) * (c + (3.0 * 0.044715 * c) * square)
    return v * half, slope


def loop(count, body):
    def step(i, carry):
        body(i)
        return carry

    lax.fori_loop(0, count, step, 0)


def layer_kernel(cfg, *refs):
    (
        lengths, x_hbm, params, wqkv_hbm, wout_hbm, wup_hbm, wdown_hbm, cot_hbm,
        out_hbm, din_hbm, down_hbm, up_hbm, outw_hbm, qkvw_hbm, small_out,
        x, cot, wqkv, wout, wup, wdown, halo_lo, halo_hi, nf, link,
        act_q, act_k, act_v, qs, ks, vs, prob, att, res, n2, dm, hid, du, dbr, da, outs,
        dke, dve, dmx, dnb, msg_hi, msg_lo, got_lo, got_hi, dq_hi, dq_lo, dq_got_lo, dq_got_hi,
        edge, edge_mix, sums, small_cur, small_recv,
        part, recv,
        in_sem, out_sem, halo_send, halo_recv, rs_send, rs_recv, ag_send, ag_recv, sm_send, sm_recv,
    ) = refs
    orders, rows, seqs, frames, feats, ff, tm_size = cfg
    units = len(orders)
    levels = len(orders[0])
    ext = frames + 2 * HALO
    own = PAD + HALO
    seq_length = frames * tm_size
    vids = lengths.shape[1]
    temper = HD ** (-0.5)
    lanes = [pl.ds(c * 128, 128) for c in range(feats // 128)]
    blocks = frames // QB
    pairs = seqs // 2
    per_unit = rows // feats
    base = lax.axis_index("tm") * frames
    red = Reducer(orders, rows, part, recv, (hid, du), (rs_send, rs_recv, ag_send, ag_recv))

    loads = [
        pltpu.make_async_copy(src, dst, in_sem.at[i])
        for i, (src, dst) in enumerate(
            [(x_hbm, x), (wqkv_hbm, wqkv), (wout_hbm, wout), (wup_hbm, wup), (wdown_hbm, wdown), (cot_hbm, cot)]
        )
    ]
    for load in loads:
        load.start()

    def across(src, dst, i, step):
        return pltpu.make_async_remote_copy(
            src_ref=src, dst_ref=dst, send_sem=halo_send.at[i], recv_sem=halo_recv.at[i],
            device_id=neighbour(step, tm_size), device_id_type=MESH,
        )

    enter(orders[0], tm_size)
    to_next = across(x_hbm.at[:, pl.ds(frames - HALO, HALO)], halo_lo, 0, 1)
    to_prev = across(x_hbm.at[:, pl.ds(0, HALO)], halo_hi, 1, -1)
    to_next.start()
    to_prev.start()

    sums[...] = jnp.zeros_like(sums)

    def bounds_of(s):
        total, found = 0, []
        for j in range(vids):
            total = total + lengths[s, j]
            found.append(total)
        return found

    gain_one = params[pl.ds(9, 1), :]
    gain_two = params[pl.ds(10, 1), :]
    scale = params[pl.ds(11, 1), :]

    def normed_rows(rows_in):
        centered, r = moments(rows_in.astype(F32))
        return (centered * r * gain_one).astype(BF16).astype(F32)

    loads[0].wait()

    def norm_own(s):
        nf[s, pl.ds(own, frames), :] = normed_rows(x[s])
        zero = jnp.zeros((PAD, feats), F32)
        nf[s, pl.ds(0, PAD), :] = zero
        nf[s, pl.ds(PAD + ext, PAD), :] = zero
        pos = base - own + lax.broadcasted_iota(jnp.int32, (ext + 2 * PAD, 128), 0)
        cut = pos == 0
        for bound in bounds_of(s):
            cut = cut | (pos == bound)
        link[s] = jnp.where(cut, 0.0, 1.0)

    loop(seqs, norm_own)
    to_next.wait_recv()
    to_prev.wait_recv()

    def norm_halo(s):
        nf[s, pl.ds(PAD, HALO), :] = normed_rows(halo_lo[s])
        nf[s, pl.ds(own + frames, HALO), :] = normed_rows(halo_hi[s])

    loop(seqs, norm_halo)
    loads[1].wait()

    def mix_project(t):
        for i in range(2):
            s = 2 * t + i
            before_on = link[s, pl.ds(PAD, ext), :]
            after_on = link[s, pl.ds(PAD + 1, ext), :]
            for lane in lanes:
                before = nf[s, pl.ds(PAD - 1, ext), lane] * before_on
                centre = nf[s, pl.ds(PAD, ext), lane]
                after = nf[s, pl.ds(PAD + 1, ext), lane] * after_on
                for n, dst in enumerate((act_q, act_k, act_v)):
                    k0, k1, k2 = (params[pl.ds(3 * n + c, 1), lane] for c in range(3))
                    mixed = (k0 * before + k1 * centre + k2 * after).astype(BF16)
                    if n == 0:
                        dst[s, :, lane] = mixed[HALO : HALO + frames]
                    else:
                        dst[s, :, lane] = mixed
        two = pl.ds(2 * t, 2)
        for n, (src, dst) in enumerate(((act_q, qs), (act_k, ks), (act_v, vs))):
            size = src.shape[1]
            value = nn(src[two].reshape(2 * size, feats), wqkv[n])
            dst[two] = value.astype(BF16).reshape(2, size, feats)

    loop(pairs, mix_project)

    def attend(s):
        bounds = bounds_of(s)
        row = lax.broadcasted_iota(jnp.int32, (QB, KB), 0)
        col = lax.broadcasted_iota(jnp.int32, (QB, KB), 1) - HALO
        band = (col - row <= HALF) & (col - row >= -HALF)
        for b in range(blocks):
            pos_q = row + (base + b * QB)
            pos_k = col + (base + b * QB)
            seg_q = jnp.zeros((QB, KB), jnp.int32)
            seg_k = jnp.zeros((QB, KB), jnp.int32)
            for bound in bounds:
                seg_q = seg_q + (pos_q >= bound).astype(jnp.int32)
                seg_k = seg_k + (pos_k >= bound).astype(jnp.int32)
            allowed = band & (seg_q == seg_k) & (pos_k >= 0) & (pos_k < seq_length)
            for h in range(HEADS):
                head = pl.ds(h * HD, HD)
                q = qs[s, pl.ds(b * QB, QB), head]
                k = ks[s, pl.ds(b * QB, KB), head]
                v = vs[s, pl.ds(b * QB, KB), head]
                scores = jnp.where(allowed, nt(q, k) * temper, -1e30)
                top = jnp.max(scores, axis=-1, keepdims=True)
                raised = jnp.where(allowed, jnp.exp(scores - top), 0.0)
                probs = raised / jnp.sum(raised, axis=-1, keepdims=True)
                prob[s * blocks + b, h] = probs
                att[s, pl.ds(b * QB, QB), head] = nn(probs.astype(BF16), v).astype(BF16)

    loop(seqs, attend)
    for load in loads[2:]:
        load.wait()
    tall = 2 * frames
    chunk = feats
    tokens = seqs * frames
    out_copies = [
        pltpu.make_async_copy(outs.at[pl.ds(2 * t, 2)], out_hbm.at[pl.ds(2 * t, 2)], out_sem.at[t])
        for t in range(pairs)
    ]

    def feed_forward(t):
        two = pl.ds(2 * t, 2)
        flat = lambda ref: ref[two].reshape(tall, ref.shape[2])
        residual = flat(x).astype(F32) + nn(flat(att), wout[...])
        res[two] = residual.reshape(2, frames, feats)
        centered, r = moments(residual)
        n2[two] = (centered * r * gain_two).astype(BF16).reshape(2, frames, feats)
        dm[two] = (flat(cot).astype(F32) * scale).astype(BF16).reshape(2, frames, feats)

        def part_ff(j):
            cols = pl.ds(pl.multiple_of(j * chunk, chunk), chunk)
            upper = nn(flat(n2), wup[:, cols])
            d_hidden = nt(flat(dm), wdown[cols, :])
            value, slope = gelu_pair(upper)
            tile = pl.ds(pl.multiple_of(j * tokens + t * tall, tall), tall)
            hid[tile, :] = value.astype(BF16)
            du[tile, :] = (slope * d_hidden).astype(BF16)

        loop(ff // chunk, part_ff)
        mlp_out, e = 0.0, 0.0
        for j in range(ff // chunk):
            tile = pl.ds(pl.multiple_of(j * tokens + t * tall, tall), tall)
            mlp_out = mlp_out + nn(hid[tile, :], wdown[pl.ds(j * chunk, chunk), :])
            e = e + nt(du[tile, :], wup[:, pl.ds(j * chunk, chunk)])
        residual = flat(res)
        cotan = flat(cot).astype(F32)
        outs[two] = (residual + scale * mlp_out).astype(BF16).reshape(2, frames, feats)
        sums[11] += fold(cotan * mlp_out)
        centered, r = moments(residual)
        xhat = centered * r
        sums[10] += fold(e * xhat)
        eg = e * gain_two
        d_res = cotan + r * (
            eg - jnp.mean(eg, axis=-1, keepdims=True) - xhat * jnp.mean(eg * xhat, axis=-1, keepdims=True)
        )
        res[two] = d_res.reshape(2, frames, feats)
        d_branch = d_res.astype(BF16)
        dbr[two] = d_branch.reshape(2, frames, feats)
        da[two] = nt(d_branch, wout[...]).astype(BF16).reshape(2, frames, feats)

    loop(pairs, feed_forward)
    for copy in out_copies:
        copy.start()

    whole = lambda ref: ref[...].reshape(seqs * frames, ref.shape[2])

    def place(block, value):
        part[block // per_unit, pl.ds((block % per_unit) * feats, feats), :] = value.astype(BF16)

    ff_blocks = ff // feats

    def begin(block):
        if block % per_unit == per_unit - 1:
            red.tick(block // per_unit, 0)

    for j in range(ff_blocks):
        place(j, tn(hid[pl.ds(j * tokens, tokens), :], whole(dm)))
        begin(j)
    for j in range(ff_blocks):
        place(ff_blocks + j, tn(whole(n2), du[pl.ds(j * tokens, tokens), :]))
        begin(ff_blocks + j)
    place(2 * ff_blocks, tn(whole(att), whole(dbr)))
    begin(2 * ff_blocks)

    dq = dm
    dkl, dvl = n2, att

    def attend_back(s):
        for h in range(HEADS):
            head = pl.ds(h * HD, HD)
            d_k, d_v = [], []
            for b in range(blocks):
                here = pl.ds(b * QB, QB)
                keys = pl.ds(b * QB, KB)
                q, k, v = qs[s, here, head], ks[s, keys, head], vs[s, keys, head]
                d_att = da[s, here, head]
                probs = prob[s * blocks + b, h]
                d_weights = nt(d_att, v)
                dot = jnp.sum(probs * d_weights, axis=-1, keepdims=True)
                d_scores = (probs * (d_weights - dot)).astype(BF16)
                dq[s, here, head] = (nn(d_scores, k) * temper).astype(BF16)
                d_k.append(tn(d_scores, q) * temper)
                d_v.append(tn(probs.astype(BF16), d_att))
            for dst, got in ((dke, d_k), (dve, d_v)):
                tail = None
                for b in range(blocks):
                    value = got[b]
                    first = value[: KB - QB] if tail is None else value[: KB - QB] + tail
                    dst[s, pl.ds(b * QB, KB - QB), head] = first
                    dst[s, pl.ds(b * QB + KB - QB, 2 * QB - KB), head] = value[KB - QB : QB]
                    tail = value[QB:]
                dst[s, pl.ds(blocks * QB, KB - QB), head] = tail
        for i, src in enumerate((dke, dve)):
            cols = pl.ds(i * feats, feats)
            msg_hi[s, :, cols] = src[s, pl.ds(HALO + frames - 1, HALO), :].astype(BF16)
            msg_lo[s, :, cols] = src[s, pl.ds(1, HALO), :].astype(BF16)
        dq_hi[pl.ds(s, 1), :] = dq[s, pl.ds(frames - 16, 16), :].astype(F32)[15:16]
        dq_lo[pl.ds(s, 1), :] = dq[s, pl.ds(0, 16), :].astype(F32)[0:1]

    loop(seqs, attend_back)
    exchange = [
        across(msg_hi, got_lo, 2, 1), across(msg_lo, got_hi, 3, -1),
        across(dq_hi, dq_got_lo, 4, 1), across(dq_lo, dq_got_hi, 5, -1),
    ]
    for copy in exchange:
        copy.start()
    place(2 * ff_blocks + 1, tn(whole(act_q), whole(dq)))
    begin(2 * ff_blocks + 1)
    for copy in exchange:
        copy.wait_recv()
    edge[0, pl.ds(0, seqs), :] = dq_got_lo[...]
    edge[0, pl.ds(seqs, seqs), :] = dq_got_hi[...]

    def settle(s):
        for i, (src, dst) in enumerate(((dke, dkl), (dve, dvl))):
            cols = pl.ds(i * feats, feats)
            low = pl.ds(HALO - 1, HALO)
            high = pl.ds(HALO + frames - HALO + 1, HALO)
            src[s, low, :] = src[s, low, :] + got_lo[s, :, cols].astype(F32)
            src[s, high, :] = src[s, high, :] + got_hi[s, :, cols].astype(F32)
            dst[s] = src[s, pl.ds(HALO, frames), :].astype(BF16)
            edge[i + 1, pl.ds(s, 1), :] = src[s, pl.ds(HALO - 1, 1), :]
            edge[i + 1, pl.ds(seqs + s, 1), :] = src[s, pl.ds(HALO + frames, 1), :]

    loop(seqs, settle)
    inner = lambda ref: ref[:, pl.ds(HALO, frames), :].reshape(seqs * frames, feats)
    place(2 * ff_blocks + 2, tn(inner(act_k), whole(dkl)))
    begin(2 * ff_blocks + 2)
    place(2 * ff_blocks + 3, tn(inner(act_v), whole(dvl)))
    begin(2 * ff_blocks + 3)
    for n in range(3):
        edge_mix[n] = nt(edge[n].astype(BF16), wqkv[n])

    def input_grads(t):
        two = pl.ds(2 * t, 2)
        for n, src in enumerate((dq, dkl, dvl)):
            value = nt(src[two].reshape(tall, feats), wqkv[n])
            dmx[n, :, pl.ds(PAD, frames), :] = value.reshape(2, frames, feats)
        for i in range(2):
            s = 2 * t + i
            for n in range(3):
                dmx[n, i, pl.ds(PAD - 1, 1), :] = edge_mix[n, pl.ds(s, 1), :]
                dmx[n, i, pl.ds(PAD + frames, 1), :] = edge_mix[n, pl.ds(seqs + s, 1), :]
            here = link[s, pl.ds(own, frames), :]
            after = link[s, pl.ds(own + 1, frames), :]
            for lane in lanes:
                left = nf[s, pl.ds(own - 1, frames), lane] * here
                mid = nf[s, pl.ds(own, frames), lane]
                right = nf[s, pl.ds(own + 1, frames), lane] * after
                from_left, from_mid, from_right = 0.0, 0.0, 0.0
                for n in range(3):
                    k0, k1, k2 = (params[pl.ds(3 * n + c, 1), lane] for c in range(3))
                    g = dmx[n, i, pl.ds(PAD, frames), lane]
                    sums[3 * n, :, lane] += fold(g * left)
                    sums[3 * n + 1, :, lane] += fold(g * mid)
                    sums[3 * n + 2, :, lane] += fold(g * right)
                    from_mid = from_mid + k1 * g
                    from_right = from_right + k0 * dmx[n, i, pl.ds(PAD + 1, frames), lane]
                    from_left = from_left + k2 * dmx[n, i, pl.ds(PAD - 1, frames), lane]
                dnb[:, lane] = from_mid + from_right * after + from_left * here
            e = dnb[...]
            centered, r = moments(x[s].astype(F32))
            xhat = centered * r
            sums[9] += fold(e * xhat)
            eg = e * gain_one
            res[s] = res[s] + r * (
                eg - jnp.mean(eg, axis=-1, keepdims=True) - xhat * jnp.mean(eg * xhat, axis=-1, keepdims=True)
            )

    loop(pairs, input_grads)
    din_copy = pltpu.make_async_copy(res, din_hbm, out_sem.at[pairs])
    din_copy.start()
    small_cur[0] = jnp.sum(sums[...], axis=1)

    def small_copy(level):
        _, peer = partner_of(*orders[0][level])
        return pltpu.make_async_remote_copy(
            src_ref=small_cur.at[level], dst_ref=small_recv.at[level],
            send_sem=sm_send.at[level], recv_sem=sm_recv.at[level],
            device_id=peer, device_id_type=MESH,
        )

    small_copy(0).start()
    for i in range(1, 2 * levels + 1):
        for u in range(units):
            red.tick(u, i)
        if i <= levels:
            small_copy(i - 1).wait_recv()
            total = small_cur[i - 1] + small_recv[i - 1]
            if i < levels:
                small_cur[i] = total
                small_copy(i).start()
            else:
                small_out[...] = total
    weight_copies = []
    for block in range(2 * ff_blocks + 4):
        ref, start = red.full(block // per_unit)
        src = ref.at[pl.ds(start + (block % per_unit) * feats, feats)]
        if block < ff_blocks:
            dst = down_hbm.at[pl.ds(block * feats, feats)]
        elif block < 2 * ff_blocks:
            dst = up_hbm.at[:, pl.ds((block - ff_blocks) * feats, feats)]
        elif block == 2 * ff_blocks:
            dst = outw_hbm
        else:
            dst = qkvw_hbm.at[block - 2 * ff_blocks - 1]
        weight_copies.append(pltpu.make_async_copy(src, dst, out_sem.at[pairs + 1 + block]))
    for copy in weight_copies:
        copy.start()
    to_next.wait_send()
    to_prev.wait_send()
    for copy in exchange:
        copy.wait_send()
    for level in range(levels):
        small_copy(level).wait_send()
    for u in range(units):
        red.wait_sends(u)
    for copy in out_copies + [din_copy] + weight_copies:
        copy.wait()


def shards(
    inputs, lengths, norm_gain, conv_kernel, qkv_weight, out_weight, mlp_gain, up_weight,
    down_weight, layer_scale, cotangent,
):
    seqs, frames, feats = inputs.shape
    ff = up_weight.shape[1]
    seq_size, tm_size = lax.axis_size("seq"), lax.axis_size("tm")
    rows = max(feats, 16 * seq_size * tm_size)
    units = (2 * ff + 4 * feats) // rows
    orders = bit_orders(seq_size, tm_size)[:units]
    levels = len(orders[0])
    params = jnp.concatenate(
        [
            conv_kernel.reshape(9, feats), norm_gain[None], mlp_gain[None], layer_scale[None],
            jnp.zeros((4, feats), BF16),
        ],
        axis=0,
    ).astype(F32)
    ext = frames + 2 * HALO
    blocks = frames // QB
    dma = pltpu.SemaphoreType.DMA
    any_spec = pl.BlockSpec(memory_space=pl.ANY)
    vmem_spec = pl.BlockSpec(memory_space=pltpu.VMEM)
    low = lambda *shape: pltpu.VMEM(shape, BF16)
    wide = lambda *shape: pltpu.VMEM(shape, F32)
    acts = lambda: low(seqs, frames, feats)
    acts_ext = lambda: low(seqs, ext, feats)
    scratch = [
        acts(), acts(), low(3, feats, feats), low(feats, feats), low(feats, ff), low(ff, feats),
        low(seqs, HALO, feats), low(seqs, HALO, feats),
        wide(seqs, ext + 2 * PAD, feats), wide(seqs, ext + 2 * PAD, 128),
        acts(), acts_ext(), acts_ext(), acts(), acts_ext(), acts_ext(),
        wide(seqs * blocks, HEADS, QB, KB), acts(), wide(seqs, frames, feats), acts(), acts(),
        low(seqs * frames * ff // feats, feats), low(seqs * frames * ff // feats, feats), acts(), acts(), acts(),
        wide(seqs, ext, feats), wide(seqs, ext, feats), wide(3, 2, frames + 2 * PAD, feats), wide(frames, feats),
        low(seqs, HALO, 2 * feats), low(seqs, HALO, 2 * feats), low(seqs, HALO, 2 * feats), low(seqs, HALO, 2 * feats),
        wide(seqs, feats), wide(seqs, feats), wide(seqs, feats), wide(seqs, feats),
        wide(3, 2 * seqs, feats), wide(3, 2 * seqs, feats), wide(16, 8, feats),
        wide(levels, 16, feats), wide(levels, 16, feats),
        low(units, rows, feats), low(units, rows, feats),
        dma((6,)), dma((seqs // 2 + 1 + (2 * ff + 4 * feats) // feats,)), dma((6,)), dma((6,)),
        dma((units, levels)), dma((units, levels)), dma((units, levels)), dma((units, levels)),
        dma((levels,)), dma((levels,)),
    ]
    cfg = (orders, rows, seqs, frames, feats, ff, tm_size)
    out_type = jax.ShapeDtypeStruct
    output, d_inputs, down, up, out_w, qkv_w, small = pl.pallas_call(
        functools.partial(layer_kernel, cfg),
        out_shape=(
            out_type(inputs.shape, BF16), out_type(inputs.shape, F32), out_type((ff, feats), BF16),
            out_type((feats, ff), BF16), out_type((feats, feats), BF16), out_type((3, feats, feats), BF16),
            out_type((16, feats), F32),
        ),
        in_specs=[pl.BlockSpec(memory_space=pltpu.SMEM), any_spec, vmem_spec] + [any_spec] * 5,
        out_specs=(any_spec,) * 6 + (vmem_spec,),
        scratch_shapes=scratch,
        compiler_params=pltpu.CompilerParams(
            collective_id=0, has_side_effects=True, vmem_limit_bytes=67043328
        ),
    )(lengths, inputs, params, qkv_weight, out_weight, up_weight, down_weight, cotangent)
    return (
        output, d_inputs, small[9], small[:9].reshape(3, 3, feats), qkv_w.astype(F32), out_w.astype(F32),
        small[10], up.astype(F32), down.astype(F32), small[11],
    )


def solution(mesh):
    split = P("seq", "tm", None)
    return jax.shard_map(
        shards,
        mesh=mesh,
        in_specs=(split, P("seq", None)) + (P(),) * 8 + (split,),
        out_specs=(split, split) + (P(),) * 8,
        check_vma=False,
    )
```

time: 375 us -> 184 us (0.49); the launches traced: 368 us -> 183 us
  waiting for transfers between devices: 167 us -> 0 us
  Pallas kernels: 0 us -> 164 us
  matrix products: 57.2 us -> 0 us
  blocking collectives: 43.1 us -> 0 us
  local copies, waits for them, and re-layouts: 34.2 us -> 7.91 us
  starting transfers between devices: 23.3 us -> 0 us
  other arithmetic: 28.1 us -> 10.7 us
  between operations: 14.9 us -> 0.66 us
    pallas_call x0 -> x1, Pallas kernels: none -> 164 us  [shards(): pl.pallas_call(functools.partial(layer_kernel, cfg), out_shape=(out_type(...]
    psum x1 -> x0, waiting for transfers between devices: 159 us -> none  [shards(): lax.psum((d_gain_one, d_kernel, d_qkv, d_out, d_gain_two, d_up, d_down, d...]
    dot_general x24 -> x0, matrix products: 57.2 us -> none  [the longest x6 10.4 us: project(): jnp.einsum('std,de->ste', acts, weight, preferred_element_type=jnp.float32)]
    psum x1 -> x0, blocking collectives: 43.1 us -> none  [shards(): lax.psum((d_gain_one, d_kernel, d_qkv, d_out, d_gain_two, d_up, d_down, d...]
    ppermute x8 -> x0, starting transfers between devices: 23.2 us -> none  [the longest x4 12.2 us: from_behind(): return lax.ppermute(shard, axis, pairs)]
    unnamed x53 -> x12, local copies, waits for them, and re-layouts: 19 us -> 2.31 us
    ppermute x8 -> x0, waiting for transfers between devices: 8.38 us -> none  [the longest x2 6.28 us: extended(): after = lax.ppermute(first, axis, down)]
    scatter-add x4 -> x0, local copies, waits for them, and re-layouts: 6.56 us -> none  [the longest x2 6.35 us: shards(): own_rows.at[:, :reach].add(from_low).at[:, frames - reach:].add(from_high)]
  transfers between devices with their start and end apart: 9 -> 0, of which waited for: 5 -> 0; matrix products, arithmetic and copies ran while one was open for 8% -> 0% of each run, Pallas kernels for 0% -> 0%
where the time goes in v2:
time: 184 us; the launch traced here: 183 us
  Pallas kernels  164 us (89%)
  other arithmetic  10.7 us (6%)
  local copies, waits for them, and re-layouts  7.91 us (4%)
    pallas_call x1, Pallas kernels, shards(): pl.pallas_call(functools.partial(layer_kernel, cfg), out_shape=(out_type(...  164 us
    convert_element_type x1, other arithmetic, shards(): up.astype(F32)  4.28 us

profile of v2, /device:TPU:1, one launch (start us, length us, event | category | flops | bytes accessed | tf_op | source)
XLA Modules:
  0.0 183.4 jit_solution(4896363458648916607)
XLA Ops:
  0.6 0.7 reshape.26
  1.4 0.7 broadcast_in_dim.12
  2.1 0.7 broadcast_in_dim.13
  2.7 0.7 broadcast_in_dim.14
  3.5 0.6 convert_element_type.15.refs_2_
  4.1 164.1 %shard_map.186 = (bf16[8,128,512]{2,1,0:T(8,128)(2,1)}, f32[8,128,512]{2,1,0:T(8,128)}, bf16[2048,512]{1,0:T(8,128)(2,1)}, bf16[512,2048]{1,0:T(8,128)(2,1)}, bf...) custom-call(s32[8,8]{1,0:T(8,128)} %refs_0_.1, bf16[8,128,512]{2,1,0:T(8,128)(2,1)} %refs_1_.1, ...), custom_call_target="tpu_custom_call" | custom-call | tf_op jit(solution)/shard_map/pallas_call | solution.py:603
  168.2 1.4 fusion
  169.6 1.4 reshape.27
  171.0 0.0 copy-start
  171.0 4.3 %convert_element_type.18 = f32[512,2048]{1,0:T(8,128)} convert(bf16[512,2048]{1,0:T(8,128)(2,1)} %get-tuple-element.22) | non-fusion elementwise | flops 1048576 | bytes 6291456 | tf_op jit(solution)/shard_map/convert_element_type | solution.py:619
  175.3 0.0 copy-done
  175.3 0.0 copy-start.2
  175.3 2.6 %convert_element_type.19 = f32[2048,512]{1,0:T(8,128)} convert(bf16[2048,512]{1,0:T(8,128)(2,1)S(1)} %copy-done) | non-fusion elementwise | flops 1048576 | bytes 6291456 | tf_op jit(solution)/shard_map/convert_element_type | solution.py:619
  177.9 0.0 copy-done.2
  177.9 0.0 copy-start.4
  177.9 0.0 copy-start.3
  177.9 2.1 %convert_element_type.16 = f32[3,512,512]{2,1,0:T(8,128)} convert(bf16[3,512,512]{2,1,0:T(8,128)(2,1)S(1)} %copy-done.2) | non-fusion elementwise | flops 786432 | bytes 4718592 | tf_op jit(solution)/shard_map/convert_element_type | solution.py:618
  180.0 0.0 copy-start.1
  180.0 0.0 copy-done.4
  180.0 1.1 convert_element_type.17
  181.1 0.0 copy-done.3
  181.1 1.0 copy.23
  182.1 0.0 copy-done.1
  182.1 1.3 copy.24
  (2 shorter events, 0.0 us)
Async XLA Ops:
  171.0 4.3 %copy-start = (bf16[2048,512]{1,0:T(8,128)(2,1)S(1)}, bf16[2048,512]{1,0:T(8,128)(2,1)}, u32[]{:S(2)}) copy-start(bf16[2048,512]{1,0:T(8,128)(2,1)} %get-tuple-element.23) | copy-start | bytes 6291460
  175.3 2.6 %copy-start.2 = (bf16[3,512,512]{2,1,0:T(8,128)(2,1)S(1)}, bf16[3,512,512]{2,1,0:T(8,128)(2,1)}, u32[]{:S(2)}) copy-start(bf16[3,512,512]{2,1,0:T(8,128)(2,1)} %get-tuple-element.20) | copy-start | bytes 4718596
  177.9 2.1 %copy-start.4 = (bf16[512,512]{1,0:T(8,128)(2,1)S(1)}, bf16[512,512]{1,0:T(8,128)(2,1)}, u32[]{:S(2)}) copy-start(bf16[512,512]{1,0:T(8,128)(2,1)} %get-tuple-element.21) | copy-start | bytes 1572868
  177.9 3.2 %copy-start.3 = (bf16[8,128,512]{2,1,0:T(8,128)(2,1)S(1)}, bf16[8,128,512]{2,1,0:T(8,128)(2,1)}, u32[]{:S(2)}) copy-start(bf16[8,128,512]{2,1,0:T(8,128)(2,1)} %get-tuple-element.37) | copy-start | bytes 3145732
  180.0 2.1 %copy-start.1 = (f32[8,128,512]{2,1,0:T(8,128)S(1)}, f32[8,128,512]{2,1,0:T(8,128)}, u32[]{:S(2)}) copy-start(f32[8,128,512]{2,1,0:T(8,128)} %get-tuple-element.38) | copy-start | bytes 6291460

commit v3 on v2

--- a/solution.py
+++ b/solution.py
@@ -12,8 +12,6 @@
 HALF = 9
 HALO = 16
 PAD = 8
-QB = 64
-KB = QB + 2 * HALO
 EPS = 1e-05
 MESH = pl.DeviceIdType.MESH
 F32 = jnp.float32
@@ -38,10 +36,6 @@
     if axis == "seq":
         return mine, (other, lax.axis_index("tm"))
     return mine, (lax.axis_index("seq"), other)
-
-
-def neighbour(step, size):
-    return (lax.axis_index("seq"), lax.rem(lax.axis_index("tm") + step + size, size))
 
 
 class Reducer:
@@ -77,7 +71,11 @@
 
     def full(self, unit):
         held = self.fulls[0].shape[0] // self.rows
-        return self.fulls[unit // held], (unit % held) * self.rows
+        index = unit % held
+        if unit < held and self.rows == self.fulls[0].shape[1]:
+            half = held // 2
+            index = 2 * (unit % half) + unit // half
+        return self.fulls[unit // held], index * self.rows
 
     def gather_copy(self, unit, level):
         _, peer = partner_of(*self.orders[unit][level])
@@ -133,13 +131,101 @@
             self.gather_copy(unit, level).wait_send()
 
 
+def beside(tm_size):
+    at = lax.axis_index("tm")
+    seq = lax.axis_index("seq")
+    return [(at < tm_size - 1, (seq, at + 1)), (at > 0, (seq, at - 1))]
+
+
+def plan_steps(orders, rows, feats, pieces, small_from):
+    levels = len(orders[0])
+    rate = {"core": 185e3, "link": 85e3}
+    free, reached, arrival = {}, {}, {}
+    small_bytes = 16 * feats * 4
+
+    def send(unit, now, level, size):
+        axis, bit = (orders[unit] if unit >= 0 else orders[0])[level]
+        if (axis, bit) == ("tm", 0):
+            uses, lag = [("core", size / rate["core"])], 1.0
+        elif axis == "seq":
+            uses, lag = [((axis, bit), 2 * size / rate["link"])], 1.8
+        elif bit == 1:
+            uses, lag = [((axis, 1), 2 * size / rate["link"])], 1.8
+        else:
+            uses = [((axis, 1), 2 * size / rate["link"]), ((axis, bit), 4 * size / rate["link"])]
+            lag = 2.6
+        start = max([now] + [free.get(name, 0.0) for name, _ in uses])
+        for name, busy in uses:
+            free[name] = start + busy
+        return start + max(busy for _, busy in uses) + lag
+
+    def bytes_of(level):
+        return (rows >> (level + 1)) * feats * 2
+
+    def step(unit, now):
+        i = reached[unit]
+        reached[unit] = i + 1
+        if unit < 0:
+            if i < levels:
+                arrival[unit] = send(unit, now, i, small_bytes)
+            return 0.05 if i <= levels else 0.0
+        cost = 0.02 + (bytes_of(i - 1) / 2.4e6 if 0 < i <= levels else 0.0)
+        if i < levels:
+            arrival[unit] = send(unit, now + cost, i, bytes_of(i))
+        elif i < 2 * levels:
+            level = 2 * levels - 1 - i
+            arrival[unit] = send(unit, now + cost, level, bytes_of(level))
+        return cost
+
+    def last(unit):
+        return levels if unit < 0 else 2 * levels
+
+    now, placed = 0.0, {}
+    for slot, us, begins in pieces:
+        now += us
+        todo = []
+        if begins is not None:
+            reached[begins] = 0
+            now += step(begins, now)
+        while True:
+            ready = [u for u in reached if reached[u] <= last(u) and arrival[u] <= now]
+            if not ready:
+                break
+            unit = min(ready, key=lambda u: (arrival[u], u))
+            todo.append((unit, reached[unit]))
+            now += step(unit, now)
+        placed[slot] = todo
+    work_end = now
+    if small_from:
+        reached[-1] = 0
+        now += step(-1, now)
+    tail = []
+    while True:
+        left = [u for u in reached if reached[u] <= last(u)]
+        if not left:
+            break
+        unit = min(left, key=lambda u: (arrival[u], u))
+        now = max(now, arrival[unit])
+        tail.append((unit, reached[unit]))
+        now += step(unit, now)
+    return placed, tail, (work_end, now)
+
+
+def greet(bits, tm_size):
+    barrier = pltpu.get_barrier_semaphore()
+    for axis, bit in bits:
+        pl.semaphore_signal(barrier, inc=1, device_id=partner_of(axis, bit)[1], device_id_type=MESH)
+    for there, peer in beside(tm_size):
+        @pl.when(there)
+        def _():
+            pl.semaphore_signal(barrier, inc=1, device_id=peer, device_id_type=MESH)
+
+
 def enter(bits, tm_size):
-    barrier = pltpu.get_barrier_semaphore()
-    peers = [partner_of(axis, bit)[1] for axis, bit in bits]
-    peers = peers + [neighbour(1, tm_size), neighbour(-1, tm_size)]
-    for peer in peers:
-        pl.semaphore_signal(barrier, inc=1, device_id=peer, device_id_type=MESH)
-    pl.semaphore_wait(barrier, len(peers))
+    count = len(bits)
+    for there, _ in beside(tm_size):
+        count = count + there.astype(jnp.int32)
+    pl.semaphore_wait(pltpu.get_barrier_semaphore(), count)
 
 
 def nn(a, b):
@@ -186,9 +272,9 @@
 
 def layer_kernel(cfg, *refs):
     (
-        lengths, x_hbm, params, wqkv_hbm, wout_hbm, wup_hbm, wdown_hbm, cot_hbm,
+        lengths, x_hbm, norm_gain, conv_kernel, mlp_gain, layer_scale, wqkv_hbm, wout_hbm, wup_hbm, wdown_hbm, cot_hbm,
         out_hbm, din_hbm, down_hbm, up_hbm, outw_hbm, qkvw_hbm, small_out,
-        x, cot, wqkv, wout, wup, wdown, halo_lo, halo_hi, nf, link,
+        params, x, cot, wqkv, wout, wup, wdown, halo_lo, halo_hi, nf, link,
         act_q, act_k, act_v, qs, ks, vs, prob, att, res, n2, dm, hid, du, dbr, da, outs,
         dke, dve, dmx, dnb, msg_hi, msg_lo, got_lo, got_hi, dq_hi, dq_lo, dq_got_lo, dq_got_hi,
         edge, edge_mix, sums, small_cur, small_recv,
@@ -204,7 +290,6 @@
     vids = lengths.shape[1]
     temper = HD ** (-0.5)
     lanes = [pl.ds(c * 128, 128) for c in range(feats // 128)]
-    blocks = frames // QB
     pairs = seqs // 2
     per_unit = rows // feats
     base = lax.axis_index("tm") * frames
@@ -219,18 +304,41 @@
     for load in loads:
         load.start()
 
-    def across(src, dst, i, step):
-        return pltpu.make_async_remote_copy(
-            src_ref=src, dst_ref=dst, send_sem=halo_send.at[i], recv_sem=halo_recv.at[i],
-            device_id=neighbour(step, tm_size), device_id_type=MESH,
-        )
-
-    enter(orders[0], tm_size)
-    to_next = across(x_hbm.at[:, pl.ds(frames - HALO, HALO)], halo_lo, 0, 1)
-    to_prev = across(x_hbm.at[:, pl.ds(0, HALO)], halo_hi, 1, -1)
-    to_next.start()
-    to_prev.start()
-
+    class Across:
+        def __init__(self, src, dst, i, side):
+            (self.sends, peer), (self.gets, _) = beside(tm_size)[side], beside(tm_size)[1 - side]
+            self.copy = pltpu.make_async_remote_copy(
+                src_ref=src, dst_ref=dst, send_sem=halo_send.at[i], recv_sem=halo_recv.at[i],
+                device_id=peer, device_id_type=MESH,
+            )
+
+        def start(self):
+            pl.when(self.sends)(lambda: self.copy.start())
+
+        def wait_recv(self):
+            pl.when(self.gets)(lambda: self.copy.wait_recv())
+
+        def wait_send(self):
+            pl.when(self.sends)(lambda: self.copy.wait_send())
+
+    greet(orders[0], tm_size)
+    for n in range(3):
+        params[pl.ds(3 * n, 3), :] = conv_kernel[n].astype(F32)
+    for i, src in enumerate((norm_gain, mlp_gain, layer_scale)):
+        params[pl.ds(9 + i, 1), :] = src[...].astype(F32).reshape(1, feats)
+
+    def clear_missing(side, refs_in):
+        there = beside(tm_size)[side][0]
+
+        @pl.when(jnp.logical_not(there))
+        def _():
+            for ref in refs_in:
+                ref[...] = jnp.zeros_like(ref)
+
+    clear_missing(1, (halo_lo, got_lo, dq_got_lo))
+    clear_missing(0, (halo_hi, got_hi, dq_got_hi))
+    to_next = Across(x_hbm.at[:, pl.ds(frames - HALO, HALO)], halo_lo, 0, 0)
+    to_prev = Across(x_hbm.at[:, pl.ds(0, HALO)], halo_hi, 1, 1)
     sums[...] = jnp.zeros_like(sums)
 
     def bounds_of(s):
@@ -262,6 +370,9 @@
         link[s] = jnp.where(cut, 0.0, 1.0)
 
     loop(seqs, norm_own)
+    enter(orders[0], tm_size)
+    to_next.start()
+    to_prev.start()
     to_next.wait_recv()
     to_prev.wait_recv()
 
@@ -297,30 +408,26 @@
     loop(pairs, mix_project)
 
     def attend(s):
-        bounds = bounds_of(s)
-        row = lax.broadcasted_iota(jnp.int32, (QB, KB), 0)
-        col = lax.broadcasted_iota(jnp.int32, (QB, KB), 1) - HALO
-        band = (col - row <= HALF) & (col - row >= -HALF)
-        for b in range(blocks):
-            pos_q = row + (base + b * QB)
-            pos_k = col + (base + b * QB)
-            seg_q = jnp.zeros((QB, KB), jnp.int32)
-            seg_k = jnp.zeros((QB, KB), jnp.int32)
-            for bound in bounds:
-                seg_q = seg_q + (pos_q >= bound).astype(jnp.int32)
-                seg_k = seg_k + (pos_k >= bound).astype(jnp.int32)
-            allowed = band & (seg_q == seg_k) & (pos_k >= 0) & (pos_k < seq_length)
-            for h in range(HEADS):
-                head = pl.ds(h * HD, HD)
-                q = qs[s, pl.ds(b * QB, QB), head]
-                k = ks[s, pl.ds(b * QB, KB), head]
-                v = vs[s, pl.ds(b * QB, KB), head]
-                scores = jnp.where(allowed, nt(q, k) * temper, -1e30)
-                top = jnp.max(scores, axis=-1, keepdims=True)
-                raised = jnp.where(allowed, jnp.exp(scores - top), 0.0)
-                probs = raised / jnp.sum(raised, axis=-1, keepdims=True)
-                prob[s * blocks + b, h] = probs
-                att[s, pl.ds(b * QB, QB), head] = nn(probs.astype(BF16), v).astype(BF16)
+        key = lax.broadcasted_iota(jnp.int32, (ext, frames), 0) - HALO
+        query = lax.broadcasted_iota(jnp.int32, (ext, frames), 1)
+        band = (key - query <= HALF) & (key - query >= -HALF)
+        pos_k = key + base
+        pos_q = lax.broadcasted_iota(jnp.int32, (8, frames), 1) + base
+        seg_k = jnp.zeros((ext, frames), jnp.int32)
+        seg_q = jnp.zeros((8, frames), jnp.int32)
+        for bound in bounds_of(s):
+            seg_k = seg_k + (pos_k >= bound).astype(jnp.int32)
+            seg_q = seg_q + (pos_q >= bound).astype(jnp.int32)
+        allowed = band & (seg_k == seg_q[0:1]) & (pos_k >= 0) & (pos_k < seq_length)
+        bias = jnp.where(allowed, 0.0, -1e30)
+        for h in range(HEADS):
+            head = pl.ds(h * HD, HD)
+            scores = nt(ks[s, :, head], qs[s, :, head]) * temper + bias
+            top = jnp.max(scores, axis=0, keepdims=True)
+            raised = jnp.exp(scores - top)
+            probs = raised * (1.0 / jnp.sum(raised, axis=0, keepdims=True))
+            prob[s, h] = probs
+            att[s, :, head] = tn(probs.astype(BF16), vs[s, :, head]).astype(BF16)
 
     loop(seqs, attend)
     for load in loads[2:]:
@@ -333,33 +440,118 @@
         for t in range(pairs)
     ]
 
-    def feed_forward(t):
+    def flat(ref, t):
+        return ref[pl.ds(2 * t, 2)].reshape(tall, ref.shape[2])
+
+    def back(value):
+        return value.reshape(2, frames, feats)
+
+    def residual_norm(t):
         two = pl.ds(2 * t, 2)
-        flat = lambda ref: ref[two].reshape(tall, ref.shape[2])
-        residual = flat(x).astype(F32) + nn(flat(att), wout[...])
-        res[two] = residual.reshape(2, frames, feats)
+        residual = flat(x, t).astype(F32) + nn(flat(att, t), wout[...])
+        res[two] = back(residual)
         centered, r = moments(residual)
-        n2[two] = (centered * r * gain_two).astype(BF16).reshape(2, frames, feats)
-        dm[two] = (flat(cot).astype(F32) * scale).astype(BF16).reshape(2, frames, feats)
-
-        def part_ff(j):
-            cols = pl.ds(pl.multiple_of(j * chunk, chunk), chunk)
-            upper = nn(flat(n2), wup[:, cols])
-            d_hidden = nt(flat(dm), wdown[cols, :])
+        n2[two] = back((centered * r * gain_two).astype(BF16))
+        dm[two] = back((flat(cot, t).astype(F32) * scale).astype(BF16))
+
+    loop(pairs, residual_norm)
+    whole = lambda ref: ref[...].reshape(seqs * frames, ref.shape[2])
+    early = pl.ds(0, frames)
+
+    def place(block, value):
+        part[block // per_unit, pl.ds((block % per_unit) * feats, feats), :] = value.astype(BF16)
+
+    ff_blocks = ff // feats
+    weight_copies = []
+
+    def block_copy(block):
+        ref, start = red.full(block // per_unit)
+        src = ref.at[pl.ds(start + (block % per_unit) * feats, feats)]
+        if block < ff_blocks:
+            dst = down_hbm.at[pl.ds(block * feats, feats)]
+        elif block < 2 * ff_blocks:
+            dst = up_hbm.at[:, pl.ds((block - ff_blocks) * feats, feats)]
+        elif block == 2 * ff_blocks:
+            dst = outw_hbm
+        else:
+            dst = qkvw_hbm.at[block - 2 * ff_blocks - 1]
+        return pltpu.make_async_copy(src, dst, out_sem.at[pairs + 1 + block])
+
+    def unit_begun(block):
+        return block // per_unit if block % per_unit == per_unit - 1 else None
+
+    pieces = []
+    for j in range(ff_blocks):
+        pieces += [(("f", j, t), 0.95, None) for t in range(pairs)]
+        pieces += [(("d", j), 0.73, unit_begun(j)), (("u", j), 0.73, unit_begun(ff_blocks + j))]
+    pieces += [(("x", t), 0.8, None) for t in range(pairs)]
+    pieces += [("o", 0.73, unit_begun(2 * ff_blocks))]
+    pieces += [(("b", s), 1.0, None) for s in range(seqs)]
+    pieces += [
+        ("q", 0.73, unit_begun(2 * ff_blocks + 1)), ("w", 2.5, None),
+        ("k", 0.73, unit_begun(2 * ff_blocks + 2)), ("v", 0.73, unit_begun(2 * ff_blocks + 3)),
+    ]
+    pieces += [(("i", s), 0.8, None) for s in range(seqs)]
+    placed, tail, _ = plan_steps(orders, rows, feats, pieces, True)
+
+    def advance(u, i):
+        red.tick(u, i)
+        if i == 2 * levels:
+            for block in range(u * per_unit, (u + 1) * per_unit):
+                weight_copies.append(block_copy(block))
+                weight_copies[-1].start()
+
+    def slot(name, index=None, count=0):
+        if index is None:
+            for u, i in placed[name]:
+                advance(u, i)
+            return
+        for k in range(count):
+            if placed[name + (k,)]:
+                pl.when(index == k)(lambda k=k: [advance(u, i) for u, i in placed[name + (k,)]] and None)
+
+    def begin(block):
+        u = unit_begun(block)
+        if u is not None:
+            advance(u, 0)
+
+    mlp_sum, e_sum = dke, dve
+
+    def add_back(ref, t, first, value):
+        two = pl.ds(2 * t, 2)
+        ref[two, early, :] = back(value) if first else ref[two, early, :] + back(value)
+
+    for j in range(ff_blocks):
+        cols = pl.ds(j * chunk, chunk)
+
+        def hidden_chunk(t, j=j, cols=cols):
+            upper = nn(flat(n2, t), wup[:, cols])
+            d_hidden = nt(flat(dm, t), wdown[cols, :])
             value, slope = gelu_pair(upper)
+            value, slope = value.astype(BF16), (slope * d_hidden).astype(BF16)
             tile = pl.ds(pl.multiple_of(j * tokens + t * tall, tall), tall)
-            hid[tile, :] = value.astype(BF16)
-            du[tile, :] = (slope * d_hidden).astype(BF16)
-
-        loop(ff // chunk, part_ff)
-        mlp_out, e = 0.0, 0.0
-        for j in range(ff // chunk):
-            tile = pl.ds(pl.multiple_of(j * tokens + t * tall, tall), tall)
-            mlp_out = mlp_out + nn(hid[tile, :], wdown[pl.ds(j * chunk, chunk), :])
-            e = e + nt(du[tile, :], wup[:, pl.ds(j * chunk, chunk)])
-        residual = flat(res)
-        cotan = flat(cot).astype(F32)
-        outs[two] = (residual + scale * mlp_out).astype(BF16).reshape(2, frames, feats)
+            hid[tile, :] = value
+            du[tile, :] = slope
+            add_back(mlp_sum, t, j == 0, nn(value, wdown[cols, :]))
+            add_back(e_sum, t, j == 0, nt(slope, wup[:, cols]))
+            slot(("f", j), t, pairs)
+
+        loop(pairs, hidden_chunk)
+        rows_j = pl.ds(j * tokens, tokens)
+        place(j, tn(hid[rows_j, :], whole(dm)))
+        begin(j)
+        slot(("d", j))
+        place(ff_blocks + j, tn(whole(n2), du[rows_j, :]))
+        begin(ff_blocks + j)
+        slot(("u", j))
+
+    def feed_back(t):
+        two = pl.ds(2 * t, 2)
+        mlp_out = mlp_sum[two, early, :].reshape(tall, feats)
+        e = e_sum[two, early, :].reshape(tall, feats)
+        residual = flat(res, t)
+        cotan = flat(cot, t).astype(F32)
+        outs[two] = back((residual + scale * mlp_out).astype(BF16))
         sums[11] += fold(cotan * mlp_out)
         centered, r = moments(residual)
         xhat = centered * r
@@ -368,34 +560,19 @@
         d_res = cotan + r * (
             eg - jnp.mean(eg, axis=-1, keepdims=True) - xhat * jnp.mean(eg * xhat, axis=-1, keepdims=True)
         )
-        res[two] = d_res.reshape(2, frames, feats)
+        res[two] = back(d_res)
         d_branch = d_res.astype(BF16)
-        dbr[two] = d_branch.reshape(2, frames, feats)
-        da[two] = nt(d_branch, wout[...]).astype(BF16).reshape(2, frames, feats)
-
-    loop(pairs, feed_forward)
+        dbr[two] = back(d_branch)
+        da[two] = back(nt(d_branch, wout[...]).astype(BF16))
+        slot(("x",), t, pairs)
+
+    loop(pairs, feed_back)
     for copy in out_copies:
         copy.start()
 
-    whole = lambda ref: ref[...].reshape(seqs * frames, ref.shape[2])
-
-    def place(block, value):
-        part[block // per_unit, pl.ds((block % per_unit) * feats, feats), :] = value.astype(BF16)
-
-    ff_blocks = ff // feats
-
-    def begin(block):
-        if block % per_unit == per_unit - 1:
-            red.tick(block // per_unit, 0)
-
-    for j in range(ff_blocks):
-        place(j, tn(hid[pl.ds(j * tokens, tokens), :], whole(dm)))
-        begin(j)
-    for j in range(ff_blocks):
-        place(ff_blocks + j, tn(whole(n2), du[pl.ds(j * tokens, tokens), :]))
-        begin(ff_blocks + j)
     place(2 * ff_blocks, tn(whole(att), whole(dbr)))
     begin(2 * ff_blocks)
+    slot("o")
 
     dq = dm
     dkl, dvl = n2, att
@@ -403,44 +580,31 @@
     def attend_back(s):
         for h in range(HEADS):
             head = pl.ds(h * HD, HD)
-            d_k, d_v = [], []
-            for b in range(blocks):
-                here = pl.ds(b * QB, QB)
-                keys = pl.ds(b * QB, KB)
-                q, k, v = qs[s, here, head], ks[s, keys, head], vs[s, keys, head]
-                d_att = da[s, here, head]
-                probs = prob[s * blocks + b, h]
-                d_weights = nt(d_att, v)
-                dot = jnp.sum(probs * d_weights, axis=-1, keepdims=True)
-                d_scores = (probs * (d_weights - dot)).astype(BF16)
-                dq[s, here, head] = (nn(d_scores, k) * temper).astype(BF16)
-                d_k.append(tn(d_scores, q) * temper)
-                d_v.append(tn(probs.astype(BF16), d_att))
-            for dst, got in ((dke, d_k), (dve, d_v)):
-                tail = None
-                for b in range(blocks):
-                    value = got[b]
-                    first = value[: KB - QB] if tail is None else value[: KB - QB] + tail
-                    dst[s, pl.ds(b * QB, KB - QB), head] = first
-                    dst[s, pl.ds(b * QB + KB - QB, 2 * QB - KB), head] = value[KB - QB : QB]
-                    tail = value[QB:]
-                dst[s, pl.ds(blocks * QB, KB - QB), head] = tail
+            q, d_att, probs = qs[s, :, head], da[s, :, head], prob[s, h]
+            d_weights = nt(vs[s, :, head], d_att)
+            dot = jnp.sum(probs * d_weights, axis=0, keepdims=True)
+            d_scores = (probs * (d_weights - dot)).astype(BF16)
+            dq[s, :, head] = (tn(d_scores, ks[s, :, head]) * temper).astype(BF16)
+            dke[s, :, head] = nn(d_scores, q) * temper
+            dve[s, :, head] = nn(probs.astype(BF16), d_att)
         for i, src in enumerate((dke, dve)):
             cols = pl.ds(i * feats, feats)
             msg_hi[s, :, cols] = src[s, pl.ds(HALO + frames - 1, HALO), :].astype(BF16)
             msg_lo[s, :, cols] = src[s, pl.ds(1, HALO), :].astype(BF16)
         dq_hi[pl.ds(s, 1), :] = dq[s, pl.ds(frames - 16, 16), :].astype(F32)[15:16]
         dq_lo[pl.ds(s, 1), :] = dq[s, pl.ds(0, 16), :].astype(F32)[0:1]
+        slot(("b",), s, seqs)
 
     loop(seqs, attend_back)
     exchange = [
-        across(msg_hi, got_lo, 2, 1), across(msg_lo, got_hi, 3, -1),
-        across(dq_hi, dq_got_lo, 4, 1), across(dq_lo, dq_got_hi, 5, -1),
+        Across(msg_hi, got_lo, 2, 0), Across(msg_lo, got_hi, 3, 1),
+        Across(dq_hi, dq_got_lo, 4, 0), Across(dq_lo, dq_got_hi, 5, 1),
     ]
     for copy in exchange:
         copy.start()
     place(2 * ff_blocks + 1, tn(whole(act_q), whole(dq)))
     begin(2 * ff_blocks + 1)
+    slot("q")
     for copy in exchange:
         copy.wait_recv()
     edge[0, pl.ds(0, seqs), :] = dq_got_lo[...]
@@ -458,11 +622,14 @@
             edge[i + 1, pl.ds(seqs + s, 1), :] = src[s, pl.ds(HALO + frames, 1), :]
 
     loop(seqs, settle)
+    slot("w")
     inner = lambda ref: ref[:, pl.ds(HALO, frames), :].reshape(seqs * frames, feats)
     place(2 * ff_blocks + 2, tn(inner(act_k), whole(dkl)))
     begin(2 * ff_blocks + 2)
+    slot("k")
     place(2 * ff_blocks + 3, tn(inner(act_v), whole(dvl)))
     begin(2 * ff_blocks + 3)
+    slot("v")
     for n in range(3):
         edge_mix[n] = nt(edge[n].astype(BF16), wqkv[n])
 
@@ -501,6 +668,9 @@
             res[s] = res[s] + r * (
                 eg - jnp.mean(eg, axis=-1, keepdims=True) - xhat * jnp.mean(eg * xhat, axis=-1, keepdims=True)
             )
+            for k in range(i, seqs, 2):
+                if placed[("i", k)]:
+                    pl.when(s == k)(lambda k=k: [advance(u, step) for u, step in placed[("i", k)]] and None)
 
     loop(pairs, input_grads)
     din_copy = pltpu.make_async_copy(res, din_hbm, out_sem.at[pairs])
@@ -516,32 +686,17 @@
         )
 
     small_copy(0).start()
-    for i in range(1, 2 * levels + 1):
-        for u in range(units):
-            red.tick(u, i)
-        if i <= levels:
-            small_copy(i - 1).wait_recv()
-            total = small_cur[i - 1] + small_recv[i - 1]
-            if i < levels:
-                small_cur[i] = total
-                small_copy(i).start()
-            else:
-                small_out[...] = total
-    weight_copies = []
-    for block in range(2 * ff_blocks + 4):
-        ref, start = red.full(block // per_unit)
-        src = ref.at[pl.ds(start + (block % per_unit) * feats, feats)]
-        if block < ff_blocks:
-            dst = down_hbm.at[pl.ds(block * feats, feats)]
-        elif block < 2 * ff_blocks:
-            dst = up_hbm.at[:, pl.ds((block - ff_blocks) * feats, feats)]
-        elif block == 2 * ff_blocks:
-            dst = outw_hbm
+    for u, small_at in tail:
+        if u >= 0:
+            advance(u, small_at)
+            continue
+        small_copy(small_at - 1).wait_recv()
+        total = small_cur[small_at - 1] + small_recv[small_at - 1]
+        if small_at < levels:
+            small_cur[small_at] = total
+            small_copy(small_at).start()
         else:
-            dst = qkvw_hbm.at[block - 2 * ff_blocks - 1]
-        weight_copies.append(pltpu.make_async_copy(src, dst, out_sem.at[pairs + 1 + block]))
-    for copy in weight_copies:
-        copy.start()
+            small_out[...] = total
     to_next.wait_send()
     to_prev.wait_send()
     for copy in exchange:
@@ -552,6 +707,43 @@
         red.wait_sends(u)
     for copy in out_copies + [din_copy] + weight_copies:
         copy.wait()
+
+
+def widen_kernel(
+    down, up, out_w, qkv_w, small, d_gain_one, d_kernel, d_qkv, d_out, d_gain_two, d_up, d_down, d_scale,
+    narrow, broad, in_sem, out_sem,
+):
+    count, feats, _ = narrow.shape
+    ff_blocks = (count - 4) // 2
+    moves = []
+    for j in range(ff_blocks):
+        here = pl.ds(j * feats, feats)
+        moves.append((down.at[here], d_down.at[here]))
+    for j in range(ff_blocks):
+        here = pl.ds(j * feats, feats)
+        moves.append((up.at[:, here], d_up.at[:, here]))
+    moves.append((out_w, d_out))
+    for n in range(3):
+        moves.append((qkv_w.at[n], d_qkv.at[n]))
+    loads = [pltpu.make_async_copy(m[0], narrow.at[i], in_sem.at[i]) for i, m in enumerate(moves)]
+    stores = [pltpu.make_async_copy(broad.at[i], m[1], out_sem.at[i]) for i, m in enumerate(moves)]
+    for load in loads:
+        load.start()
+    for n in range(3):
+        d_kernel[n] = small[pl.ds(3 * n, 3), :]
+    for i, dst in enumerate((d_gain_one, d_gain_two, d_scale)):
+        dst[...] = small[pl.ds(9 + i, 1), :].reshape(feats)
+    for i in range(count):
+        loads[i].wait()
+
+        def widen(r):
+            here = pl.ds(pl.multiple_of(r * 32, 32), 32)
+            broad[i, here, :] = narrow[i, here, :].astype(F32)
+
+        loop(feats // 32, widen)
+        stores[i].start()
+    for store in stores:
+        store.wait()
 
 
 def shards(
@@ -565,15 +757,7 @@
     units = (2 * ff + 4 * feats) // rows
     orders = bit_orders(seq_size, tm_size)[:units]
     levels = len(orders[0])
-    params = jnp.concatenate(
-        [
-            conv_kernel.reshape(9, feats), norm_gain[None], mlp_gain[None], layer_scale[None],
-            jnp.zeros((4, feats), BF16),
-        ],
-        axis=0,
-    ).astype(F32)
     ext = frames + 2 * HALO
-    blocks = frames // QB
     dma = pltpu.SemaphoreType.DMA
     any_spec = pl.BlockSpec(memory_space=pl.ANY)
     vmem_spec = pl.BlockSpec(memory_space=pltpu.VMEM)
@@ -582,11 +766,11 @@
     acts = lambda: low(seqs, frames, feats)
     acts_ext = lambda: low(seqs, ext, feats)
     scratch = [
-        acts(), acts(), low(3, feats, feats), low(feats, feats), low(feats, ff), low(ff, feats),
+        wide(16, feats), acts(), acts(), low(3, feats, feats), low(feats, feats), low(feats, ff), low(ff, feats),
         low(seqs, HALO, feats), low(seqs, HALO, feats),
         wide(seqs, ext + 2 * PAD, feats), wide(seqs, ext + 2 * PAD, 128),
         acts(), acts_ext(), acts_ext(), acts(), acts_ext(), acts_ext(),
-        wide(seqs * blocks, HEADS, QB, KB), acts(), wide(seqs, frames, feats), acts(), acts(),
+        wide(seqs, HEADS, ext, frames), acts(), wide(seqs, frames, feats), acts(), acts(),
         low(seqs * frames * ff // feats, feats), low(seqs * frames * ff // feats, feats), acts(), acts(), acts(),
         wide(seqs, ext, feats), wide(seqs, ext, feats), wide(3, 2, frames + 2 * PAD, feats), wide(frames, feats),
         low(seqs, HALO, 2 * feats), low(seqs, HALO, 2 * feats), low(seqs, HALO, 2 * feats), low(seqs, HALO, 2 * feats),
@@ -607,17 +791,29 @@
             out_type((feats, ff), BF16), out_type((feats, feats), BF16), out_type((3, feats, feats), BF16),
             out_type((16, feats), F32),
         ),
-        in_specs=[pl.BlockSpec(memory_space=pltpu.SMEM), any_spec, vmem_spec] + [any_spec] * 5,
+        in_specs=[pl.BlockSpec(memory_space=pltpu.SMEM), any_spec] + [vmem_spec] * 4 + [any_spec] * 5,
         out_specs=(any_spec,) * 6 + (vmem_spec,),
         scratch_shapes=scratch,
         compiler_params=pltpu.CompilerParams(
             collective_id=0, has_side_effects=True, vmem_limit_bytes=67043328
         ),
-    )(lengths, inputs, params, qkv_weight, out_weight, up_weight, down_weight, cotangent)
-    return (
-        output, d_inputs, small[9], small[:9].reshape(3, 3, feats), qkv_w.astype(F32), out_w.astype(F32),
-        small[10], up.astype(F32), down.astype(F32), small[11],
-    )
+    )(lengths, inputs, norm_gain, conv_kernel, mlp_gain, layer_scale, qkv_weight, out_weight, up_weight, down_weight, cotangent)
+    count = (2 * ff + 4 * feats) // feats
+    d_gain_one, d_kernel, d_qkv, d_out, d_gain_two, d_up, d_down, d_scale = pl.pallas_call(
+        widen_kernel,
+        out_shape=(
+            out_type((feats,), F32), out_type((3, 3, feats), F32), out_type((3, feats, feats), F32),
+            out_type((feats, feats), F32), out_type((feats,), F32), out_type((feats, ff), F32),
+            out_type((ff, feats), F32), out_type((feats,), F32),
+        ),
+        in_specs=[pl.BlockSpec(memory_space=pltpu.HBM)] * 4 + [vmem_spec],
+        out_specs=(vmem_spec, vmem_spec, any_spec, any_spec, vmem_spec, any_spec, any_spec, vmem_spec),
+        scratch_shapes=[
+            low(count, feats, feats), wide(count, feats, feats), dma((count,)), dma((count,)),
+        ],
+        compiler_params=pltpu.CompilerParams(vmem_limit_bytes=67043328),
+    )(down, up, out_w, qkv_w, small)
+    return (output, d_inputs, d_gain_one, d_kernel, d_qkv, d_out, d_gain_two, d_up, d_down, d_scale)
 
 
 def solution(mesh):

time: 184 us -> 131 us (0.71)
  Pallas kernels: 164 us -> 126 us
  other arithmetic: 10.7 us -> 0 us
  local copies, waits for them, and re-layouts: 7.91 us -> 3.73 us
    pallas_call x1, Pallas kernels: 164 us -> 119 us  [shards(): pl.pallas_call(functools.partial(layer_kernel, cfg), out_shape=(out_type(...]
    convert_element_type x5 -> x0, other arithmetic: 10.7 us -> none  [the longest x1 4.28 us: shards(): up.astype(F32)]
    pallas_call x0 -> x1, Pallas kernels: none -> 7.54 us  [shards(): pl.pallas_call(widen_kernel, out_shape=(out_type((feats,), F32), out_type...]
    reshape x2 -> x0, local copies, waits for them, and re-layouts: 2.1 us -> none  [the longest x1 1.38 us: shards(): small[:9].reshape(3, 3, feats)]
    broadcast_in_dim x4 -> x0, local copies, waits for them, and re-layouts: 2.05 us -> none  [the longest x1 0.68 us: shards(): norm_gain[None]]
    unnamed x12 -> x4, local copies, waits for them, and re-layouts: 2.31 us -> 3.73 us
where the time goes in v3:
time: 131 us; the launch traced here: 130 us
  Pallas kernels  126 us (96%)
  local copies, waits for them, and re-layouts  3.73 us (3%)
    pallas_call x1, Pallas kernels, shards(): pl.pallas_call(functools.partial(layer_kernel, cfg), out_shape=(out_type(...  119 us
    pallas_call x1, Pallas kernels, shards(): pl.pallas_call(widen_kernel, out_shape=(out_type((feats,), F32), out_type...  7.54 us
    unnamed x4, local copies, waits for them, and re-layouts  3.73 us

profile of v3, /device:TPU:1, one launch (start us, length us, event | category | flops | bytes accessed | tf_op | source)
XLA Modules:
  0.0 130.5 jit_solution(14274551621020073667)
XLA Ops:
  0.6 118.5 %shard_map.186 = (bf16[8,128,512]{2,1,0:T(8,128)(2,1)}, f32[8,128,512]{2,1,0:T(8,128)}, bf16[2048,512]{1,0:T(8,128)(2,1)}, bf16[512,2048]{1,0:T(8,128)(2,1)}, bf...) custom-call(s32[8,8]{1,0:T(8,128)} %refs_0_.1, bf16[8,128,512]{2,1,0:T(8,128)(2,1)} %refs_1_.1, ...), custom_call_target="tpu_custom_call" | custom-call | tf_op jit(solution)/shard_map/pallas_call | solution.py:787
  119.2 7.5 %shard_map.187 = (f32[512]{0:T(512)}, f32[3,3,512]{2,1,0:T(4,128)}, f32[3,512,512]{2,1,0:T(8,128)}, f32[512,512]{1,0:T(8,128)}, f32[512]{0:T(512)}, /*index=5*/f...) custom-call(bf16[2048,512]{1,0:T(8,128)(2,1)} %get-tuple-element.27.down, bf16[512,2048]{1,0:T(8,128)(2,1)} %get-tuple-element.28.up, ...), custom_call_target="tpu_custom_call" | custom-call | tf_op jit(solution)/shard_map/pallas_call | solution.py:802
  126.7 0.0 copy-start
  126.7 2.4 %copy.23 = bf16[8,128,512]{2,1,0:T(8,128)(2,1)} copy(bf16[8,128,512]{2,1,0:T(8,128)(2,1)} %get-tuple-element.50) | data formatting | bytes 2097152
  129.2 0.0 copy-done
  129.2 1.3 %copy.24 = f32[8,128,512]{2,1,0:T(8,128)} copy(f32[8,128,512]{2,1,0:T(8,128)S(1)} %copy-done) | data formatting | bytes 4194304
Async XLA Ops:
  126.7 2.4 %copy-start = (f32[8,128,512]{2,1,0:T(8,128)S(1)}, f32[8,128,512]{2,1,0:T(8,128)}, u32[]{:S(2)}) copy-start(f32[8,128,512]{2,1,0:T(8,128)} %get-tuple-element.51) | copy-start | bytes 6291460

commit v4 on v3

v4 whole, which is shorter than its diff:
```python
import functools

import jax
import jax.numpy as jnp
from jax import lax
from jax.experimental import pallas as pl
from jax.experimental.pallas import tpu as pltpu
from jax.sharding import PartitionSpec as P

HEADS = 4
HD = 128
HALF = 9
HALO = 16
PAD = 8
EPS = 1e-05
MESH = pl.DeviceIdType.MESH
F32 = jnp.float32
BF16 = jnp.bfloat16


CHOICE = (4, 0, 1, 1, 1, 7, 0, 1, 1, 0, 1, 5)


def step_orders(seq_size, tm_size):
    seq_bits = [("seq", b) for b in range(seq_size.bit_length() - 1)]
    tm_bits = [("tm", b) for b in range(tm_size.bit_length() - 1)]
    one = lambda bits: [(bit,) for bit in bits]
    two = lambda bits: [tuple(bits[i : i + 2]) for i in range(0, len(bits), 2)]
    core, rest = one(tm_bits[:1]), tm_bits[1:]
    swapped = seq_bits[::-1]
    kinds = [
        core + one(seq_bits) + two(rest),
        core + one(swapped) + two(rest),
        core + one(rest[:1]) + one(seq_bits) + one(rest[1:]),
        core + one(rest[:1]) + one(swapped) + one(rest[1:]),
        core + two(seq_bits) + two(rest),
        core + two(rest) + two(seq_bits),
        core + one(seq_bits) + one(rest),
        core + one(swapped) + one(rest),
    ]
    return kinds, [kinds[c] for c in CHOICE]


def bit_of(axis, bit):
    return lax.rem(lax.axis_index(axis) // (1 << bit), 2)


def peer_of(bits, flips):
    at = {"seq": lax.axis_index("seq"), "tm": lax.axis_index("tm")}
    for i, (axis, bit) in enumerate(bits):
        if flips >> i & 1:
            at[axis] = at[axis] + (1 - 2 * bit_of(axis, bit)) * (1 << bit)
    return at["seq"], at["tm"]


def digit_of(bits, flips=0):
    total = 0
    for i, (axis, bit) in enumerate(bits):
        mine = bit_of(axis, bit)
        total = total + (1 - mine if flips >> i & 1 else mine) * (1 << i)
    return total


class Reducer:
    def __init__(self, orders, rows, part, recv, fulls, sems):
        self.orders, self.rows = orders, rows
        self.part, self.recv, self.fulls = part, recv, fulls
        self.rs_send, self.rs_recv, self.ag_send, self.ag_recv = sems

    def levels(self, unit):
        return len(self.orders[unit])

    def size(self, unit, level):
        return self.rows >> sum(len(bits) for bits in self.orders[unit][:level])

    def owned(self, unit, level):
        off = 0
        for i in range(level):
            off = off + digit_of(self.orders[unit][i]) * self.size(unit, i + 1)
        return off

    def peers(self, unit, level):
        return range(1, 1 << len(self.orders[unit][level]))

    def slot(self, unit, level, flips):
        return sum((1 << len(bits)) - 1 for bits in self.orders[unit][:level]) + flips - 1

    def landing(self, unit, level, flips):
        return self.rows - self.size(unit, level) + (flips - 1) * self.size(unit, level + 1)

    def scatter_copies(self, unit, level):
        bits, found = self.orders[unit][level], []
        size = self.size(unit, level + 1)
        for flips in self.peers(unit, level):
            off = pl.multiple_of(self.owned(unit, level) + digit_of(bits, flips) * size, 16)
            at = self.slot(unit, level, flips)
            found.append(pltpu.make_async_remote_copy(
                src_ref=self.part.at[unit, pl.ds(off, size)],
                dst_ref=self.recv.at[unit, pl.ds(self.landing(unit, level, flips), size)],
                send_sem=self.rs_send.at[unit, at],
                recv_sem=self.rs_recv.at[unit, at],
                device_id=peer_of(bits, flips),
                device_id_type=MESH,
            ))
        return found

    def full(self, unit):
        held = self.fulls[0].shape[0] // self.rows
        index = unit % held
        if unit < held and self.rows == self.fulls[0].shape[1]:
            half = held // 2
            index = 2 * (unit % half) + unit // half
        return self.fulls[unit // held], index * self.rows

    def gather_copies(self, unit, level):
        bits, found = self.orders[unit][level], []
        ref, start = self.full(unit)
        off = pl.multiple_of(start + self.owned(unit, level + 1), 16)
        region = ref.at[pl.ds(off, self.size(unit, level + 1))]
        for flips in self.peers(unit, level):
            at = self.slot(unit, level, flips)
            found.append(pltpu.make_async_remote_copy(
                src_ref=region,
                dst_ref=region,
                send_sem=self.ag_send.at[unit, at],
                recv_sem=self.ag_recv.at[unit, at],
                device_id=peer_of(bits, flips),
                device_id_type=MESH,
            ))
        return found

    def combine(self, unit, level):
        for copy in self.scatter_copies(unit, level):
            copy.wait_recv()
        off, size = self.owned(unit, level + 1), self.size(unit, level + 1)
        step = min(size, 32)

        def body(i, carry):
            here = pl.ds(pl.multiple_of(off + i * step, 16), step)
            total = self.part[unit, here, :].astype(F32)
            for flips in self.peers(unit, level):
                there = pl.ds(pl.multiple_of(self.landing(unit, level, flips) + i * step, 16), step)
                total = total + self.recv[unit, there, :].astype(F32)
            if level == self.levels(unit) - 1:
                ref, start = self.full(unit)
                ref[pl.ds(pl.multiple_of(start + off + i * step, 16), step), :] = total.astype(BF16)
            else:
                self.part[unit, here, :] = total.astype(BF16)
            return carry

        lax.fori_loop(0, size // step, body, 0)

    def tick(self, unit, i):
        levels = self.levels(unit)
        if 0 < i <= levels:
            self.combine(unit, i - 1)
        elif i > levels:
            for copy in self.gather_copies(unit, 2 * levels - i):
                copy.wait_recv()
        if i < levels:
            out = self.scatter_copies(unit, i)
        elif i < 2 * levels:
            out = self.gather_copies(unit, 2 * levels - 1 - i)
        else:
            out = []
        for copy in out:
            copy.start()

    def wait_sends(self, unit):
        for level in range(self.levels(unit)):
            for copy in self.scatter_copies(unit, level) + self.gather_copies(unit, level):
                copy.wait_send()


def plan_steps(orders, small_steps, rows, feats, pieces):
    core_rate, link_rate = 600e3, 115e3
    free, reached, arrival = {}, {}, {}
    levels = {u: len(order) for u, order in enumerate(orders)}
    levels[-1] = len(small_steps)

    def size_of(unit, level):
        return (rows >> sum(len(bits) for bits in orders[unit][: level + 1])) * feats * 2

    def send(unit, now, level):
        bits = (orders[unit] if unit >= 0 else small_steps)[level]
        size = size_of(unit, level) if unit >= 0 else 16 * feats * 4
        wire = 2 * size / link_rate
        near, far = ("tm", 1), ("tm", 2)
        if bits[0] == ("tm", 0):
            uses, lag = [("core", size / core_rate)], 1.1
        elif len(bits) == 2:
            if bits[0][0] == "seq":
                uses, lag = [(bit, 2 * wire) for bit in bits], 3.3
            else:
                uses, lag = [(near, 3 * wire), (far, 4 * wire)], 4.0
        elif bits[0][0] == "seq" or bits[0] == near:
            uses, lag = [(bits[0], wire)], 2.6
        else:
            uses, lag = [(near, wire), (far, 2 * wire)], 3.3
        start = max([now] + [free.get(name, 0.0) for name, _ in uses])
        for name, busy in uses:
            free[name] = start + busy
        return start + max(busy for _, busy in uses) + lag

    def step(unit, now):
        i = reached[unit]
        reached[unit] = i + 1
        cost = 0.05
        if unit >= 0:
            cost = 0.02 + (size_of(unit, i - 1) / 2.4e6 if 0 < i <= levels[unit] else 0.0)
        if i < levels[unit]:
            arrival[unit] = send(unit, now + cost, i)
        elif i < last(unit):
            arrival[unit] = send(unit, now + cost, 2 * levels[unit] - 1 - i)
        return cost

    def last(unit):
        return levels[unit] if unit < 0 else 2 * levels[unit]

    now, placed = 0.0, {}
    for slot, us, begins in pieces:
        now += us
        todo = []
        if begins is not None:
            reached[begins] = 0
            now += step(begins, now)
        while True:
            ready = [u for u in reached if reached[u] <= last(u) and arrival[u] <= now]
            if not ready:
                break
            unit = min(ready, key=lambda u: (arrival[u], u))
            todo.append((unit, reached[unit]))
            now += step(unit, now)
        placed[slot] = todo
    work_end = now
    reached[-1] = 0
    now += step(-1, now)
    tail = []
    while True:
        left = [u for u in reached if reached[u] <= last(u)]
        if not left:
            break
        unit = min(left, key=lambda u: (arrival[u], u))
        now = max(now, arrival[unit])
        tail.append((unit, reached[unit]))
        now += step(unit, now)
    return placed, tail, (work_end, now)


def make_pieces(seqs, ff_blocks, per_unit):
    pairs = seqs // 2
    begun = lambda block: block // per_unit if block % per_unit == per_unit - 1 else None
    pieces = []
    for j in range(ff_blocks):
        pieces += [(("f", j, t), 0.95, None) for t in range(pairs)]
        pieces += [(("d", j), 0.73, begun(j)), (("u", j), 0.73, begun(ff_blocks + j))]
    pieces += [(("x", t), 0.75, None) for t in range(pairs)]
    pieces += [(("b", s), 1.1, None) for s in range(seqs)]
    pieces += [
        ("q", 0.73, begun(2 * ff_blocks + 1)), ("o", 0.73, begun(2 * ff_blocks)), ("w", 1.5, None),
        ("k", 0.73, begun(2 * ff_blocks + 2)), ("v", 0.73, begun(2 * ff_blocks + 3)),
    ]
    pieces += [(("i", s), 0.95, None) for s in range(seqs)]
    return pieces


def beside(tm_size):
    at = lax.axis_index("tm")
    seq = lax.axis_index("seq")
    return [(at < tm_size - 1, (seq, at + 1)), (at > 0, (seq, at - 1))]


def greet(bits, tm_size):
    barrier = pltpu.get_barrier_semaphore()
    for step, flips in bits:
        pl.semaphore_signal(barrier, inc=1, device_id=peer_of(step, flips), device_id_type=MESH)
    for there, peer in beside(tm_size):
        @pl.when(there)
        def _():
            pl.semaphore_signal(barrier, inc=1, device_id=peer, device_id_type=MESH)


def enter(bits, tm_size):
    count = len(bits)
    for there, _ in beside(tm_size):
        count = count + there.astype(jnp.int32)
    pl.semaphore_wait(pltpu.get_barrier_semaphore(), count)


def nn(a, b):
    return lax.dot_general(a, b, (((1,), (0,)), ((), ())), preferred_element_type=F32)


def nt(a, b):
    return lax.dot_general(a, b, (((1,), (1,)), ((), ())), preferred_element_type=F32)


def tn(a, b):
    return lax.dot_general(a, b, (((0,), (0,)), ((), ())), preferred_element_type=F32)


def moments(v):
    mean = jnp.mean(v, axis=-1, keepdims=True)
    centered = v - mean
    var = jnp.mean(centered * centered, axis=-1, keepdims=True)
    return centered, lax.rsqrt(var + EPS)


def fold(v):
    rows, cols = v.shape
    return jnp.sum(v.reshape(rows // 8, 8, cols), axis=0)


def gelu_pair(v):
    c = 0.7978845608028654
    square = v * v
    inner = v * (c + (c * 0.044715) * square)
    t = jnp.tanh(inner)
    half = 0.5 * (1.0 + t)
    slope = half + (0.5 * v) * (1.0 - t * t) * (c + (3.0 * 0.044715 * c) * square)
    return v * half, slope


def loop(count, body):
    def step(i, carry):
        body(i)
        return carry

    lax.fori_loop(0, count, step, 0)


def layer_kernel(cfg, *refs):
    (
        lengths, x_hbm, norm_gain, conv_kernel, mlp_gain, layer_scale, wqkv_hbm, wout_hbm, wup_hbm, wdown_hbm, cot_hbm,
        out_hbm, din_hbm, down_hbm, up_hbm, outw_hbm, qkvw_hbm, small_out,
        params, x, cot, wqkv, wout, wup, wdown, halo_lo, halo_hi, nf, link,
        act_q, act_k, act_v, qs, ks, vs, prob, att, res, n2, dm, hid, du, dbr, da, outs,
        dke, dve, dmx, msg_hi, msg_lo, got_lo, got_hi, dq_hi, dq_lo, dq_got_lo, dq_got_hi,
        edge, edge_mix, sums, small_cur, small_recv,
        part, recv,
        in_sem, out_sem, halo_send, halo_recv, rs_send, rs_recv, ag_send, ag_recv, sm_send, sm_recv,
    ) = refs
    orders, small_steps, rows, seqs, frames, feats, ff, tm_size = cfg
    units = len(orders)
    levels = len(small_steps)
    greeted = sorted({(bits, flips) for order in orders + [small_steps] for bits in order for flips in range(1, 1 << len(bits))})
    known = {}
    for bits, flips in greeted:
        known.setdefault(tuple(bit for i, bit in enumerate(bits) if flips >> i & 1), (bits, flips))
    greeted = list(known.values())
    ext = frames + 2 * HALO
    own = PAD + HALO
    seq_length = frames * tm_size
    vids = lengths.shape[1]
    temper = HD ** (-0.5)
    lanes = [pl.ds(c * 128, 128) for c in range(feats // 128)]
    pairs = seqs // 2
    per_unit = rows // feats
    base = lax.axis_index("tm") * frames
    red = Reducer(orders, rows, part, recv, (hid, du), (rs_send, rs_recv, ag_send, ag_recv))

    loads = [
        pltpu.make_async_copy(src, dst, in_sem.at[i])
        for i, (src, dst) in enumerate(
            [(x_hbm, x), (wqkv_hbm, wqkv), (wout_hbm, wout), (wup_hbm, wup), (wdown_hbm, wdown), (cot_hbm, cot)]
        )
    ]
    for load in loads:
        load.start()

    class Across:
        def __init__(self, src, dst, i, side):
            (self.sends, peer), (self.gets, _) = beside(tm_size)[side], beside(tm_size)[1 - side]
            self.copy = pltpu.make_async_remote_copy(
                src_ref=src, dst_ref=dst, send_sem=halo_send.at[i], recv_sem=halo_recv.at[i],
                device_id=peer, device_id_type=MESH,
            )

        def start(self):
            pl.when(self.sends)(lambda: self.copy.start())

        def wait_recv(self):
            pl.when(self.gets)(lambda: self.copy.wait_recv())

        def wait_send(self):
            pl.when(self.sends)(lambda: self.copy.wait_send())

    greet(greeted, tm_size)
    for n in range(3):
        params[pl.ds(3 * n, 3), :] = conv_kernel[n].astype(F32)
    for i, src in enumerate((norm_gain, mlp_gain, layer_scale)):
        params[pl.ds(9 + i, 1), :] = src[...].astype(F32).reshape(1, feats)

    def clear_missing(side, refs_in):
        there = beside(tm_size)[side][0]

        @pl.when(jnp.logical_not(there))
        def _():
            for ref in refs_in:
                ref[...] = jnp.zeros_like(ref)

    clear_missing(1, (halo_lo, got_lo, dq_got_lo))
    clear_missing(0, (halo_hi, got_hi, dq_got_hi))
    to_next = Across(x.at[:, pl.ds(frames - HALO, HALO)], halo_lo, 0, 0)
    to_prev = Across(x.at[:, pl.ds(0, HALO)], halo_hi, 1, 1)
    sums[...] = jnp.zeros_like(sums)

    def bounds_of(s):
        total, found = 0, []
        for j in range(vids):
            total = total + lengths[s, j]
            found.append(total)
        return found

    gain_one = params[pl.ds(9, 1), :]
    gain_two = params[pl.ds(10, 1), :]
    scale = params[pl.ds(11, 1), :]

    def normed_rows(rows_in):
        centered, r = moments(rows_in.astype(F32))
        return (centered * r * gain_one).astype(BF16).astype(F32)

    loads[0].wait()

    def norm_own(s):
        nf[s, pl.ds(own, frames), :] = normed_rows(x[s])
        zero = jnp.zeros((PAD, feats), F32)
        nf[s, pl.ds(0, PAD), :] = zero
        nf[s, pl.ds(PAD + ext, PAD), :] = zero
        pos = base - own + lax.broadcasted_iota(jnp.int32, (ext + 2 * PAD, 128), 0)
        cut = pos == 0
        for bound in bounds_of(s):
            cut = cut | (pos == bound)
        link[s] = jnp.where(cut, 0.0, 1.0)

    loop(seqs, norm_own)
    enter(greeted, tm_size)
    to_next.start()
    to_prev.start()
    loads[1].wait()
    streams = ((act_q, qs, 0), (act_k, ks, HALO), (act_v, vs, HALO))

    def mixed_rows(s, start, count, lane):
        before = nf[s, pl.ds(PAD + start - 1, count), lane] * link[s, pl.ds(PAD + start, count), :]
        centre = nf[s, pl.ds(PAD + start, count), lane]
        after = nf[s, pl.ds(PAD + start + 1, count), lane] * link[s, pl.ds(PAD + start + 1, count), :]
        found = []
        for n in range(3):
            k0, k1, k2 = (params[pl.ds(3 * n + c, 1), lane] for c in range(3))
            found.append((k0 * before + k1 * centre + k2 * after).astype(BF16))
        return found

    def mix_project(t):
        two = pl.ds(2 * t, 2)
        rows_of = lambda i: [mixed_rows(2 * t + i, HALO, frames, lane) for lane in lanes]
        found = [rows_of(0), rows_of(1)]
        acts = [
            jnp.concatenate([jnp.concatenate([m[n] for m in half], axis=1) for half in found], axis=0)
            for n in range(3)
        ]
        values = [nn(act, wqkv[n]).astype(BF16) for n, act in enumerate(acts)]
        for (kept, dst, skip), act, value in zip(streams, acts, values):
            kept[two] = act.reshape(2, frames, feats)
            dst[two, pl.ds(skip, frames), :] = value.reshape(2, frames, feats)

    loop(pairs, mix_project)
    to_next.wait_recv()
    to_prev.wait_recv()
    ends = 2 * HALO

    def norm_halo(i):
        four = pl.ds(pl.multiple_of(4 * i, 4), 4)
        for src, at in ((halo_lo, PAD), (halo_hi, own + frames)):
            value = normed_rows(src[four].reshape(4 * HALO, feats))
            nf[four, pl.ds(at, HALO), :] = value.reshape(4, HALO, feats)

    loop(seqs // 4, norm_halo)

    def mix_ends(s):
        sides = ((0, 0, HALO, 0), (ends, frames, 0, frames - HALO))
        found = [[mixed_rows(s, start, ends, lane) for lane in lanes] for _, start, _, _ in sides]
        for (at, _, keep, row), half in zip(sides, found):
            for n in range(3):
                mixed = jnp.concatenate([m[n] for m in half], axis=1)
                tile = pl.ds(pl.multiple_of((n * seqs + s) * 2 * ends + at, ends), ends)
                hid[tile, :] = mixed
                streams[n][0][s, pl.ds(row, HALO), :] = mixed[keep : keep + HALO]

    loop(seqs, mix_ends)
    for n, (_, dst, skip) in enumerate(streams):
        count = seqs * 2 * ends
        value = nn(hid[pl.ds(n * count, count), :], wqkv[n]).astype(BF16).reshape(seqs, 2 * ends, feats)
        piece = lambda first, last: lax.slice_in_dim(value, first, last, axis=1)
        if skip:
            dst[:, pl.ds(0, ends), :] = piece(0, ends)
            dst[:, pl.ds(frames, ends), :] = piece(ends, 2 * ends)
        else:
            dst[:, pl.ds(0, HALO), :] = piece(HALO, ends)
            dst[:, pl.ds(frames - HALO, HALO), :] = piece(ends, ends + HALO)

    def attend(s):
        key = lax.broadcasted_iota(jnp.int32, (ext, frames), 0) - HALO
        query = lax.broadcasted_iota(jnp.int32, (ext, frames), 1)
        band = (key - query <= HALF) & (key - query >= -HALF)
        pos_k = key + base
        pos_q = lax.broadcasted_iota(jnp.int32, (8, frames), 1) + base
        seg_k = jnp.zeros((ext, frames), jnp.int32)
        seg_q = jnp.zeros((8, frames), jnp.int32)
        for bound in bounds_of(s):
            seg_k = seg_k + (pos_k >= bound).astype(jnp.int32)
            seg_q = seg_q + (pos_q >= bound).astype(jnp.int32)
        allowed = band & (seg_k == seg_q[0:1]) & (pos_k >= 0) & (pos_k < seq_length)
        bias = jnp.where(allowed, 0.0, -1e30)
        heads = [pl.ds(h * HD, HD) for h in range(HEADS)]
        scores = [nt(ks[s, :, head], qs[s, :, head]) * temper + bias for head in heads]
        raised = [jnp.exp(value - jnp.max(value, axis=0, keepdims=True)) for value in scores]
        probs = [value * (1.0 / jnp.sum(value, axis=0, keepdims=True)) for value in raised]
        for h, head in enumerate(heads):
            prob[s, h] = probs[h]
        found = [tn(probs[h].astype(BF16), vs[s, :, head]) for h, head in enumerate(heads)]
        for h, head in enumerate(heads):
            att[s, :, head] = found[h].astype(BF16)

    loop(seqs, attend)
    for load in loads[2:]:
        load.wait()
    tall = 2 * frames
    chunk = feats
    tokens = seqs * frames
    out_copies = [
        pltpu.make_async_copy(outs.at[pl.ds(2 * t, 2)], out_hbm.at[pl.ds(2 * t, 2)], out_sem.at[t])
        for t in range(pairs)
    ]

    def flat(ref, t):
        return ref[pl.ds(2 * t, 2)].reshape(tall, ref.shape[2])

    def back(value):
        return value.reshape(2, frames, feats)

    def residual_norm(t):
        two = pl.ds(2 * t, 2)
        residual = flat(x, t).astype(F32) + nn(flat(att, t), wout[...])
        d_mlp = (flat(cot, t).astype(F32) * scale).astype(BF16)
        centered, r = moments(residual)
        normed_two = (centered * r * gain_two).astype(BF16)
        res[two] = back(residual)
        n2[two] = back(normed_two)
        dm[two] = back(d_mlp)

    loop(pairs, residual_norm)
    whole = lambda ref: ref[...].reshape(seqs * frames, ref.shape[2])
    early = pl.ds(0, frames)

    def place(block, value):
        part[block // per_unit, pl.ds((block % per_unit) * feats, feats), :] = value.astype(BF16)

    ff_blocks = ff // feats

    def block_copy(block):
        ref, start = red.full(block // per_unit)
        src = ref.at[pl.ds(start + (block % per_unit) * feats, feats)]
        if block < ff_blocks:
            dst = down_hbm.at[pl.ds(block * feats, feats)]
        elif block < 2 * ff_blocks:
            dst = up_hbm.at[:, pl.ds((block - ff_blocks) * feats, feats)]
        elif block == 2 * ff_blocks:
            dst = outw_hbm
        else:
            dst = qkvw_hbm.at[block - 2 * ff_blocks - 1]
        return pltpu.make_async_copy(src, dst, out_sem.at[pairs + 1 + block])

    def unit_begun(block):
        return block // per_unit if block % per_unit == per_unit - 1 else None

    placed, tail, _ = plan_steps(orders, small_steps, rows, feats, make_pieces(seqs, ff_blocks, per_unit))

    def advance(u, i):
        red.tick(u, i)
        if i == 2 * red.levels(u):
            for block in range(u * per_unit, (u + 1) * per_unit):
                block_copy(block).start()

    def slot(name, index=None, count=0):
        if index is None:
            for u, i in placed[name]:
                advance(u, i)
            return
        for k in range(count):
            if placed[name + (k,)]:
                pl.when(index == k)(lambda k=k: [advance(u, i) for u, i in placed[name + (k,)]] and None)

    def begin(block):
        u = unit_begun(block)
        if u is not None:
            advance(u, 0)

    mlp_sum, e_sum = dke, dve

    for j in range(ff_blocks):
        cols = pl.ds(j * chunk, chunk)

        def hidden_chunk(t, j=j, cols=cols):
            upper = nn(flat(n2, t), wup[:, cols])
            d_hidden = nt(flat(dm, t), wdown[cols, :])
            value, slope = gelu_pair(upper)
            value, slope = value.astype(BF16), (slope * d_hidden).astype(BF16)
            tile = pl.ds(pl.multiple_of(j * tokens + t * tall, tall), tall)
            mlp_part, e_part = nn(value, wdown[cols, :]), nt(slope, wup[:, cols])
            two = pl.ds(2 * t, 2)
            if j:
                mlp_part = mlp_part + mlp_sum[two, early, :].reshape(tall, feats)
                e_part = e_part + e_sum[two, early, :].reshape(tall, feats)
            hid[tile, :] = value
            du[tile, :] = slope
            mlp_sum[two, early, :] = back(mlp_part)
            e_sum[two, early, :] = back(e_part)
            slot(("f", j), t, pairs)

        loop(pairs, hidden_chunk)
        rows_j = pl.ds(j * tokens, tokens)
        place(j, tn(hid[rows_j, :], whole(dm)))
        begin(j)
        slot(("d", j))
        place(ff_blocks + j, tn(whole(n2), du[rows_j, :]))
        begin(ff_blocks + j)
        slot(("u", j))

    def feed_back(t):
        two = pl.ds(2 * t, 2)
        mlp_out = mlp_sum[two, early, :].reshape(tall, feats)
        e = e_sum[two, early, :].reshape(tall, feats)
        residual = flat(res, t)
        cotan = flat(cot, t).astype(F32)
        output = (residual + scale * mlp_out).astype(BF16)
        centered, r = moments(residual)
        xhat = centered * r
        eg = e * gain_two
        d_res = cotan + r * (
            eg - jnp.mean(eg, axis=-1, keepdims=True) - xhat * jnp.mean(eg * xhat, axis=-1, keepdims=True)
        )
        d_branch = d_res.astype(BF16)
        d_att = nt(d_branch, wout[...]).astype(BF16)
        scale_sum = sums[11] + fold(cotan * mlp_out)
        gain_sum = sums[10] + fold(e * xhat)
        outs[two] = back(output)
        res[two] = back(d_res)
        dbr[two] = back(d_branch)
        da[two] = back(d_att)
        sums[11] = scale_sum
        sums[10] = gain_sum
        slot(("x",), t, pairs)

    loop(pairs, feed_back)
    for copy in out_copies:
        copy.start()


    dq = dm
    dkl, dvl = n2, att

    exchange = []
    for t in range(pairs):
        two = pl.ds(2 * t, 2)
        exchange += [
            Across(msg_hi.at[two], got_lo.at[two], 4 + 2 * t, 0),
            Across(msg_lo.at[two], got_hi.at[two], 5 + 2 * t, 1),
        ]
    exchange += [Across(dq_hi, dq_got_lo, 2, 0), Across(dq_lo, dq_got_hi, 3, 1)]

    def attend_back(s):
        heads = [pl.ds(h * HD, HD) for h in range(HEADS)]
        d_atts = [da[s, :, head] for head in heads]
        probs = [prob[s, h] for h in range(HEADS)]
        d_weights = [nt(vs[s, :, head], d_att) for head, d_att in zip(heads, d_atts)]
        d_scores = [
            (p * (d_w - jnp.sum(p * d_w, axis=0, keepdims=True))).astype(BF16) for p, d_w in zip(probs, d_weights)
        ]
        found = [
            (tn(d_s, ks[s, :, head]), nn(d_s, qs[s, :, head]), nn(p.astype(BF16), d_att))
            for head, d_s, p, d_att in zip(heads, d_scores, probs, d_atts)
        ]
        for head, (d_q, d_k, d_v) in zip(heads, found):
            dq[s, :, head] = (d_q * temper).astype(BF16)
            dke[s, :, head] = d_k * temper
            dve[s, :, head] = d_v
        for i, src in enumerate((dke, dve)):
            cols = pl.ds(i * feats, feats)
            msg_hi[s, :, cols] = src[s, pl.ds(HALO + frames - 1, HALO), :].astype(BF16)
            msg_lo[s, :, cols] = src[s, pl.ds(1, HALO), :].astype(BF16)
        dq_hi[pl.ds(s, 1), :] = dq[s, pl.ds(frames - 16, 16), :].astype(F32)[15:16]
        dq_lo[pl.ds(s, 1), :] = dq[s, pl.ds(0, 16), :].astype(F32)[0:1]
        for t in range(pairs):
            pl.when(s == 2 * t + 1)(lambda t=t: [copy.start() for copy in exchange[2 * t : 2 * t + 2]] and None)
        slot(("b",), s, seqs)

    loop(seqs, attend_back)
    for copy in exchange[2 * pairs :]:
        copy.start()
    place(2 * ff_blocks + 1, tn(whole(act_q), whole(dq)))
    begin(2 * ff_blocks + 1)
    slot("q")
    place(2 * ff_blocks, tn(whole(att), whole(dbr)))
    begin(2 * ff_blocks)
    slot("o")
    for copy in exchange:
        copy.wait_recv()
    edge[0, pl.ds(0, seqs), :] = dq_got_lo[...]
    edge[0, pl.ds(seqs, seqs), :] = dq_got_hi[...]

    def settle(s):
        for i, (src, dst) in enumerate(((dke, dkl), (dve, dvl))):
            cols = pl.ds(i * feats, feats)
            low = pl.ds(HALO - 1, HALO)
            high = pl.ds(HALO + frames - HALO + 1, HALO)
            src[s, low, :] = src[s, low, :] + got_lo[s, :, cols].astype(F32)
            src[s, high, :] = src[s, high, :] + got_hi[s, :, cols].astype(F32)
            dst[s] = src[s, pl.ds(HALO, frames), :].astype(BF16)
            edge[i + 1, pl.ds(s, 1), :] = src[s, pl.ds(HALO - 1, 1), :]
            edge[i + 1, pl.ds(seqs + s, 1), :] = src[s, pl.ds(HALO + frames, 1), :]

    loop(seqs, settle)
    slot("w")
    place(2 * ff_blocks + 2, tn(whole(act_k), whole(dkl)))
    begin(2 * ff_blocks + 2)
    slot("k")
    place(2 * ff_blocks + 3, tn(whole(act_v), whole(dvl)))
    begin(2 * ff_blocks + 3)
    slot("v")
    for n in range(3):
        edge_mix[n] = nt(edge[n].astype(BF16), wqkv[n])

    def input_grads(t):
        two = pl.ds(2 * t, 2)
        for n, src in enumerate((dq, dkl, dvl)):
            value = nt(src[two].reshape(tall, feats), wqkv[n])
            dmx[n, :, pl.ds(PAD, frames), :] = value.reshape(2, frames, feats)
        for i in range(2):
            s = 2 * t + i
            for n in range(3):
                dmx[n, i, pl.ds(PAD - 1, 1), :] = edge_mix[n, pl.ds(s, 1), :]
                dmx[n, i, pl.ds(PAD + frames, 1), :] = edge_mix[n, pl.ds(seqs + s, 1), :]
            here = link[s, pl.ds(own, frames), :]
            after = link[s, pl.ds(own + 1, frames), :]
            e_parts, taps = [], []
            for lane in lanes:
                left = nf[s, pl.ds(own - 1, frames), lane] * here
                mid = nf[s, pl.ds(own, frames), lane]
                right = nf[s, pl.ds(own + 1, frames), lane] * after
                from_left, from_mid, from_right = 0.0, 0.0, 0.0
                for n in range(3):
                    k0, k1, k2 = (params[pl.ds(3 * n + c, 1), lane] for c in range(3))
                    g = dmx[n, i, pl.ds(PAD, frames), lane]
                    taps.append([fold(g * left), fold(g * mid), fold(g * right)])
                    from_mid = from_mid + k1 * g
                    from_right = from_right + k0 * dmx[n, i, pl.ds(PAD + 1, frames), lane]
                    from_left = from_left + k2 * dmx[n, i, pl.ds(PAD - 1, frames), lane]
                e_parts.append(from_mid + from_right * after + from_left * here)
            e = jnp.concatenate(e_parts, axis=1)
            centered, r = moments(x[s].astype(F32))
            xhat = centered * r
            eg = e * gain_one
            d_in = res[s] + r * (
                eg - jnp.mean(eg, axis=-1, keepdims=True) - xhat * jnp.mean(eg * xhat, axis=-1, keepdims=True)
            )
            for n in range(3):
                for c in range(3):
                    tap = jnp.concatenate([taps[3 * l + n][c] for l in range(len(lanes))], axis=1)
                    sums[3 * n + c] = sums[3 * n + c] + tap
            sums[9] = sums[9] + fold(e * xhat)
            res[s] = d_in
            for k in range(i, seqs, 2):
                if placed[("i", k)]:
                    pl.when(s == k)(lambda k=k: [advance(u, step) for u, step in placed[("i", k)]] and None)

    loop(pairs, input_grads)
    din_copy = pltpu.make_async_copy(res, din_hbm, out_sem.at[pairs])
    din_copy.start()
    small_cur[0] = jnp.sum(sums[...], axis=1)

    def small_copy(level):
        peer = peer_of(small_steps[level], 1)
        return pltpu.make_async_remote_copy(
            src_ref=small_cur.at[level], dst_ref=small_recv.at[level],
            send_sem=sm_send.at[level], recv_sem=sm_recv.at[level],
            device_id=peer, device_id_type=MESH,
        )

    small_copy(0).start()
    for u, small_at in tail:
        if u >= 0:
            advance(u, small_at)
            continue
        small_copy(small_at - 1).wait_recv()
        total = small_cur[small_at - 1] + small_recv[small_at - 1]
        if small_at < levels:
            small_cur[small_at] = total
            small_copy(small_at).start()
        else:
            small_out[...] = total
    to_next.wait_send()
    to_prev.wait_send()
    for copy in exchange:
        copy.wait_send()
    for level in range(levels):
        small_copy(level).wait_send()
    for u in range(units):
        red.wait_sends(u)
    for copy in out_copies + [din_copy] + [block_copy(b) for b in range(2 * ff_blocks + 4)]:
        copy.wait()


def widen_kernel(
    output_in, d_in, down, up, out_w, qkv_w, small, output, d_inputs, d_gain_one, d_kernel, d_qkv, d_out, d_gain_two, d_up, d_down, d_scale,
    low_held, wide_held, narrow, broad, in_sem, out_sem,
):
    count, feats, _ = narrow.shape
    ff_blocks = (count - 4) // 2
    moves = []
    for j in range(ff_blocks):
        here = pl.ds(j * feats, feats)
        moves.append((down.at[here], d_down.at[here]))
    for j in range(ff_blocks):
        here = pl.ds(j * feats, feats)
        moves.append((up.at[:, here], d_up.at[:, here]))
    moves.append((out_w, d_out))
    for n in range(3):
        moves.append((qkv_w.at[n], d_qkv.at[n]))
    loads = [pltpu.make_async_copy(m[0], narrow.at[i], in_sem.at[i]) for i, m in enumerate(moves)]
    stores = [pltpu.make_async_copy(broad.at[i], m[1], out_sem.at[i]) for i, m in enumerate(moves)]
    passes = []
    for i, (src, held, dst) in enumerate(((output_in, low_held, output), (d_in, wide_held, d_inputs))):
        passes.append((
            pltpu.make_async_copy(src, held, in_sem.at[count + i]),
            pltpu.make_async_copy(held, dst, out_sem.at[count + i]),
        ))
    for load in loads + [get for get, _ in passes]:
        load.start()
    for n in range(3):
        d_kernel[n] = small[pl.ds(3 * n, 3), :]
    for i, dst in enumerate((d_gain_one, d_gain_two, d_scale)):
        dst[...] = small[pl.ds(9 + i, 1), :].reshape(feats)
    for i in range(count):
        loads[i].wait()

        def widen(r):
            here = pl.ds(pl.multiple_of(r * 32, 32), 32)
            broad[i, here, :] = narrow[i, here, :].astype(F32)

        loop(feats // 32, widen)
        stores[i].start()
    for get, put in passes:
        get.wait()
        put.start()
    for store in stores + [put for _, put in passes]:
        store.wait()


def shards(
    inputs, lengths, norm_gain, conv_kernel, qkv_weight, out_weight, mlp_gain, up_weight,
    down_weight, layer_scale, cotangent,
):
    seqs, frames, feats = inputs.shape
    ff = up_weight.shape[1]
    seq_size, tm_size = lax.axis_size("seq"), lax.axis_size("tm")
    rows = max(feats, 16 * seq_size * tm_size)
    units = (2 * ff + 4 * feats) // rows
    kinds, orders = step_orders(seq_size, tm_size)
    orders, small_steps = orders[:units], kinds[-2]
    levels = len(small_steps)
    copies = max(sum((1 << len(bits)) - 1 for bits in order) for order in orders)
    ext = frames + 2 * HALO
    dma = pltpu.SemaphoreType.DMA
    any_spec = pl.BlockSpec(memory_space=pl.ANY)
    vmem_spec = pl.BlockSpec(memory_space=pltpu.VMEM)
    low = lambda *shape: pltpu.VMEM(shape, BF16)
    wide = lambda *shape: pltpu.VMEM(shape, F32)
    acts = lambda: low(seqs, frames, feats)
    acts_ext = lambda: low(seqs, ext, feats)
    scratch = [
        wide(16, feats), acts(), acts(), low(3, feats, feats), low(feats, feats), low(feats, ff), low(ff, feats),
        low(seqs, HALO, feats), low(seqs, HALO, feats),
        wide(seqs, ext + 2 * PAD, feats), wide(seqs, ext + 2 * PAD, 128),
        acts(), acts(), acts(), acts(), acts_ext(), acts_ext(),
        wide(seqs, HEADS, ext, frames), acts(), wide(seqs, frames, feats), acts(), acts(),
        low(seqs * frames * ff // feats, feats), low(seqs * frames * ff // feats, feats), acts(), acts(), acts(),
        wide(seqs, ext, feats), wide(seqs, ext, feats), wide(3, 2, frames + 2 * PAD, feats),
        low(seqs, HALO, 2 * feats), low(seqs, HALO, 2 * feats), low(seqs, HALO, 2 * feats), low(seqs, HALO, 2 * feats),
        wide(seqs, feats), wide(seqs, feats), wide(seqs, feats), wide(seqs, feats),
        wide(3, 2 * seqs, feats), wide(3, 2 * seqs, feats), wide(16, 8, feats),
        wide(levels, 16, feats), wide(levels, 16, feats),
        low(units, rows, feats), low(units, rows, feats),
        dma((6,)), dma((seqs // 2 + 1 + (2 * ff + 4 * feats) // feats,)), dma((4 + seqs,)), dma((4 + seqs,)),
        dma((units, copies)), dma((units, copies)), dma((units, copies)), dma((units, copies)),
        dma((levels,)), dma((levels,)),
    ]
    cfg = (orders, small_steps, rows, seqs, frames, feats, ff, tm_size)
    out_type = jax.ShapeDtypeStruct
    output, d_inputs, down, up, out_w, qkv_w, small = pl.pallas_call(
        functools.partial(layer_kernel, cfg),
        out_shape=(
            out_type(inputs.shape, BF16), out_type(inputs.shape, F32), out_type((ff, feats), BF16),
            out_type((feats, ff), BF16), out_type((feats, feats), BF16), out_type((3, feats, feats), BF16),
            out_type((16, feats), F32),
        ),
        in_specs=[pl.BlockSpec(memory_space=pltpu.SMEM), any_spec] + [vmem_spec] * 4 + [any_spec] * 5,
        out_specs=(any_spec,) * 6 + (vmem_spec,),
        scratch_shapes=scratch,
        compiler_params=pltpu.CompilerParams(
            collective_id=0, has_side_effects=True, vmem_limit_bytes=67043328
        ),
    )(lengths, inputs, norm_gain, conv_kernel, mlp_gain, layer_scale, qkv_weight, out_weight, up_weight, down_weight, cotangent)
    count = (2 * ff + 4 * feats) // feats
    hbm_spec = pl.BlockSpec(memory_space=pltpu.HBM)
    return pl.pallas_call(
        widen_kernel,
        out_shape=(
            out_type(inputs.shape, BF16), out_type(inputs.shape, F32),
            out_type((feats,), F32), out_type((3, 3, feats), F32), out_type((3, feats, feats), F32),
            out_type((feats, feats), F32), out_type((feats,), F32), out_type((feats, ff), F32),
            out_type((ff, feats), F32), out_type((feats,), F32),
        ),
        in_specs=[hbm_spec] * 6 + [vmem_spec],
        out_specs=(hbm_spec,) * 2 + (vmem_spec, vmem_spec, hbm_spec, hbm_spec, vmem_spec, hbm_spec, hbm_spec, vmem_spec),
        scratch_shapes=[
            acts(), wide(seqs, frames, feats), low(count, feats, feats), wide(count, feats, feats),
            dma((count + 2,)), dma((count + 2,)),
        ],
        compiler_params=pltpu.CompilerParams(vmem_limit_bytes=67043328),
    )(output, d_inputs, down, up, out_w, qkv_w, small)


def solution(mesh):
    split = P("seq", "tm", None)
    return jax.shard_map(
        shards,
        mesh=mesh,
        in_specs=(split, P("seq", None)) + (P(),) * 8 + (split,),
        out_specs=(split, split) + (P(),) * 8,
        check_vma=False,
    )
```

time: 131 us -> 112 us (0.85)
  Pallas kernels: 126 us -> 110 us
  local copies, waits for them, and re-layouts: 3.73 us -> 0 us
    pallas_call x1, Pallas kernels: 119 us -> 99.8 us  [shards(): pl.pallas_call(functools.partial(layer_kernel, cfg), out_shape=(out_type(...]
    unnamed x4 -> x0, local copies, waits for them, and re-layouts: 3.73 us -> none
    pallas_call x1, Pallas kernels: 7.54 us -> 10.6 us  [shards(): pl.pallas_call(widen_kernel, out_shape=(out_type(inputs.shape, BF16), out...]
where the time goes in v4:
time: 112 us; the launch traced here: 111 us
  Pallas kernels  110 us (98%)
    pallas_call x1, Pallas kernels, shards(): pl.pallas_call(functools.partial(layer_kernel, cfg), out_shape=(out_type(...  99.8 us
    pallas_call x1, Pallas kernels, shards(): pl.pallas_call(widen_kernel, out_shape=(out_type(inputs.shape, BF16), out...  10.6 us

profile of v4, /device:TPU:1, one launch (start us, length us, event | category | flops | bytes accessed | tf_op | source)
XLA Modules:
  0.0 111.2 jit_solution(16781470274390574375)
XLA Ops:
  0.6 99.8 %shard_map.186 = (bf16[8,128,512]{2,1,0:T(8,128)(2,1)}, f32[8,128,512]{2,1,0:T(8,128)}, bf16[2048,512]{1,0:T(8,128)(2,1)}, bf16[512,2048]{1,0:T(8,128)(2,1)}, bf...) custom-call(s32[8,8]{1,0:T(8,128)} %refs_0_.1, bf16[8,128,512]{2,1,0:T(8,128)(2,1)} %refs_1_.1, ...), custom_call_target="tpu_custom_call" | custom-call | tf_op jit(solution)/shard_map/pallas_call | solution.py:899
  100.4 10.6 %shard_map.187 = (bf16[8,128,512]{2,1,0:T(8,128)(2,1)}, f32[8,128,512]{2,1,0:T(8,128)}, f32[512]{0:T(512)}, f32[3,3,512]{2,1,0:T(4,128)}, f32[3,512,512]{2,1,0:T...) custom-call(bf16[8,128,512]{2,1,0:T(8,128)(2,1)} %get-tuple-element.17, ...), custom_call_target="tpu_custom_call" | custom-call | tf_op jit(solution)/shard_map/pallas_call | solution.py:915

commit v5 on v4

--- a/solution.py
+++ b/solution.py
@@ -18,7 +18,7 @@
 BF16 = jnp.bfloat16
 
 
-CHOICE = (4, 0, 1, 1, 1, 7, 0, 1, 1, 0, 1, 5)
+CHOICE = (4, 4, 10, 7, 4, 10, 10, 6, 4, 5, 4, 4)
 
 
 def step_orders(seq_size, tm_size):
@@ -37,6 +37,13 @@
         core + two(rest) + two(seq_bits),
         core + one(seq_bits) + one(rest),
         core + one(swapped) + one(rest),
+        core + two(rest) + one(seq_bits),
+        core + two(rest) + one(swapped),
+        core + two(seq_bits) + one(rest),
+        core + one(seq_bits[:1]) + two(rest) + one(seq_bits[1:]),
+        core + one(swapped[:1]) + two(rest) + one(swapped[1:]),
+        core + one(seq_bits[:1]) + one(rest[:1]) + one(seq_bits[1:]) + one(rest[1:]),
+        core + one(swapped[:1]) + one(rest[:1]) + one(swapped[1:]) + one(rest[1:]),
     ]
     return kinds, [kinds[c] for c in CHOICE]
 
@@ -59,6 +66,15 @@
         mine = bit_of(axis, bit)
         total = total + (1 - mine if flips >> i & 1 else mine) * (1 << i)
     return total
+
+
+def gathered_at(unit, rows, held_rows, feats):
+    held = held_rows // rows
+    index = unit % held
+    if unit < held and rows == feats:
+        half = held // 2
+        index = 2 * (unit % half) + unit // half
+    return unit // held, index * rows
 
 
 class Reducer:
@@ -105,12 +121,8 @@
         return found
 
     def full(self, unit):
-        held = self.fulls[0].shape[0] // self.rows
-        index = unit % held
-        if unit < held and self.rows == self.fulls[0].shape[1]:
-            half = held // 2
-            index = 2 * (unit % half) + unit // half
-        return self.fulls[unit // held], index * self.rows
+        which, start = gathered_at(unit, self.rows, *self.fulls[0].shape)
+        return self.fulls[which], start
 
     def gather_copies(self, unit, level):
         bits, found = self.orders[unit][level], []
@@ -173,7 +185,7 @@
 
 
 def plan_steps(orders, small_steps, rows, feats, pieces):
-    core_rate, link_rate = 600e3, 115e3
+    core_rate, link_rate = 600e3, 104e3
     free, reached, arrival = {}, {}, {}
     levels = {u: len(order) for u, order in enumerate(orders)}
     levels[-1] = len(small_steps)
@@ -217,9 +229,13 @@
     def last(unit):
         return levels[unit] if unit < 0 else 2 * levels[unit]
 
-    now, placed = 0.0, {}
+    now, crossed, placed = 0.0, 0.0, {}
     for slot, us, begins in pieces:
-        now += us
+        now = (max(now, crossed) if slot == "w" else now) + us
+        if slot[0] == "b" and slot[1] % 2:
+            free[("tm", 1)] = max(now, free.get(("tm", 1), 0.0)) + 0.65
+            free[("tm", 2)] = max(now, free.get(("tm", 2), 0.0)) + 0.65
+            crossed = max(free[("tm", 1)], free[("tm", 2)]) + 2.6
         todo = []
         if begins is not None:
             reached[begins] = 0
@@ -252,15 +268,15 @@
     begun = lambda block: block // per_unit if block % per_unit == per_unit - 1 else None
     pieces = []
     for j in range(ff_blocks):
-        pieces += [(("f", j, t), 0.95, None) for t in range(pairs)]
+        pieces += [(("f", j, t), 0.93, None) for t in range(pairs)]
         pieces += [(("d", j), 0.73, begun(j)), (("u", j), 0.73, begun(ff_blocks + j))]
-    pieces += [(("x", t), 0.75, None) for t in range(pairs)]
-    pieces += [(("b", s), 1.1, None) for s in range(seqs)]
+    pieces += [(("x", t), 0.63, None) for t in range(pairs)]
+    pieces += [(("b", s), 0.68, None) for s in range(seqs)]
     pieces += [
-        ("q", 0.73, begun(2 * ff_blocks + 1)), ("o", 0.73, begun(2 * ff_blocks)), ("w", 1.5, None),
+        ("q", 0.73, begun(2 * ff_blocks + 1)), ("o", 0.73, begun(2 * ff_blocks)), ("w", 0.8, None),
         ("k", 0.73, begun(2 * ff_blocks + 2)), ("v", 0.73, begun(2 * ff_blocks + 3)),
     ]
-    pieces += [(("i", s), 0.95, None) for s in range(seqs)]
+    pieces += [(("i", s), 0.92, None) for s in range(seqs)]
     return pieces
 
 
@@ -332,13 +348,13 @@
 def layer_kernel(cfg, *refs):
     (
         lengths, x_hbm, norm_gain, conv_kernel, mlp_gain, layer_scale, wqkv_hbm, wout_hbm, wup_hbm, wdown_hbm, cot_hbm,
-        out_hbm, din_hbm, down_hbm, up_hbm, outw_hbm, qkvw_hbm, small_out,
+        outs, res, hid, du, small_out,
         params, x, cot, wqkv, wout, wup, wdown, halo_lo, halo_hi, nf, link,
-        act_q, act_k, act_v, qs, ks, vs, prob, att, res, n2, dm, hid, du, dbr, da, outs,
+        act_q, act_k, act_v, qs, ks, vs, prob, att, n2, dm, dbr, da,
         dke, dve, dmx, msg_hi, msg_lo, got_lo, got_hi, dq_hi, dq_lo, dq_got_lo, dq_got_hi,
         edge, edge_mix, sums, small_cur, small_recv,
         part, recv,
-        in_sem, out_sem, halo_send, halo_recv, rs_send, rs_recv, ag_send, ag_recv, sm_send, sm_recv,
+        in_sem, halo_send, halo_recv, rs_send, rs_recv, ag_send, ag_recv, sm_send, sm_recv,
     ) = refs
     orders, small_steps, rows, seqs, frames, feats, ff, tm_size = cfg
     units = len(orders)
@@ -527,11 +543,6 @@
     tall = 2 * frames
     chunk = feats
     tokens = seqs * frames
-    out_copies = [
-        pltpu.make_async_copy(outs.at[pl.ds(2 * t, 2)], out_hbm.at[pl.ds(2 * t, 2)], out_sem.at[t])
-        for t in range(pairs)
-    ]
-
     def flat(ref, t):
         return ref[pl.ds(2 * t, 2)].reshape(tall, ref.shape[2])
 
@@ -557,19 +568,6 @@
 
     ff_blocks = ff // feats
 
-    def block_copy(block):
-        ref, start = red.full(block // per_unit)
-        src = ref.at[pl.ds(start + (block % per_unit) * feats, feats)]
-        if block < ff_blocks:
-            dst = down_hbm.at[pl.ds(block * feats, feats)]
-        elif block < 2 * ff_blocks:
-            dst = up_hbm.at[:, pl.ds((block - ff_blocks) * feats, feats)]
-        elif block == 2 * ff_blocks:
-            dst = outw_hbm
-        else:
-            dst = qkvw_hbm.at[block - 2 * ff_blocks - 1]
-        return pltpu.make_async_copy(src, dst, out_sem.at[pairs + 1 + block])
-
     def unit_begun(block):
         return block // per_unit if block % per_unit == per_unit - 1 else None
 
@@ -577,9 +575,6 @@
 
     def advance(u, i):
         red.tick(u, i)
-        if i == 2 * red.levels(u):
-            for block in range(u * per_unit, (u + 1) * per_unit):
-                block_copy(block).start()
 
     def slot(name, index=None, count=0):
         if index is None:
@@ -652,8 +647,6 @@
         slot(("x",), t, pairs)
 
     loop(pairs, feed_back)
-    for copy in out_copies:
-        copy.start()
 
 
     dq = dm
@@ -774,8 +767,6 @@
                     pl.when(s == k)(lambda k=k: [advance(u, step) for u, step in placed[("i", k)]] and None)
 
     loop(pairs, input_grads)
-    din_copy = pltpu.make_async_copy(res, din_hbm, out_sem.at[pairs])
-    din_copy.start()
     small_cur[0] = jnp.sum(sums[...], axis=1)
 
     def small_copy(level):
@@ -806,53 +797,36 @@
         small_copy(level).wait_send()
     for u in range(units):
         red.wait_sends(u)
-    for copy in out_copies + [din_copy] + [block_copy(b) for b in range(2 * ff_blocks + 4)]:
-        copy.wait()
 
 
 def widen_kernel(
-    output_in, d_in, down, up, out_w, qkv_w, small, output, d_inputs, d_gain_one, d_kernel, d_qkv, d_out, d_gain_two, d_up, d_down, d_scale,
-    low_held, wide_held, narrow, broad, in_sem, out_sem,
+    places, outs, res, hid, du, small,
+    output, d_inputs, d_gain_one, d_kernel, d_qkv, d_out, d_gain_two, d_up, d_down, d_scale, broad, sem,
 ):
-    count, feats, _ = narrow.shape
+    count, feats, _ = broad.shape
     ff_blocks = (count - 4) // 2
-    moves = []
-    for j in range(ff_blocks):
-        here = pl.ds(j * feats, feats)
-        moves.append((down.at[here], d_down.at[here]))
-    for j in range(ff_blocks):
-        here = pl.ds(j * feats, feats)
-        moves.append((up.at[:, here], d_up.at[:, here]))
-    moves.append((out_w, d_out))
-    for n in range(3):
-        moves.append((qkv_w.at[n], d_qkv.at[n]))
-    loads = [pltpu.make_async_copy(m[0], narrow.at[i], in_sem.at[i]) for i, m in enumerate(moves)]
-    stores = [pltpu.make_async_copy(broad.at[i], m[1], out_sem.at[i]) for i, m in enumerate(moves)]
-    passes = []
-    for i, (src, held, dst) in enumerate(((output_in, low_held, output), (d_in, wide_held, d_inputs))):
-        passes.append((
-            pltpu.make_async_copy(src, held, in_sem.at[count + i]),
-            pltpu.make_async_copy(held, dst, out_sem.at[count + i]),
-        ))
-    for load in loads + [get for get, _ in passes]:
-        load.start()
+    passes = [pltpu.make_async_copy(src, dst, sem.at[count + i]) for i, (src, dst) in enumerate(((outs, output), (res, d_inputs)))]
+    for put in passes:
+        put.start()
+    targets = [d_down.at[pl.ds(j * feats, feats)] for j in range(ff_blocks)]
+    targets += [d_up.at[:, pl.ds(j * feats, feats)] for j in range(ff_blocks)]
+    targets += [d_out] + [d_qkv.at[n] for n in range(3)]
+    stores = []
+    for i, (which, start) in enumerate(places):
+        src = (hid, du)[which]
+
+        def widen(r, src=src, start=start, i=i):
+            here = pl.ds(pl.multiple_of(r * 64, 64), 64)
+            broad[i, here, :] = src[pl.ds(pl.multiple_of(start + r * 64, 64), 64), :].astype(F32)
+
+        loop(feats // 64, widen)
+        stores.append(pltpu.make_async_copy(broad.at[i], targets[i], sem.at[i]))
+        stores[-1].start()
     for n in range(3):
         d_kernel[n] = small[pl.ds(3 * n, 3), :]
     for i, dst in enumerate((d_gain_one, d_gain_two, d_scale)):
         dst[...] = small[pl.ds(9 + i, 1), :].reshape(feats)
-    for i in range(count):
-        loads[i].wait()
-
-        def widen(r):
-            here = pl.ds(pl.multiple_of(r * 32, 32), 32)
-            broad[i, here, :] = narrow[i, here, :].astype(F32)
-
-        loop(feats // 32, widen)
-        stores[i].start()
-    for get, put in passes:
-        get.wait()
-        put.start()
-    for store in stores + [put for _, put in passes]:
+    for store in passes + stores:
         store.wait()
 
 
@@ -866,7 +840,7 @@
     rows = max(feats, 16 * seq_size * tm_size)
     units = (2 * ff + 4 * feats) // rows
     kinds, orders = step_orders(seq_size, tm_size)
-    orders, small_steps = orders[:units], kinds[-2]
+    orders, small_steps = orders[:units], kinds[6]
     levels = len(small_steps)
     copies = max(sum((1 << len(bits)) - 1 for bits in order) for order in orders)
     ext = frames + 2 * HALO
@@ -882,52 +856,58 @@
         low(seqs, HALO, feats), low(seqs, HALO, feats),
         wide(seqs, ext + 2 * PAD, feats), wide(seqs, ext + 2 * PAD, 128),
         acts(), acts(), acts(), acts(), acts_ext(), acts_ext(),
-        wide(seqs, HEADS, ext, frames), acts(), wide(seqs, frames, feats), acts(), acts(),
-        low(seqs * frames * ff // feats, feats), low(seqs * frames * ff // feats, feats), acts(), acts(), acts(),
+        wide(seqs, HEADS, ext, frames), acts(), acts(), acts(),
+        acts(), acts(),
         wide(seqs, ext, feats), wide(seqs, ext, feats), wide(3, 2, frames + 2 * PAD, feats),
         low(seqs, HALO, 2 * feats), low(seqs, HALO, 2 * feats), low(seqs, HALO, 2 * feats), low(seqs, HALO, 2 * feats),
         wide(seqs, feats), wide(seqs, feats), wide(seqs, feats), wide(seqs, feats),
         wide(3, 2 * seqs, feats), wide(3, 2 * seqs, feats), wide(16, 8, feats),
         wide(levels, 16, feats), wide(levels, 16, feats),
         low(units, rows, feats), low(units, rows, feats),
-        dma((6,)), dma((seqs // 2 + 1 + (2 * ff + 4 * feats) // feats,)), dma((4 + seqs,)), dma((4 + seqs,)),
+        dma((6,)), dma((4 + seqs,)), dma((4 + seqs,)),
         dma((units, copies)), dma((units, copies)), dma((units, copies)), dma((units, copies)),
         dma((levels,)), dma((levels,)),
     ]
     cfg = (orders, small_steps, rows, seqs, frames, feats, ff, tm_size)
     out_type = jax.ShapeDtypeStruct
-    output, d_inputs, down, up, out_w, qkv_w, small = pl.pallas_call(
+    stay = lambda v: pltpu.with_memory_space_constraint(v, pltpu.HBM)
+    held = out_type((seqs * frames * ff // feats, feats), BF16)
+    outs, res, hid, du, small = pl.pallas_call(
         functools.partial(layer_kernel, cfg),
         out_shape=(
-            out_type(inputs.shape, BF16), out_type(inputs.shape, F32), out_type((ff, feats), BF16),
-            out_type((feats, ff), BF16), out_type((feats, feats), BF16), out_type((3, feats, feats), BF16),
-            out_type((16, feats), F32),
+            pltpu.VMEM(inputs.shape, BF16), pltpu.VMEM(inputs.shape, F32), pltpu.VMEM(held.shape, BF16),
+            pltpu.VMEM(held.shape, BF16), pltpu.VMEM((16, feats), F32),
         ),
         in_specs=[pl.BlockSpec(memory_space=pltpu.SMEM), any_spec] + [vmem_spec] * 4 + [any_spec] * 5,
-        out_specs=(any_spec,) * 6 + (vmem_spec,),
+        out_specs=(vmem_spec,) * 5,
         scratch_shapes=scratch,
         compiler_params=pltpu.CompilerParams(
-            collective_id=0, has_side_effects=True, vmem_limit_bytes=67043328
+            collective_id=0, has_side_effects=True, vmem_limit_bytes=50 << 20
         ),
-    )(lengths, inputs, norm_gain, conv_kernel, mlp_gain, layer_scale, qkv_weight, out_weight, up_weight, down_weight, cotangent)
+    )(
+        lengths, stay(inputs), norm_gain, conv_kernel, mlp_gain, layer_scale, stay(qkv_weight), stay(out_weight),
+        stay(up_weight), stay(down_weight), stay(cotangent),
+    )
     count = (2 * ff + 4 * feats) // feats
+    per_unit = rows // feats
+    places = []
+    for block in range(count):
+        which, start = gathered_at(block // per_unit, rows, *held.shape)
+        places.append((which, start + block % per_unit * feats))
     hbm_spec = pl.BlockSpec(memory_space=pltpu.HBM)
     return pl.pallas_call(
-        widen_kernel,
+        functools.partial(widen_kernel, places),
         out_shape=(
             out_type(inputs.shape, BF16), out_type(inputs.shape, F32),
             out_type((feats,), F32), out_type((3, 3, feats), F32), out_type((3, feats, feats), F32),
             out_type((feats, feats), F32), out_type((feats,), F32), out_type((feats, ff), F32),
             out_type((ff, feats), F32), out_type((feats,), F32),
         ),
-        in_specs=[hbm_spec] * 6 + [vmem_spec],
+        in_specs=[vmem_spec] * 5,
         out_specs=(hbm_spec,) * 2 + (vmem_spec, vmem_spec, hbm_spec, hbm_spec, vmem_spec, hbm_spec, hbm_spec, vmem_spec),
-        scratch_shapes=[
-            acts(), wide(seqs, frames, feats), low(count, feats, feats), wide(count, feats, feats),
-            dma((count + 2,)), dma((count + 2,)),
-        ],
-        compiler_params=pltpu.CompilerParams(vmem_limit_bytes=67043328),
-    )(output, d_inputs, down, up, out_w, qkv_w, small)
+        scratch_shapes=[wide(count, feats, feats), dma((count + 2,))],
+        compiler_params=pltpu.CompilerParams(vmem_limit_bytes=16 << 20),
+    )(outs, res, hid, du, small)
 
 
 def solution(mesh):

time: 112 us -> 103 us (0.920)
  Pallas kernels: 110 us -> 102 us
    pallas_call x2, Pallas kernels: 110 us -> 102 us  [the longest x1 96.1 us: shards(): pl.pallas_call(functools.partial(layer_kernel, cfg), out_shape=(pltpu.VME...]
where the time goes in v5:
time: 103 us
  Pallas kernels  102 us (99%)
    pallas_call x1, Pallas kernels, shards(): pl.pallas_call(functools.partial(layer_kernel, cfg), out_shape=(pltpu.VME...  96.1 us
    pallas_call x1, Pallas kernels, shards(): pl.pallas_call(functools.partial(widen_kernel, places), out_shape=(out_ty...  6.24 us

profile of v5, /device:TPU:1, one launch (start us, length us, event | category | flops | bytes accessed | tf_op | source)
XLA Modules:
  0.0 103.2 jit_solution(3069821072422000392)
XLA Ops:
  0.6 96.1 %shard_map.186 = (bf16[8,128,512]{2,1,0:T(8,128)(2,1)S(1)}, f32[8,128,512]{2,1,0:T(8,128)S(1)}, bf16[4096,512]{1,0:T(8,128)(2,1)S(1)}, bf16[4096,512]{1,0:T(8,128)(2,1)S(1)}, f32[16,512]{1,0:T(8,128)S(1)}) custom-call(s32[8,8]{1,0:T(8,128)} %refs_0_.1, bf16[8,128,512]{2,1,0:T(8,128)(2,1)} %refs_1_.1, bf16[512]{0:T(512)(128)(2,1)} %refs_2_.1, ...), custom_call_target="tpu_custom_call" | custom-call | tf_op jit(solution)/shard_map/pallas_call | solution.py:875
  96.8 6.2 %shard_map.187 = (bf16[8,128,512]{2,1,0:T(8,128)(2,1)}, f32[8,128,512]{2,1,0:T(8,128)}, f32[512]{0:T(512)}, f32[3,3,512]{2,1,0:T(4,128)}, f32[3,512,512]{2,1,0:T...) custom-call(bf16[8,128,512]{2,1,0:T(8,128)(2,1)S(1)} %get-tuple-elemen, ...), custom_call_target="tpu_custom_call" | custom-call | tf_op jit(solution)/shard_map/pallas_call | solution.py:898

commit v6 on v5

--- a/solution.py
+++ b/solution.py
@@ -18,7 +18,8 @@
 BF16 = jnp.bfloat16
 
 
-CHOICE = (4, 4, 10, 7, 4, 10, 10, 6, 4, 5, 4, 4)
+LEAD = (5, 0, 2, 2, 0, 0, 5, 0, -3, 2, 10, 10)
+CHOICE = (4, 3, 6, 1, 0, 1, 2, 4, 0, 1, 0, 1)
 
 
 def step_orders(seq_size, tm_size):
@@ -184,7 +185,7 @@
                 copy.wait_send()
 
 
-def plan_steps(orders, small_steps, rows, feats, pieces):
+def plan_steps(orders, small_steps, rows, feats, pieces, lead):
     core_rate, link_rate = 600e3, 104e3
     free, reached, arrival = {}, {}, {}
     levels = {u: len(order) for u, order in enumerate(orders)}
@@ -244,7 +245,7 @@
             ready = [u for u in reached if reached[u] <= last(u) and arrival[u] <= now]
             if not ready:
                 break
-            unit = min(ready, key=lambda u: (arrival[u], u))
+            unit = min(ready, key=lambda u: (arrival[u] - lead[u], u))
             todo.append((unit, reached[unit]))
             now += step(unit, now)
         placed[slot] = todo
@@ -268,15 +269,15 @@
     begun = lambda block: block // per_unit if block % per_unit == per_unit - 1 else None
     pieces = []
     for j in range(ff_blocks):
-        pieces += [(("f", j, t), 0.93, None) for t in range(pairs)]
+        pieces += [(("f", j, t), 1.53, None) for t in range(seqs // 4)]
         pieces += [(("d", j), 0.73, begun(j)), (("u", j), 0.73, begun(ff_blocks + j))]
     pieces += [(("x", t), 0.63, None) for t in range(pairs)]
-    pieces += [(("b", s), 0.68, None) for s in range(seqs)]
+    pieces += [(("b", s), 0.64, None) for s in range(seqs)]
     pieces += [
-        ("q", 0.73, begun(2 * ff_blocks + 1)), ("o", 0.73, begun(2 * ff_blocks)), ("w", 0.8, None),
+        ("q", 0.73, begun(2 * ff_blocks + 1)), ("o", 0.73, begun(2 * ff_blocks)), ("w", 0.5, None),
         ("k", 0.73, begun(2 * ff_blocks + 2)), ("v", 0.73, begun(2 * ff_blocks + 3)),
     ]
-    pieces += [(("i", s), 0.92, None) for s in range(seqs)]
+    pieces += [(("i", s), 0.91, None) for s in range(seqs)]
     return pieces
 
 
@@ -381,8 +382,7 @@
             [(x_hbm, x), (wqkv_hbm, wqkv), (wout_hbm, wout), (wup_hbm, wup), (wdown_hbm, wdown), (cot_hbm, cot)]
         )
     ]
-    for load in loads:
-        load.start()
+    loads[0].start()
 
     class Across:
         def __init__(self, src, dst, i, side):
@@ -437,19 +437,27 @@
         return (centered * r * gain_one).astype(BF16).astype(F32)
 
     loads[0].wait()
-
-    def norm_own(s):
-        nf[s, pl.ds(own, frames), :] = normed_rows(x[s])
-        zero = jnp.zeros((PAD, feats), F32)
-        nf[s, pl.ds(0, PAD), :] = zero
-        nf[s, pl.ds(PAD + ext, PAD), :] = zero
+    for load in loads[1:]:
+        load.start()
+
+    def norm_own(t):
+        two = pl.ds(2 * t, 2)
+        value = normed_rows(x[two].reshape(2 * frames, feats))
         pos = base - own + lax.broadcasted_iota(jnp.int32, (ext + 2 * PAD, 128), 0)
-        cut = pos == 0
-        for bound in bounds_of(s):
-            cut = cut | (pos == bound)
-        link[s] = jnp.where(cut, 0.0, 1.0)
-
-    loop(seqs, norm_own)
+        links = []
+        for i in range(2):
+            cut = pos == 0
+            for bound in bounds_of(2 * t + i):
+                cut = cut | (pos == bound)
+            links.append(jnp.where(cut, 0.0, 1.0))
+        zero = jnp.zeros((2, PAD, feats), F32)
+        nf[two, pl.ds(own, frames), :] = value.reshape(2, frames, feats)
+        nf[two, pl.ds(0, PAD), :] = zero
+        nf[two, pl.ds(PAD + ext, PAD), :] = zero
+        for i in range(2):
+            link[2 * t + i] = links[i]
+
+    loop(pairs, norm_own)
     enter(greeted, tm_size)
     to_next.start()
     to_prev.start()
@@ -571,7 +579,7 @@
     def unit_begun(block):
         return block // per_unit if block % per_unit == per_unit - 1 else None
 
-    placed, tail, _ = plan_steps(orders, small_steps, rows, feats, make_pieces(seqs, ff_blocks, per_unit))
+    placed, tail, _ = plan_steps(orders, small_steps, rows, feats, make_pieces(seqs, ff_blocks, per_unit), LEAD)
 
     def advance(u, i):
         red.tick(u, i)
@@ -596,23 +604,24 @@
         cols = pl.ds(j * chunk, chunk)
 
         def hidden_chunk(t, j=j, cols=cols):
-            upper = nn(flat(n2, t), wup[:, cols])
-            d_hidden = nt(flat(dm, t), wdown[cols, :])
+            four = pl.ds(4 * t, 4)
+            high = 4 * frames
+            upper = nn(n2[four].reshape(high, feats), wup[:, cols])
+            d_hidden = nt(dm[four].reshape(high, feats), wdown[cols, :])
             value, slope = gelu_pair(upper)
             value, slope = value.astype(BF16), (slope * d_hidden).astype(BF16)
-            tile = pl.ds(pl.multiple_of(j * tokens + t * tall, tall), tall)
+            tile = pl.ds(pl.multiple_of(j * tokens + t * high, high), high)
             mlp_part, e_part = nn(value, wdown[cols, :]), nt(slope, wup[:, cols])
-            two = pl.ds(2 * t, 2)
             if j:
-                mlp_part = mlp_part + mlp_sum[two, early, :].reshape(tall, feats)
-                e_part = e_part + e_sum[two, early, :].reshape(tall, feats)
+                mlp_part = mlp_part + mlp_sum[four, early, :].reshape(high, feats)
+                e_part = e_part + e_sum[four, early, :].reshape(high, feats)
             hid[tile, :] = value
             du[tile, :] = slope
-            mlp_sum[two, early, :] = back(mlp_part)
-            e_sum[two, early, :] = back(e_part)
-            slot(("f", j), t, pairs)
-
-        loop(pairs, hidden_chunk)
+            mlp_sum[four, early, :] = mlp_part.reshape(4, frames, feats)
+            e_sum[four, early, :] = e_part.reshape(4, frames, feats)
+            slot(("f", j), t, seqs // 4)
+
+        loop(seqs // 4, hidden_chunk)
         rows_j = pl.ds(j * tokens, tokens)
         place(j, tn(hid[rows_j, :], whole(dm)))
         begin(j)

time: 103 us -> 99.9 us (0.970)
  Pallas kernels: 102 us -> 98.9 us
    pallas_call x1, Pallas kernels: 96.1 us -> 92.7 us  [shards(): pl.pallas_call(functools.partial(layer_kernel, cfg), out_shape=(pltpu.VME...]
where the time goes in v6:
time: 99.9 us; the launch traced here: 99.7 us
  Pallas kernels  98.9 us (99%)
    pallas_call x1, Pallas kernels, shards(): pl.pallas_call(functools.partial(layer_kernel, cfg), out_shape=(pltpu.VME...  92.7 us
    pallas_call x1, Pallas kernels, shards(): pl.pallas_call(functools.partial(widen_kernel, places), out_shape=(out_ty...  6.24 us

profile of v6, /device:TPU:1, one launch (start us, length us, event | category | flops | bytes accessed | tf_op | source)
XLA Modules:
  0.0 99.7 jit_solution(1126520180246088337)
XLA Ops:
  0.6 92.7 %shard_map.186 = (bf16[8,128,512]{2,1,0:T(8,128)(2,1)S(1)}, f32[8,128,512]{2,1,0:T(8,128)S(1)}, bf16[4096,512]{1,0:T(8,128)(2,1)S(1)}, bf16[4096,512]{1,0:T(8,128)(2,1)S(1)}, f32[16,512]{1,0:T(8,128)S(1)}) custom-call(s32[8,8]{1,0:T(8,128)} %refs_0_.1, bf16[8,128,512]{2,1,0:T(8,128)(2,1)} %refs_1_.1, bf16[512]{0:T(512)(128)(2,1)} %refs_2_.1, ...), custom_call_target="tpu_custom_call" | custom-call | tf_op jit(solution)/shard_map/pallas_call | solution.py:884
  93.3 6.2 %shard_map.187 = (bf16[8,128,512]{2,1,0:T(8,128)(2,1)}, f32[8,128,512]{2,1,0:T(8,128)}, f32[512]{0:T(512)}, f32[3,3,512]{2,1,0:T(4,128)}, f32[3,512,512]{2,1,0:T...) custom-call(bf16[8,128,512]{2,1,0:T(8,128)(2,1)S(1)} %get-tuple-elemen, ...), custom_call_target="tpu_custom_call" | custom-call | tf_op jit(solution)/shard_map/pallas_call | solution.py:907

commit v7 on v6

--- a/solution.py
+++ b/solution.py
@@ -500,17 +500,20 @@
 
     loop(seqs // 4, norm_halo)
 
-    def mix_ends(s):
+    def mix_ends(t):
         sides = ((0, 0, HALO, 0), (ends, frames, 0, frames - HALO))
-        found = [[mixed_rows(s, start, ends, lane) for lane in lanes] for _, start, _, _ in sides]
-        for (at, _, keep, row), half in zip(sides, found):
-            for n in range(3):
-                mixed = jnp.concatenate([m[n] for m in half], axis=1)
+        found = []
+        for s in (2 * t, 2 * t + 1):
+            for at, start, keep, row in sides:
+                half = [mixed_rows(s, start, ends, lane) for lane in lanes]
+                found.append((s, at, keep, row, [jnp.concatenate([m[n] for m in half], axis=1) for n in range(3)]))
+        for s, at, keep, row, streams_here in found:
+            for n, mixed in enumerate(streams_here):
                 tile = pl.ds(pl.multiple_of((n * seqs + s) * 2 * ends + at, ends), ends)
                 hid[tile, :] = mixed
                 streams[n][0][s, pl.ds(row, HALO), :] = mixed[keep : keep + HALO]
 
-    loop(seqs, mix_ends)
+    loop(pairs, mix_ends)
     for n, (_, dst, skip) in enumerate(streams):
         count = seqs * 2 * ends
         value = nn(hid[pl.ds(n * count, count), :], wqkv[n]).astype(BF16).reshape(seqs, 2 * ends, feats)
@@ -522,30 +525,32 @@
             dst[:, pl.ds(0, HALO), :] = piece(HALO, ends)
             dst[:, pl.ds(frames - HALO, HALO), :] = piece(ends, ends + HALO)
 
-    def attend(s):
+    def attend(t):
         key = lax.broadcasted_iota(jnp.int32, (ext, frames), 0) - HALO
         query = lax.broadcasted_iota(jnp.int32, (ext, frames), 1)
-        band = (key - query <= HALF) & (key - query >= -HALF)
         pos_k = key + base
         pos_q = lax.broadcasted_iota(jnp.int32, (8, frames), 1) + base
-        seg_k = jnp.zeros((ext, frames), jnp.int32)
-        seg_q = jnp.zeros((8, frames), jnp.int32)
-        for bound in bounds_of(s):
-            seg_k = seg_k + (pos_k >= bound).astype(jnp.int32)
-            seg_q = seg_q + (pos_q >= bound).astype(jnp.int32)
-        allowed = band & (seg_k == seg_q[0:1]) & (pos_k >= 0) & (pos_k < seq_length)
-        bias = jnp.where(allowed, 0.0, -1e30)
-        heads = [pl.ds(h * HD, HD) for h in range(HEADS)]
-        scores = [nt(ks[s, :, head], qs[s, :, head]) * temper + bias for head in heads]
-        raised = [jnp.exp(value - jnp.max(value, axis=0, keepdims=True)) for value in scores]
-        probs = [value * (1.0 / jnp.sum(value, axis=0, keepdims=True)) for value in raised]
-        for h, head in enumerate(heads):
-            prob[s, h] = probs[h]
-        found = [tn(probs[h].astype(BF16), vs[s, :, head]) for h, head in enumerate(heads)]
-        for h, head in enumerate(heads):
-            att[s, :, head] = found[h].astype(BF16)
-
-    loop(seqs, attend)
+        near = (key - query <= HALF) & (key - query >= -HALF) & (pos_k >= 0) & (pos_k < seq_length)
+        results = []
+        for s in (2 * t, 2 * t + 1):
+            seg_k = jnp.zeros((ext, frames), jnp.int32)
+            seg_q = jnp.zeros((8, frames), jnp.int32)
+            for bound in bounds_of(s):
+                seg_k = seg_k + (pos_k >= bound).astype(jnp.int32)
+                seg_q = seg_q + (pos_q >= bound).astype(jnp.int32)
+            bias = jnp.where(near & (seg_k == seg_q[0:1]), 0.0, -1e30)
+            heads = [pl.ds(h * HD, HD) for h in range(HEADS)]
+            scores = [nt(ks[s, :, head], qs[s, :, head]) * temper + bias for head in heads]
+            raised = [jnp.exp(value - jnp.max(value, axis=0, keepdims=True)) for value in scores]
+            probs = [value * (1.0 / jnp.sum(value, axis=0, keepdims=True)) for value in raised]
+            found = [tn(probs[h].astype(BF16), vs[s, :, head]).astype(BF16) for h, head in enumerate(heads)]
+            results.append((s, probs, found))
+        for s, probs, found in results:
+            for h in range(HEADS):
+                prob[s, h] = probs[h]
+            att[s] = jnp.concatenate(found, axis=1)
+
+    loop(pairs, attend)
     for load in loads[2:]:
         load.wait()
     tall = 2 * frames
@@ -558,16 +563,16 @@
         return value.reshape(2, frames, feats)
 
     def residual_norm(t):
-        two = pl.ds(2 * t, 2)
-        residual = flat(x, t).astype(F32) + nn(flat(att, t), wout[...])
-        d_mlp = (flat(cot, t).astype(F32) * scale).astype(BF16)
+        four = pl.ds(4 * t, 4)
+        tall_rows = lambda ref: ref[four].reshape(4 * frames, feats)
+        residual = tall_rows(x).astype(F32) + nn(tall_rows(att), wout[...])
+        d_mlp = (tall_rows(cot).astype(F32) * scale).astype(BF16)
         centered, r = moments(residual)
         normed_two = (centered * r * gain_two).astype(BF16)
-        res[two] = back(residual)
-        n2[two] = back(normed_two)
-        dm[two] = back(d_mlp)
-
-    loop(pairs, residual_norm)
+        for ref, value in ((res, residual), (n2, normed_two), (dm, d_mlp)):
+            ref[four] = value.reshape(4, frames, feats)
+
+    loop(seqs // 4, residual_norm)
     whole = lambda ref: ref[...].reshape(seqs * frames, ref.shape[2])
     early = pl.ds(0, frames)
 

time: 99.9 us -> 98.7 us (0.988)
  Pallas kernels: 98.9 us -> 97.7 us
    pallas_call x1, Pallas kernels: 92.7 us -> 91.4 us  [shards(): pl.pallas_call(functools.partial(layer_kernel, cfg), out_shape=(pltpu.VME...]
where the time goes in v7:
time: 98.7 us; the launch traced here: 98.5 us
  Pallas kernels  97.7 us (99%)
    pallas_call x1, Pallas kernels, shards(): pl.pallas_call(functools.partial(layer_kernel, cfg), out_shape=(pltpu.VME...  91.4 us
    pallas_call x1, Pallas kernels, shards(): pl.pallas_call(functools.partial(widen_kernel, places), out_shape=(out_ty...  6.24 us

profile of v7, /device:TPU:1, one launch (start us, length us, event | category | flops | bytes accessed | tf_op | source)
XLA Modules:
  0.0 98.5 jit_solution(3730383936818906764)
XLA Ops:
  0.6 91.4 %shard_map.186 = (bf16[8,128,512]{2,1,0:T(8,128)(2,1)S(1)}, f32[8,128,512]{2,1,0:T(8,128)S(1)}, bf16[4096,512]{1,0:T(8,128)(2,1)S(1)}, bf16[4096,512]{1,0:T(8,128)(2,1)S(1)}, f32[16,512]{1,0:T(8,128)S(1)}) custom-call(s32[8,8]{1,0:T(8,128)} %refs_0_.1, bf16[8,128,512]{2,1,0:T(8,128)(2,1)} %refs_1_.1, bf16[512]{0:T(512)(128)(2,1)} %refs_2_.1, ...), custom_call_target="tpu_custom_call" | custom-call | tf_op jit(solution)/shard_map/pallas_call | solution.py:889
  92.1 6.2 %shard_map.187 = (bf16[8,128,512]{2,1,0:T(8,128)(2,1)}, f32[8,128,512]{2,1,0:T(8,128)}, f32[512]{0:T(512)}, f32[3,3,512]{2,1,0:T(4,128)}, f32[3,512,512]{2,1,0:T...) custom-call(bf16[8,128,512]{2,1,0:T(8,128)(2,1)S(1)} %get-tuple-elemen, ...), custom_call_target="tpu_custom_call" | custom-call | tf_op jit(solution)/shard_map/pallas_call | solution.py:912
